TPU v7x, 32 devices: a whole 2x2x4 slice. The times are simulated.
32 devices in a mesh: expert: 2 (over x), dp: 16 (over z, y, core).
Axes of the slice: x: 2, y: 2, z: 4, core: 2. Of those that a mesh axis runs over, the one named last changes fastest.
Arguments:
- grads: bfloat16 [2, 16, 128, 6144], P('expert', 'dp'), may hold values from -16 to 16
- master: float32 [2, 128, 6144], P('expert', 'dp'), may hold values from -0.0625 to 0.0625
- first_moment: float32 [2, 128, 6144], P('expert', 'dp'), may hold values from -0.0029296875 to 0.0029296875
- second_moment: float32 [2, 128, 6144], P('expert', 'dp'), may hold values from 1e-08 to 1e-07
Outputs:
- new_master: float32 [2, 128, 6144], P('expert', 'dp')
- new_first: float32 [2, 128, 6144], P('expert', 'dp')
- new_second: float32 [2, 128, 6144], P('expert', 'dp')
- direction: float32 [2, 128, 6144], P('expert', 'dp')
- new_weights: bfloat16 [2, 128, 6144], P('expert')
All inputs are finite; a program needn't handle non-finite values.
Results may differ from a plain program's by a relative error of at most 0.0004.
Values may be sent and summed in bfloat16 or wider, within the bound.
No kernel may reach another device: no remote copies, remote signals or barrier semaphores. Data moves between devices by JAX's collectives and lax.ppermute only.
A program may use at most 64 MiB of HBM per device.

v0:
```python
import jax
import jax.numpy as jnp
from jax import lax
from jax.sharding import PartitionSpec as P

STEP = 10
NEAR = 4


def _swap(array, size, offset):
    return lax.ppermute(array, "dp", [(i, i ^ offset) for i in range(size)])


def _pick(array, index):
    return lax.dynamic_index_in_dim(array, index, 0, keepdims=False)


def _sum_rows(grads, rows, width, size):
    far = size // NEAR
    me = lax.axis_index("dp")
    far_at, near_at = me // NEAR, me % NEAR
    blocks = grads.reshape(far, NEAR, rows, width)
    order = list(reversed(range(far)))
    pieces = []
    for k in order:
        group = _pick(blocks, far_at ^ k)
        pieces.append([_pick(group, near_at ^ j) for j in range(NEAR)])
    pieces = lax.optimization_barrier(pieces)
    moved = []
    for k, piece in zip(order, pieces):
        moved.append([_swap(piece[j], size, j) for j in (2, 3, 1)])
    sums = []
    for k, piece, others in zip(order, pieces, moved):
        total = piece[0].astype(jnp.float32)
        for other in others:
            total = total + other.astype(jnp.float32)
        sums.append(total)
    summed = sums[-1]
    for k, total in zip(order[:-1], sums):
        other = _swap(total, size, k * NEAR)
        summed = summed + other
    return summed


def shards(size, grads, master, first_moment, second_moment):
    rows, width = master.shape[1:]
    me = lax.axis_index("dp")
    summed = _sum_rows(grads[0, 0], rows, width, size)

    devices = size * lax.axis_size("expert")
    square = jnp.broadcast_to(jnp.sum(summed * summed), (devices, 1, 128))
    squares = lax.all_to_all(square, ("expert", "dp"), 0, 0)
    norm = jnp.sqrt(jnp.sum(squares[:, 0, 0]))
    clip = 1.0 / jnp.maximum(norm, 1.0)
    clipped = clip * summed
    new_first = 0.9 * first_moment[0] + 0.1 * clipped
    new_second = 0.95 * second_moment[0] + 0.05 * (clipped * clipped)
    first_fix = 1.0 - 0.9**STEP
    second_fix = 1.0 - 0.95**STEP
    direction = new_first / first_fix / (jnp.sqrt(new_second / second_fix) + 1e-08)
    new_master = master[0] - 0.001 * (direction + 0.1 * master[0])

    own = new_master.astype(jnp.bfloat16)
    held = [own]
    for k in range(2, size, 2):
        held.append(_swap(own, size, k))
    held = jnp.stack(held)
    other = _swap(held, size, 1)
    full = jnp.stack([held, other], 1).reshape(size, rows, width)
    full = jnp.take(full, jnp.arange(size) ^ me, axis=0)
    new_weights = full.reshape(1, size * rows, width)
    return (new_master[None], new_first[None], new_second[None], direction[None], new_weights)


def solution(mesh):
    state = P("expert", "dp", None)
    size = mesh.shape["dp"]
    return jax.shard_map(
        lambda *args: shards(size, *args),
        mesh=mesh,
        in_specs=(P("expert", "dp", None, None), state, state, state),
        out_specs=(state, state, state, state, P("expert", None, None)),
        check_vma=False,
    )
```

profile of v0, /device:TPU:0, one launch (start us, length us, event | category | flops | bytes accessed | tf_op | source)
XLA Modules:
  0.0 75.5 jit_solution(6919578044255277203)
XLA Ops:
  0.7 1.6 %dynamic-slice_bitcast_fusion = (bf16[8,6144]{1,0:T(8,128)(2,1)S(1)}, bf16[8,6144]{1,0:T(8,128)(2,1)S(1)}, bf16[8,6144]{1,0:T(8,128)(2,1)S(1)}, bf16[8,6144]{1,0...) fusion(bf16[4,4,8,6144]{3,2,1,0:T(8,128)(2,1)} %bitcast.94, ...), kind=kLoop, calls=%fused_computation.23 | loop fusion | bytes 3145760 | tf_op jit(solution)/shard_map/jit(dynamic_index_in_dim)/squeeze | solution.py:15
  2.4 3.1 %collective-permute-start.3 = (bf16[8,6144]{1,0:T(8,128)(2,1)S(1)}, bf16[8,6144]{1,0:T(8,128)(2,1)S(1)}, u32[]{:S(2)}, u32[]{:S(2)}) collective-permute-start(bf16[8,6144]{1,0:T(8,128)(2,1)S(1)} %get-tuple-element.26), channel_id=1, source_target_pairs={{0,2},{1,3},{2,0},{3,1},{4,6},{5,7},{6,4},{7,5},{8,10},{9,11},{10,... | collective-permute-start | bytes 294920 | tf_op jit(solution)/shard_map/ppermute | solution.py:11
  5.6 1.9 %collective-permute-start.7 = (bf16[8,6144]{1,0:T(8,128)(2,1)S(1)}, bf16[8,6144]{1,0:T(8,128)(2,1)S(1)}, u32[]{:S(2)}, u32[]{:S(2)}) collective-permute-start(bf16[8,6144]{1,0:T(8,128)(2,1)S(1)} %get-tuple-element.30), channel_id=1, source_target_pairs={{0,2},{1,3},{2,0},{3,1},{4,6},{5,7},{6,4},{7,5},{8,10},{9,11},{10,... | collective-permute-start | bytes 294920 | tf_op jit(solution)/shard_map/ppermute | solution.py:11
  7.6 1.0 %collective-permute-done.3 = bf16[8,6144]{1,0:T(8,128)(2,1)S(1)} collective-permute-done((bf16[8,6144]{1,0:T(8,128)(2,1)S(1)}, bf16[8,6144]{1,0:T(8,128)(2,1)S(1)}, u32[]{:S(2)}, u32[]{:S(2)}) %collective-permute-start.3) | collective-permute-done | bytes 98336 | tf_op jit(solution)/shard_map/ppermute | solution.py:11
  8.6 2.1 %collective-permute-done.4 = bf16[8,6144]{1,0:T(8,128)(2,1)S(1)} collective-permute-done((bf16[8,6144]{1,0:T(8,128)(2,1)S(1)}, bf16[8,6144]{1,0:T(8,128)(2,1)S(1)}, u32[]{:S(2)}, u32[]{:S(2)}) %collective-permute-start.4) | collective-permute-done | bytes 98336 | tf_op jit(solution)/shard_map/ppermute | solution.py:11
  11.1 1.8 %collective-permute-start.12 = (bf16[8,6144]{1,0:T(8,128)(2,1)S(1)}, bf16[8,6144]{1,0:T(8,128)(2,1)S(1)}, u32[]{:S(2)}, u32[]{:S(2)}) collective-permute-start(bf16[8,6144]{1,0:T(8,128)(2,1)S(1)} %get-tuple-element.35), channel_id=1, source_target_pairs={{0,3},{1,2},{2,1},{3,0},{4,7},{5,6},{6,5},{7,4},{8,11},{9,10},{10,... | collective-permute-start | bytes 294920 | tf_op jit(solution)/shard_map/ppermute | solution.py:11
  13.2 1.6 %collective-permute-done.8 = bf16[8,6144]{1,0:T(8,128)(2,1)S(1)} collective-permute-done((bf16[8,6144]{1,0:T(8,128)(2,1)S(1)}, bf16[8,6144]{1,0:T(8,128)(2,1)S(1)}, u32[]{:S(2)}, u32[]{:S(2)}) %collective-permute-start.8) | collective-permute-done | bytes 98336 | tf_op jit(solution)/shard_map/ppermute | solution.py:11
  15.2 3.6 %collective-permute-start.6 = (f32[8,6144]{1,0:T(8,128)S(1)}, f32[8,6144]{1,0:T(8,128)S(1)}, u32[]{:S(2)}, u32[]{:S(2)}) collective-permute-start(f32[8,6144]{1,0:T(8,128)S(1)} %convert_add_fusion.2), channel_id=1, source_target_pairs={{0,12},{1,13},{2,14},{3,15},{4,8},{5,9},{6,10},{7,11},{8,4},{9,5},... | collective-permute-start | bytes 589832 | tf_op jit(solution)/shard_map/ppermute | solution.py:11
  18.9 0.7 collective-permute-start.10
  19.7 1.6 %collective-permute-start.14 = (f32[8,6144]{1,0:T(8,128)S(1)}, f32[8,6144]{1,0:T(8,128)S(1)}, u32[]{:S(2)}, u32[]{:S(2)}) collective-permute-start(f32[8,6144]{1,0:T(8,128)S(1)} %convert_add_fusion), channel_id=1, source_target_pairs={{0,4},{1,5},{2,6},{3,7},{4,0},{5,1},{6,2},{7,3},{8,12},{9,13},{10,... | collective-permute-start | bytes 589832 | tf_op jit(solution)/shard_map/ppermute | solution.py:11
  21.7 1.5 %collective-permute-start.2 = (bf16[8,6144]{1,0:T(8,128)(2,1)S(1)}, bf16[8,6144]{1,0:T(8,128)(2,1)S(1)}, u32[]{:S(2)}, u32[]{:S(2)}) collective-permute-start(bf16[8,6144]{1,0:T(8,128)(2,1)S(1)} %get-tuple-element.24), channel_id=1, source_target_pairs={{0,1},{1,0},{2,3},{3,2},{4,5},{5,4},{6,7},{7,6},{8,9},{9,8},{10,11... | collective-permute-start | bytes 294920 | tf_op jit(solution)/shard_map/ppermute | solution.py:11
  23.2 3.0 %collective-permute-done.1 = bf16[8,6144]{1,0:T(8,128)(2,1)S(1)} collective-permute-done((bf16[8,6144]{1,0:T(8,128)(2,1)S(1)}, bf16[8,6144]{1,0:T(8,128)(2,1)S(1)}, u32[]{:S(2)}, u32[]{:S(2)}) %collective-permute-start.1) | collective-permute-done | bytes 98336 | tf_op jit(solution)/shard_map/ppermute | solution.py:11
  26.2 10.5 %collective-permute-done.10 = f32[8,6144]{1,0:T(8,128)S(1)} collective-permute-done((f32[8,6144]{1,0:T(8,128)S(1)}, f32[8,6144]{1,0:T(8,128)S(1)}, u32[]{:S(2)}, u32[]{:S(2)}) %collective-permute-start.10) | collective-permute-done | bytes 196640 | tf_op jit(solution)/shard_map/ppermute | solution.py:11
  37.4 1.3 %broadcast_in_dim.29 = f32[32,1,128]{2,1,0:T(1,128)} broadcast(f32[]{:T(128)} %get-tuple-element.40), dimensions={} | broadcast | bytes 16388 | tf_op jit(solution)/shard_map/broadcast_in_dim | solution.py:51
  38.6 3.8 %all-to-all-start = ((f32[32,1,128]{2,1,0:T(1,128)}), f32[32,1,128]{2,1,0:T(1,128)S(1)}, u32[]{:S(2)}, u32[]{:S(2)}) async-start(f32[32,1,128]{2,1,0:T(1,128)} %broadcast_in_dim.29), calls=%async_computation | async-start | bytes 32768 | tf_op jit(solution)/shard_map/all_to_all | solution.py:52
  42.6 6.9 %all-to-all-done = f32[32,1,128]{2,1,0:T(1,128)S(1)} async-done(((f32[32,1,128]{2,1,0:T(1,128)}), f32[32,1,128]{2,1,0:T(1,128)S(1)}, u32[]{:S(2)}, u32[]{:S(2)}) %all-to-all-start) | async-done | bytes 16416 | tf_op jit(solution)/shard_map/all_to_all | solution.py:52
  52.3 2.3 %collective-permute-start.17 = (bf16[8,6144]{1,0:T(8,128)(2,1)S(1)}, bf16[8,6144]{1,0:T(8,128)(2,1)S(1)}, u32[]{:S(2)}, u32[]{:S(2)}) collective-permute-start(bf16[8,6144]{1,0:T(8,128)(2,1)S(1)} %get-tuple-element.38), channel_id=1, source_target_pairs={{0,6},{1,7},{2,4},{3,5},{4,2},{5,3},{6,0},{7,1},{8,14},{9,15},{10,... | collective-permute-start | bytes 294920 | tf_op jit(solution)/shard_map/ppermute | solution.py:11
  55.2 2.3 %collective-permute-start.19 = (bf16[8,6144]{1,0:T(8,128)(2,1)S(1)}, bf16[8,6144]{1,0:T(8,128)(2,1)S(1)}, u32[]{:S(2)}, u32[]{:S(2)}) collective-permute-start(bf16[8,6144]{1,0:T(8,128)(2,1)S(1)} %get-tuple-element.38), channel_id=1, source_target_pairs={{0,10},{1,11},{2,8},{3,9},{4,14},{5,15},{6,12},{7,13},{8,2},{9,3},... | collective-permute-start | bytes 294920 | tf_op jit(solution)/shard_map/ppermute | solution.py:11
  58.2 4.2 %collective-permute-start.21 = (bf16[8,6144]{1,0:T(8,128)(2,1)S(1)}, bf16[8,6144]{1,0:T(8,128)(2,1)S(1)}, u32[]{:S(2)}, u32[]{:S(2)}) collective-permute-start(bf16[8,6144]{1,0:T(8,128)(2,1)S(1)} %get-tuple-element.38), channel_id=1, source_target_pairs={{0,14},{1,15},{2,12},{3,13},{4,10},{5,11},{6,8},{7,9},{8,6},{9,7},... | collective-permute-start | bytes 294920 | tf_op jit(solution)/shard_map/ppermute | solution.py:11
  62.4 6.2 %collective-permute-done.18 = bf16[8,6144]{1,0:T(8,128)(2,1)S(1)} collective-permute-done((bf16[8,6144]{1,0:T(8,128)(2,1)S(1)}, bf16[8,6144]{1,0:T(8,128)(2,1)S(1)}, u32[]{:S(2)}, u32[]{:S(2)}) %collective-permute-start.18) | collective-permute-done | bytes 98336 | tf_op jit(solution)/shard_map/ppermute | solution.py:11
  68.7 2.2 %collective-permute-done.19 = bf16[8,6144]{1,0:T(8,128)(2,1)S(1)} collective-permute-done((bf16[8,6144]{1,0:T(8,128)(2,1)S(1)}, bf16[8,6144]{1,0:T(8,128)(2,1)S(1)}, u32[]{:S(2)}, u32[]{:S(2)}) %collective-permute-start.19) | collective-permute-done | bytes 98336 | tf_op jit(solution)/shard_map/ppermute | solution.py:11
  71.0 0.8 %fusion.5 = (f32[1,8,6144]{2,1,0:T(8,128)}, f32[1,8,6144]{2,1,0:T(8,128)}, f32[1,8,6144]{2,1,0:T(8,128)}) fusion(f32[8,6144]{1,0:T(8,128)S(1)} %get-tuple-element.41, f32[]{:T(128)S(6)} %div.29, f32[1,8,6144]{2,1,0:T(8,128)S(1)} %copy-done, f32[1,8,6144]{2,1,0:T(8,128)S(1)} %copy-done.1, f32[8,6144]{1,0:T(8,128)S(1)} %get-tuple-element.39, ...), kind=kLoop, calls=%fused_computation.42 | loop fusion | flops 589824 | bytes 1572868 | tf_op jit(solution)/shard_map/broadcast_in_dim | solution.py:72
  71.9 1.4 %collective-permute-done.22 = bf16[8,8,6144]{2,1,0:T(8,128)(2,1)S(1)} collective-permute-done((bf16[8,8,6144]{2,1,0:T(8,128)(2,1)S(1)}, bf16[8,8,6144]{2,1,0:T(8,128)(2,1)S(1)}, u32[]{:S(2)}, u32[]{:S(2)}) %collective-permute-start.22) | collective-permute-done | bytes 786464 | tf_op jit(solution)/shard_map/ppermute | solution.py:11
  74.1 1.4 %bitcast_select_fusion = bf16[1,128,6144]{2,1,0:T(8,128)(2,1)} fusion(bf16[16,8,6144]{2,1,0:T(8,128)(2,1)S(1)} %gather_fusion, pred[128]{0:T(512)(128)(4,1)S(1)} %broadcast_in_dim.35), kind=kLoop, calls=%fused_computation.2 | loop fusion | flops 786432 | bytes 3145856 | tf_op jit(solution)/shard_map/jit(_take)/select_n | solution.py:70
  (56 shorter events, 6.9 us)
Async XLA Ops:
  2.4 6.2 %collective-permute-start.3 = (bf16[8,6144]{1,0:T(8,128)(2,1)S(1)}, bf16[8,6144]{1,0:T(8,128)(2,1)S(1)}, u32[]{:S(2)}, u32[]{:S(2)}) collective-permute-start(bf16[8,6144]{1,0:T(8,128)(2,1)S(1)} %get-tuple-element.26), channel_id=1, source_target_pairs={{0,2},{1,3},{2,0},{3,1},{4,6},{5,7},{6,4},{7,5},{8,10},{9,11},{10,... | collective-permute-start | bytes 294920 | tf_op jit(solution)/shard_map/ppermute | solution.py:11
  5.4 5.3 %collective-permute-start.4 = (bf16[8,6144]{1,0:T(8,128)(2,1)S(1)}, bf16[8,6144]{1,0:T(8,128)(2,1)S(1)}, u32[]{:S(2)}, u32[]{:S(2)}) collective-permute-start(bf16[8,6144]{1,0:T(8,128)(2,1)S(1)} %get-tuple-element.27), channel_id=1, source_target_pairs={{0,3},{1,2},{2,1},{3,0},{4,7},{5,6},{6,5},{7,4},{8,11},{9,10},{10,... | collective-permute-start | bytes 294920 | tf_op jit(solution)/shard_map/ppermute | solution.py:11
  5.4 5.7 %collective-permute-start.5 = (bf16[8,6144]{1,0:T(8,128)(2,1)S(1)}, bf16[8,6144]{1,0:T(8,128)(2,1)S(1)}, u32[]{:S(2)}, u32[]{:S(2)}) collective-permute-start(bf16[8,6144]{1,0:T(8,128)(2,1)S(1)} %get-tuple-element.28), channel_id=1, source_target_pairs={{0,1},{1,0},{2,3},{3,2},{4,5},{5,4},{6,7},{7,6},{8,9},{9,8},{10,11... | collective-permute-start | bytes 294920 | tf_op jit(solution)/shard_map/ppermute | solution.py:11
  5.6 7.4 %collective-permute-start.7 = (bf16[8,6144]{1,0:T(8,128)(2,1)S(1)}, bf16[8,6144]{1,0:T(8,128)(2,1)S(1)}, u32[]{:S(2)}, u32[]{:S(2)}) collective-permute-start(bf16[8,6144]{1,0:T(8,128)(2,1)S(1)} %get-tuple-element.30), channel_id=1, source_target_pairs={{0,2},{1,3},{2,0},{3,1},{4,6},{5,7},{6,4},{7,5},{8,10},{9,11},{10,... | collective-permute-start | bytes 294920 | tf_op jit(solution)/shard_map/ppermute | solution.py:11
  7.6 7.2 %collective-permute-start.8 = (bf16[8,6144]{1,0:T(8,128)(2,1)S(1)}, bf16[8,6144]{1,0:T(8,128)(2,1)S(1)}, u32[]{:S(2)}, u32[]{:S(2)}) collective-permute-start(bf16[8,6144]{1,0:T(8,128)(2,1)S(1)} %get-tuple-element.31), channel_id=1, source_target_pairs={{0,3},{1,2},{2,1},{3,0},{4,7},{5,6},{6,5},{7,4},{8,11},{9,10},{10,... | collective-permute-start | bytes 294920 | tf_op jit(solution)/shard_map/ppermute | solution.py:11
  8.6 6.6 %collective-permute-start.9 = (bf16[8,6144]{1,0:T(8,128)(2,1)S(1)}, bf16[8,6144]{1,0:T(8,128)(2,1)S(1)}, u32[]{:S(2)}, u32[]{:S(2)}) collective-permute-start(bf16[8,6144]{1,0:T(8,128)(2,1)S(1)} %get-tuple-element.32), channel_id=1, source_target_pairs={{0,1},{1,0},{2,3},{3,2},{4,5},{5,4},{6,7},{7,6},{8,9},{9,8},{10,11... | collective-permute-start | bytes 294920 | tf_op jit(solution)/shard_map/ppermute | solution.py:11
  10.7 8.2 %collective-permute-start.11 = (bf16[8,6144]{1,0:T(8,128)(2,1)S(1)}, bf16[8,6144]{1,0:T(8,128)(2,1)S(1)}, u32[]{:S(2)}, u32[]{:S(2)}) collective-permute-start(bf16[8,6144]{1,0:T(8,128)(2,1)S(1)} %get-tuple-element.34), channel_id=1, source_target_pairs={{0,2},{1,3},{2,0},{3,1},{4,6},{5,7},{6,4},{7,5},{8,10},{9,11},{10,... | collective-permute-start | bytes 294920 | tf_op jit(solution)/shard_map/ppermute | solution.py:11
  11.1 8.5 %collective-permute-start.12 = (bf16[8,6144]{1,0:T(8,128)(2,1)S(1)}, bf16[8,6144]{1,0:T(8,128)(2,1)S(1)}, u32[]{:S(2)}, u32[]{:S(2)}) collective-permute-start(bf16[8,6144]{1,0:T(8,128)(2,1)S(1)} %get-tuple-element.35), channel_id=1, source_target_pairs={{0,3},{1,2},{2,1},{3,0},{4,7},{5,6},{6,5},{7,4},{8,11},{9,10},{10,... | collective-permute-start | bytes 294920 | tf_op jit(solution)/shard_map/ppermute | solution.py:11
  13.0 6.7 %collective-permute-start.13 = (bf16[8,6144]{1,0:T(8,128)(2,1)S(1)}, bf16[8,6144]{1,0:T(8,128)(2,1)S(1)}, u32[]{:S(2)}, u32[]{:S(2)}) collective-permute-start(bf16[8,6144]{1,0:T(8,128)(2,1)S(1)} %get-tuple-element.36), channel_id=1, source_target_pairs={{0,1},{1,0},{2,3},{3,2},{4,5},{5,4},{6,7},{7,6},{8,9},{9,8},{10,11... | collective-permute-start | bytes 294920 | tf_op jit(solution)/shard_map/ppermute | solution.py:11
  14.7 7.0 %collective-permute-start = (bf16[8,6144]{1,0:T(8,128)(2,1)S(1)}, bf16[8,6144]{1,0:T(8,128)(2,1)S(1)}, u32[]{:S(2)}, u32[]{:S(2)}) collective-permute-start(bf16[8,6144]{1,0:T(8,128)(2,1)S(1)} %get-tuple-element.22), channel_id=1, source_target_pairs={{0,2},{1,3},{2,0},{3,1},{4,6},{5,7},{6,4},{7,5},{8,10},{9,11},{10,... | collective-permute-start | bytes 294920 | tf_op jit(solution)/shard_map/ppermute | solution.py:11
  15.2 10.9 %collective-permute-start.6 = (f32[8,6144]{1,0:T(8,128)S(1)}, f32[8,6144]{1,0:T(8,128)S(1)}, u32[]{:S(2)}, u32[]{:S(2)}) collective-permute-start(f32[8,6144]{1,0:T(8,128)S(1)} %convert_add_fusion.2), channel_id=1, source_target_pairs={{0,12},{1,13},{2,14},{3,15},{4,8},{5,9},{6,10},{7,11},{8,4},{9,5},... | collective-permute-start | bytes 589832 | tf_op jit(solution)/shard_map/ppermute | solution.py:11
  18.9 17.8 %collective-permute-start.10 = (f32[8,6144]{1,0:T(8,128)S(1)}, f32[8,6144]{1,0:T(8,128)S(1)}, u32[]{:S(2)}, u32[]{:S(2)}) collective-permute-start(f32[8,6144]{1,0:T(8,128)S(1)} %convert_add_fusion.1), channel_id=1, source_target_pairs={{0,8},{1,9},{2,10},{3,11},{4,12},{5,13},{6,14},{7,15},{8,0},{9,1},... | collective-permute-start | bytes 589832 | tf_op jit(solution)/shard_map/ppermute | solution.py:11
  19.7 17.0 %collective-permute-start.14 = (f32[8,6144]{1,0:T(8,128)S(1)}, f32[8,6144]{1,0:T(8,128)S(1)}, u32[]{:S(2)}, u32[]{:S(2)}) collective-permute-start(f32[8,6144]{1,0:T(8,128)S(1)} %convert_add_fusion), channel_id=1, source_target_pairs={{0,4},{1,5},{2,6},{3,7},{4,0},{5,1},{6,2},{7,3},{8,12},{9,13},{10,... | collective-permute-start | bytes 589832 | tf_op jit(solution)/shard_map/ppermute | solution.py:11
  21.3 4.8 %collective-permute-start.1 = (bf16[8,6144]{1,0:T(8,128)(2,1)S(1)}, bf16[8,6144]{1,0:T(8,128)(2,1)S(1)}, u32[]{:S(2)}, u32[]{:S(2)}) collective-permute-start(bf16[8,6144]{1,0:T(8,128)(2,1)S(1)} %get-tuple-element.23), channel_id=1, source_target_pairs={{0,3},{1,2},{2,1},{3,0},{4,7},{5,6},{6,5},{7,4},{8,11},{9,10},{10,... | collective-permute-start | bytes 294920 | tf_op jit(solution)/shard_map/ppermute | solution.py:11
  21.7 4.4 %collective-permute-start.2 = (bf16[8,6144]{1,0:T(8,128)(2,1)S(1)}, bf16[8,6144]{1,0:T(8,128)(2,1)S(1)}, u32[]{:S(2)}, u32[]{:S(2)}) collective-permute-start(bf16[8,6144]{1,0:T(8,128)(2,1)S(1)} %get-tuple-element.24), channel_id=1, source_target_pairs={{0,1},{1,0},{2,3},{3,2},{4,5},{5,4},{6,7},{7,6},{8,9},{9,8},{10,11... | collective-permute-start | bytes 294920 | tf_op jit(solution)/shard_map/ppermute | solution.py:11
  38.6 10.9 %all-to-all-start = ((f32[32,1,128]{2,1,0:T(1,128)}), f32[32,1,128]{2,1,0:T(1,128)S(1)}, u32[]{:S(2)}, u32[]{:S(2)}) async-start(f32[32,1,128]{2,1,0:T(1,128)} %broadcast_in_dim.29), calls=%async_computation | async-start | bytes 32768 | tf_op jit(solution)/shard_map/all_to_all | solution.py:52
  51.1 6.5 %collective-permute-start.15 = (bf16[8,6144]{1,0:T(8,128)(2,1)S(1)}, bf16[8,6144]{1,0:T(8,128)(2,1)S(1)}, u32[]{:S(2)}, u32[]{:S(2)}) collective-permute-start(bf16[8,6144]{1,0:T(8,128)(2,1)S(1)} %get-tuple-element.38), channel_id=1, source_target_pairs={{0,2},{1,3},{2,0},{3,1},{4,6},{5,7},{6,4},{7,5},{8,10},{9,11},{10,... | collective-permute-start | bytes 294920 | tf_op jit(solution)/shard_map/ppermute | solution.py:11
  51.7 6.5 %collective-permute-start.16 = (bf16[8,6144]{1,0:T(8,128)(2,1)S(1)}, bf16[8,6144]{1,0:T(8,128)(2,1)S(1)}, u32[]{:S(2)}, u32[]{:S(2)}) collective-permute-start(bf16[8,6144]{1,0:T(8,128)(2,1)S(1)} %get-tuple-element.38), channel_id=1, source_target_pairs={{0,4},{1,5},{2,6},{3,7},{4,0},{5,1},{6,2},{7,3},{8,12},{9,13},{10,... | collective-permute-start | bytes 294920 | tf_op jit(solution)/shard_map/ppermute | solution.py:11
  52.3 10.1 %collective-permute-start.17 = (bf16[8,6144]{1,0:T(8,128)(2,1)S(1)}, bf16[8,6144]{1,0:T(8,128)(2,1)S(1)}, u32[]{:S(2)}, u32[]{:S(2)}) collective-permute-start(bf16[8,6144]{1,0:T(8,128)(2,1)S(1)} %get-tuple-element.38), channel_id=1, source_target_pairs={{0,6},{1,7},{2,4},{3,5},{4,2},{5,3},{6,0},{7,1},{8,14},{9,15},{10,... | collective-permute-start | bytes 294920 | tf_op jit(solution)/shard_map/ppermute | solution.py:11
  54.6 14.0 %collective-permute-start.18 = (bf16[8,6144]{1,0:T(8,128)(2,1)S(1)}, bf16[8,6144]{1,0:T(8,128)(2,1)S(1)}, u32[]{:S(2)}, u32[]{:S(2)}) collective-permute-start(bf16[8,6144]{1,0:T(8,128)(2,1)S(1)} %get-tuple-element.38), channel_id=1, source_target_pairs={{0,8},{1,9},{2,10},{3,11},{4,12},{5,13},{6,14},{7,15},{8,0},{9,1},... | collective-permute-start | bytes 294920 | tf_op jit(solution)/shard_map/ppermute | solution.py:11
  55.2 15.7 %collective-permute-start.19 = (bf16[8,6144]{1,0:T(8,128)(2,1)S(1)}, bf16[8,6144]{1,0:T(8,128)(2,1)S(1)}, u32[]{:S(2)}, u32[]{:S(2)}) collective-permute-start(bf16[8,6144]{1,0:T(8,128)(2,1)S(1)} %get-tuple-element.38), channel_id=1, source_target_pairs={{0,10},{1,11},{2,8},{3,9},{4,14},{5,15},{6,12},{7,13},{8,2},{9,3},... | collective-permute-start | bytes 294920 | tf_op jit(solution)/shard_map/ppermute | solution.py:11
  57.6 13.3 %collective-permute-start.20 = (bf16[8,6144]{1,0:T(8,128)(2,1)S(1)}, bf16[8,6144]{1,0:T(8,128)(2,1)S(1)}, u32[]{:S(2)}, u32[]{:S(2)}) collective-permute-start(bf16[8,6144]{1,0:T(8,128)(2,1)S(1)} %get-tuple-element.38), channel_id=1, source_target_pairs={{0,12},{1,13},{2,14},{3,15},{4,8},{5,9},{6,10},{7,11},{8,4},{9,5},... | collective-permute-start | bytes 294920 | tf_op jit(solution)/shard_map/ppermute | solution.py:11
  58.2 12.7 %collective-permute-start.21 = (bf16[8,6144]{1,0:T(8,128)(2,1)S(1)}, bf16[8,6144]{1,0:T(8,128)(2,1)S(1)}, u32[]{:S(2)}, u32[]{:S(2)}) collective-permute-start(bf16[8,6144]{1,0:T(8,128)(2,1)S(1)} %get-tuple-element.38), channel_id=1, source_target_pairs={{0,14},{1,15},{2,12},{3,13},{4,10},{5,11},{6,8},{7,9},{8,6},{9,7},... | collective-permute-start | bytes 294920 | tf_op jit(solution)/shard_map/ppermute | solution.py:11
  70.9 2.4 %collective-permute-start.22 = (bf16[8,8,6144]{2,1,0:T(8,128)(2,1)S(1)}, bf16[8,8,6144]{2,1,0:T(8,128)(2,1)S(1)}, u32[]{:S(2)}, u32[]{:S(2)}) collective-permute-start(bf16[8,8,6144]{2,1,0:T(8,128)(2,1)S(1)} %bitcast_dynamic-update-slice_fusion), channel_id=1, source_target_pairs={{0,1},{1,0},{2,3},{3,2},{4,5},{5,4},{6,7},{7,6},{8,9},{9,8},{10,11... | collective-permute-start | bytes 2359304 | tf_op jit(solution)/shard_map/ppermute | solution.py:11
  (4 other events, 168.0 us)
where the time goes:
time: 76.6 us; the launch traced here: 75.5 us
  waiting for transfers between devices  35 us (46%)
  starting transfers between devices  31 us (40%)
  other arithmetic  4.01 us (5%)
  local copies, waits for them, and re-layouts  3.77 us (5%)
  between operations  1.65 us (2%)
    ppermute x23, waiting for transfers between devices, _swap(): return lax.ppermute(array, 'dp', [(i, i ^ offset) for i in range(size)])  28.1 us
    ppermute x23, starting transfers between devices, _swap(): return lax.ppermute(array, 'dp', [(i, i ^ offset) for i in range(size)])  27.3 us
    all_to_all x1, waiting for transfers between devices, shards(): squares = lax.all_to_all(square, ('expert', 'dp'), 0, 0)  6.91 us
    all_to_all x1, starting transfers between devices, shards(): squares = lax.all_to_all(square, ('expert', 'dp'), 0, 0)  3.77 us
    squeeze x1, local copies, waits for them, and re-layouts, _pick(): return lax.dynamic_index_in_dim(array, index, 0, keepdims=False)  1.61 us
  transfers between devices with their start and end apart: 24, of which 9 were waited for; matrix products, arithmetic and copies ran while one was open for 2% of the time, Pallas kernels for 0%

commit v1 on v0

v1 whole, which is shorter than its diff:
```python
import functools

import jax
import jax.numpy as jnp
from jax import lax
from jax.experimental import pallas as pl
from jax.experimental.pallas import tpu as pltpu
from jax.sharding import PartitionSpec as P

STEP = 10
NEAR = 4
VMEM = pl.BlockSpec(memory_space=pltpu.VMEM)


def _swap(array, size, offset):
    return lax.ppermute(array, "dp", [(i, i ^ offset) for i in range(size)])


def _pick(array, index):
    return lax.dynamic_index_in_dim(array, index, 0, keepdims=False)


def _call(body, outs, *args):
    return pl.pallas_call(
        body,
        out_shape=outs,
        in_specs=[VMEM] * len(args),
        out_specs=[VMEM] * len(outs),
        cost_estimate=pl.CostEstimate(flops=1000000, bytes_accessed=1000000, transcendentals=0),
    )(*(pltpu.with_memory_space_constraint(arg, pltpu.VMEM) for arg in args))


def _far_order(size):
    far = size // NEAR
    return [far - 2, far - 1, *reversed(range(far - 2))]


def _near_sums(grads, rows, width, size):
    far = size // NEAR
    me = lax.axis_index("dp")
    far_at, near_at = me // NEAR, me % NEAR
    blocks = grads.reshape(far, NEAR, rows, width)
    order = _far_order(size)
    pieces = []
    for k in order:
        group = _pick(blocks, far_at ^ k)
        pieces.append([_pick(group, near_at ^ j) for j in range(NEAR)])
    pieces = lax.optimization_barrier(pieces)
    moved = []
    for k, piece in zip(order, pieces):
        moved.append([_swap(piece[j], size, j) for j in (2, 3, 1)])
    sums = {}
    for k, piece, others in zip(order, pieces, moved):
        total = piece[0].astype(jnp.float32)
        for other in others:
            total = total + other.astype(jnp.float32)
        sums[k] = total
    return sums


def _finish_sum(*refs):
    *parts, summed, square = refs
    total = parts[0][...]
    for part in parts[1:]:
        total = total + part[...]
    summed[...] = total
    own = jnp.sum(jnp.sum(total * total, axis=1, keepdims=True), axis=0, keepdims=True)
    square[...] = jnp.broadcast_to(own[None], square.shape)


def _update(squares, summed, master, first, second):
    norm = jnp.sqrt(jnp.sum(squares[...], axis=0))[:, :1]
    clip = 1.0 / jnp.maximum(norm, 1.0)
    clipped = clip * summed[...]
    new_first = 0.9 * first[...] + 0.1 * clipped
    new_second = 0.95 * second[...] + 0.05 * (clipped * clipped)
    first_fix = 1.0 - 0.9**STEP
    second_fix = 1.0 - 0.95**STEP
    direction = new_first / first_fix / (jnp.sqrt(new_second / second_fix) + 1e-08)
    new_master = master[...] - 0.001 * (direction + 0.1 * master[...])
    return new_master, new_first, new_second, direction


def _weights(squares, summed, master, first, second, own):
    own[...] = _update(squares, summed, master, first, second)[0].astype(jnp.bfloat16)


def _states(squares, summed, master, first, second, *outs):
    for out, value in zip(outs, _update(squares, summed, master, first, second)):
        out[...] = value


def _place(size, *refs):
    *groups, out, done = refs
    me = lax.axis_index("dp")
    far = size // NEAR
    copies = []
    for g, group in enumerate(groups):
        for k in range(far):
            offset = k * NEAR + g
            copies.append(pltpu.make_async_copy(group.at[k], out.at[me ^ offset], done.at[offset]))
    for copy in copies:
        copy.start()
    for copy in copies:
        copy.wait()


def _step(size, grads, master, first, second):
    rows, width = master.shape
    f32 = jax.ShapeDtypeStruct((rows, width), jnp.float32)
    order = _far_order(size)
    sums = _near_sums(grads, rows, width, size)
    parts = [sums[0]]
    for k in order[:-1]:
        parts.append(_swap(sums[k], size, k * NEAR))

    devices = size * lax.axis_size("expert")
    kept = pltpu.VMEM((rows, width), jnp.float32)
    square = pltpu.VMEM((devices, 1, 128), jnp.float32)
    summed, square = _call(_finish_sum, (kept, square), *parts)
    squares = lax.all_to_all(square, ("expert", "dp"), 0, 0)
    state = (squares, summed, master, first, second)
    (own,) = _call(_weights, (pltpu.VMEM((rows, width), jnp.bfloat16),), *state)
    results = _call(_states, (f32,) * 4, *state)

    here, there = {0: own}, {}
    for k in order[:-1]:
        here[k] = _swap(own, size, k * NEAR)
    for k in (0, *order[:-1]):
        there[k] = _swap(here[k], size, 2)
    here = jnp.stack([here[k] for k in range(size // NEAR)])
    there = jnp.stack([there[k] for k in range(size // NEAR)])
    here_pair = _swap(here, size, 1)
    there_pair = _swap(there, size, 1)
    new_weights = pl.pallas_call(
        functools.partial(_place, size),
        out_shape=jax.ShapeDtypeStruct((size, rows, width), jnp.bfloat16),
        in_specs=[VMEM] * 4,
        out_specs=pl.BlockSpec(memory_space=pl.ANY),
        scratch_shapes=[pltpu.SemaphoreType.DMA((size,))],
    )(*(pltpu.with_memory_space_constraint(x, pltpu.VMEM) for x in (here, here_pair, there, there_pair)))
    return results, new_weights


def shards(size, grads, master, first_moment, second_moment):
    results, new_weights = _step(size, grads[0, 0], master[0], first_moment[0], second_moment[0])
    new_weights = new_weights.reshape(1, -1, master.shape[2])
    return (*(result[None] for result in results), new_weights)


def solution(mesh):
    state = P("expert", "dp", None)
    size = mesh.shape["dp"]
    return jax.shard_map(
        functools.partial(shards, size),
        mesh=mesh,
        in_specs=(P("expert", "dp", None, None), state, state, state),
        out_specs=(state, state, state, state, P("expert", None, None)),
        check_vma=False,
    )
```

time: 76.6 us -> 78.1 us (1.020); the launches traced: 75.5 us -> 77.9 us
  blocking collectives: 0 us -> 11.6 us
  starting transfers between devices: 31 us -> 25.4 us
  other arithmetic: 4.01 us -> 0.32 us
  Pallas kernels: 0 us -> 2.84 us
  local copies, waits for them, and re-layouts: 3.77 us -> 1.62 us
  between operations: 1.65 us -> 0.83 us
    all_to_all x0 -> x1, blocking collectives: none -> 11.6 us  [_step(): squares = lax.all_to_all(square, ('expert', 'dp'), 0, 0)]
    ppermute x23 -> x24, waiting for transfers between devices: 28.1 us -> 35.3 us  [_swap(): return lax.ppermute(array, 'dp', [(i, i ^ offset) for i in range(size)])]
    all_to_all x1 -> x0, waiting for transfers between devices: 6.91 us -> none  [shards(): squares = lax.all_to_all(square, ('expert', 'dp'), 0, 0)]
    all_to_all x1 -> x0, starting transfers between devices: 3.77 us -> none  [shards(): squares = lax.all_to_all(square, ('expert', 'dp'), 0, 0)]
    pallas_call x0 -> x4, Pallas kernels: none -> 2.84 us  [the longest x3 1.58 us: _call(): pl.pallas_call(body, out_shape=outs, in_specs=[VMEM] * len(args), out_spe...]
    ppermute x23 -> x24, starting transfers between devices: 27.3 us -> 25.4 us  [_swap(): return lax.ppermute(array, 'dp', [(i, i ^ offset) for i in range(size)])]
    broadcast_in_dim x3 -> x0, local copies, waits for them, and re-layouts: 1.43 us -> none  [the longest x1 1.26 us: shards(): square = jnp.broadcast_to(jnp.sum(summed * summed), (devices, 1, 128))]
    select_n x2 -> x0, other arithmetic: 1.36 us -> none  [shards(): full = jnp.take(full, jnp.arange(size) ^ me, axis=0)]
  transfers between devices with their start and end apart: 24 -> 24, of which waited for: 9 -> 12; matrix products, arithmetic and copies ran while one was open for 2% -> 0% of each run, Pallas kernels for 0% -> 1%
where the time goes in v1:
time: 78.1 us; the launch traced here: 77.9 us
  waiting for transfers between devices  35.3 us (45%)
  starting transfers between devices  25.4 us (33%)
  blocking collectives  11.6 us (15%)
  Pallas kernels  2.84 us (4%)
  local copies, waits for them, and re-layouts  1.62 us (2%)
  between operations  0.83 us (1%)
    ppermute x24, waiting for transfers between devices, _swap(): return lax.ppermute(array, 'dp', [(i, i ^ offset) for i in range(size)])  35.3 us
    ppermute x24, starting transfers between devices, _swap(): return lax.ppermute(array, 'dp', [(i, i ^ offset) for i in range(size)])  25.4 us
    all_to_all x1, blocking collectives, _step(): squares = lax.all_to_all(square, ('expert', 'dp'), 0, 0)  11.6 us
    squeeze x1, local copies, waits for them, and re-layouts, _pick(): return lax.dynamic_index_in_dim(array, index, 0, keepdims=False)  1.6 us
    pallas_call x3, Pallas kernels, _call(): pl.pallas_call(body, out_shape=outs, in_specs=[VMEM] * len(args), out_spe...  1.58 us
  transfers between devices with their start and end apart: 24, of which 12 were waited for; matrix products, arithmetic and copies ran while one was open for 0% of the time, Pallas kernels for 1%

profile of v1, /device:TPU:0, one launch (start us, length us, event | category | flops | bytes accessed | tf_op | source)
XLA Modules:
  0.0 77.9 jit_solution(16980969791862563726)
XLA Ops:
  0.7 1.6 %dynamic-slice_bitcast_fusion = (bf16[8,6144]{1,0:T(8,128)(2,1)S(1)}, bf16[8,6144]{1,0:T(8,128)(2,1)S(1)}, bf16[8,6144]{1,0:T(8,128)(2,1)S(1)}, bf16[8,6144]{1,0...) fusion(bf16[4,4,8,6144]{3,2,1,0:T(8,128)(2,1)} %bitcast.56, ...), kind=kLoop, calls=%fused_computation.6 | loop fusion | bytes 3145760 | tf_op jit(solution)/shard_map/jit(dynamic_index_in_dim)/squeeze | solution.py:20
  2.3 3.1 %collective-permute-start.7 = (bf16[8,6144]{1,0:T(8,128)(2,1)S(1)}, bf16[8,6144]{1,0:T(8,128)(2,1)S(1)}, u32[]{:S(2)}, u32[]{:S(2)}) collective-permute-start(bf16[8,6144]{1,0:T(8,128)(2,1)S(1)} %get-tuple-element.36), channel_id=1, source_target_pairs={{0,2},{1,3},{2,0},{3,1},{4,6},{5,7},{6,4},{7,5},{8,10},{9,11},{10,... | collective-permute-start | bytes 294920 | tf_op jit(solution)/shard_map/ppermute | solution.py:16
  5.6 1.9 %collective-permute-start = (bf16[8,6144]{1,0:T(8,128)(2,1)S(1)}, bf16[8,6144]{1,0:T(8,128)(2,1)S(1)}, u32[]{:S(2)}, u32[]{:S(2)}) collective-permute-start(bf16[8,6144]{1,0:T(8,128)(2,1)S(1)} %get-tuple-element.28), channel_id=1, source_target_pairs={{0,2},{1,3},{2,0},{3,1},{4,6},{5,7},{6,4},{7,5},{8,10},{9,11},{10,... | collective-permute-start | bytes 294920 | tf_op jit(solution)/shard_map/ppermute | solution.py:16
  8.6 2.5 %collective-permute-start.11 = (bf16[8,6144]{1,0:T(8,128)(2,1)S(1)}, bf16[8,6144]{1,0:T(8,128)(2,1)S(1)}, u32[]{:S(2)}, u32[]{:S(2)}) collective-permute-start(bf16[8,6144]{1,0:T(8,128)(2,1)S(1)} %get-tuple-element.40), channel_id=1, source_target_pairs={{0,2},{1,3},{2,0},{3,1},{4,6},{5,7},{6,4},{7,5},{8,10},{9,11},{10,... | collective-permute-start | bytes 294920 | tf_op jit(solution)/shard_map/ppermute | solution.py:16
  11.1 1.8 %collective-permute-start.12 = (bf16[8,6144]{1,0:T(8,128)(2,1)S(1)}, bf16[8,6144]{1,0:T(8,128)(2,1)S(1)}, u32[]{:S(2)}, u32[]{:S(2)}) collective-permute-start(bf16[8,6144]{1,0:T(8,128)(2,1)S(1)} %get-tuple-element.41), channel_id=1, source_target_pairs={{0,3},{1,2},{2,1},{3,0},{4,7},{5,6},{6,5},{7,4},{8,11},{9,10},{10,... | collective-permute-start | bytes 294920 | tf_op jit(solution)/shard_map/ppermute | solution.py:16
  13.0 4.0 %collective-permute-done.11 = bf16[8,6144]{1,0:T(8,128)(2,1)S(1)} collective-permute-done((bf16[8,6144]{1,0:T(8,128)(2,1)S(1)}, bf16[8,6144]{1,0:T(8,128)(2,1)S(1)}, u32[]{:S(2)}, u32[]{:S(2)}) %collective-permute-start.11) | collective-permute-done | bytes 98336 | tf_op jit(solution)/shard_map/ppermute | solution.py:16
  16.9 2.5 %collective-permute-start.3 = (bf16[8,6144]{1,0:T(8,128)(2,1)S(1)}, bf16[8,6144]{1,0:T(8,128)(2,1)S(1)}, u32[]{:S(2)}, u32[]{:S(2)}) collective-permute-start(bf16[8,6144]{1,0:T(8,128)(2,1)S(1)} %get-tuple-element.32), channel_id=1, source_target_pairs={{0,2},{1,3},{2,0},{3,1},{4,6},{5,7},{6,4},{7,5},{8,10},{9,11},{10,... | collective-permute-start | bytes 294920 | tf_op jit(solution)/shard_map/ppermute | solution.py:16
  19.4 1.3 %collective-permute-start.4 = (bf16[8,6144]{1,0:T(8,128)(2,1)S(1)}, bf16[8,6144]{1,0:T(8,128)(2,1)S(1)}, u32[]{:S(2)}, u32[]{:S(2)}) collective-permute-start(bf16[8,6144]{1,0:T(8,128)(2,1)S(1)} %get-tuple-element.33), channel_id=1, source_target_pairs={{0,3},{1,2},{2,1},{3,0},{4,7},{5,6},{6,5},{7,4},{8,11},{9,10},{10,... | collective-permute-start | bytes 294920 | tf_op jit(solution)/shard_map/ppermute | solution.py:16
  20.8 1.3 %collective-permute-done.3 = bf16[8,6144]{1,0:T(8,128)(2,1)S(1)} collective-permute-done((bf16[8,6144]{1,0:T(8,128)(2,1)S(1)}, bf16[8,6144]{1,0:T(8,128)(2,1)S(1)}, u32[]{:S(2)}, u32[]{:S(2)}) %collective-permute-start.3) | collective-permute-done | bytes 98336 | tf_op jit(solution)/shard_map/ppermute | solution.py:16
  22.0 2.1 %collective-permute-done.4 = bf16[8,6144]{1,0:T(8,128)(2,1)S(1)} collective-permute-done((bf16[8,6144]{1,0:T(8,128)(2,1)S(1)}, bf16[8,6144]{1,0:T(8,128)(2,1)S(1)}, u32[]{:S(2)}, u32[]{:S(2)}) %collective-permute-start.4) | collective-permute-done | bytes 98336 | tf_op jit(solution)/shard_map/ppermute | solution.py:16
  24.1 1.8 %collective-permute-start.14 = (f32[8,6144]{1,0:T(8,128)S(1)}, f32[8,6144]{1,0:T(8,128)S(1)}, u32[]{:S(2)}, u32[]{:S(2)}) collective-permute-start(f32[8,6144]{1,0:T(8,128)S(1)} %convert_add_fusion), channel_id=1, source_target_pairs={{0,4},{1,5},{2,6},{3,7},{4,0},{5,1},{6,2},{7,3},{8,12},{9,13},{10,... | collective-permute-start | bytes 589832 | tf_op jit(solution)/shard_map/ppermute | solution.py:16
  25.9 2.5 %collective-permute-start.10 = (f32[8,6144]{1,0:T(8,128)S(1)}, f32[8,6144]{1,0:T(8,128)S(1)}, u32[]{:S(2)}, u32[]{:S(2)}) collective-permute-start(f32[8,6144]{1,0:T(8,128)S(1)} %convert_add_fusion.1), channel_id=1, source_target_pairs={{0,12},{1,13},{2,14},{3,15},{4,8},{5,9},{6,10},{7,11},{8,4},{9,5},... | collective-permute-start | bytes 589832 | tf_op jit(solution)/shard_map/ppermute | solution.py:16
  28.7 2.5 %collective-permute-done.14.refs_3_ = f32[8,6144]{1,0:T(8,128)S(1)} collective-permute-done((f32[8,6144]{1,0:T(8,128)S(1)}, f32[8,6144]{1,0:T(8,128)S(1)}, u32[]{:S(2)}, u32[]{:S(2)}) %collective-permute-start.14) | collective-permute-done | bytes 196640 | tf_op jit(solution)/shard_map/ppermute | solution.py:16
  31.2 7.2 %collective-permute-done.10.refs_2_ = f32[8,6144]{1,0:T(8,128)S(1)} collective-permute-done((f32[8,6144]{1,0:T(8,128)S(1)}, f32[8,6144]{1,0:T(8,128)S(1)}, u32[]{:S(2)}, u32[]{:S(2)}) %collective-permute-start.10) | collective-permute-done | bytes 196640 | tf_op jit(solution)/shard_map/ppermute | solution.py:16
  38.4 7.4 %collective-permute-done.6.refs_1_ = f32[8,6144]{1,0:T(8,128)S(1)} collective-permute-done((f32[8,6144]{1,0:T(8,128)S(1)}, f32[8,6144]{1,0:T(8,128)S(1)}, u32[]{:S(2)}, u32[]{:S(2)}) %collective-permute-start.6) | collective-permute-done | bytes 196640 | tf_op jit(solution)/shard_map/ppermute | solution.py:16
  46.0 11.6 %all_to_all.5.squares = f32[32,1,128]{2,1,0:T(1,128)S(1)} all-to-all(f32[32,1,128]{2,1,0:T(1,128)S(1)} %get-tuple-element.43), channel_id=1, replica_groups=mesh['expert'=2,'dp'=16] {'expert','dp'}, dimensions={0} | all-to-all | bytes 32768 | tf_op jit(solution)/shard_map/all_to_all | solution.py:121
  58.5 1.5 %collective-permute-start.16 = (bf16[8,6144]{1,0:T(8,128)(2,1)S(1)}, bf16[8,6144]{1,0:T(8,128)(2,1)S(1)}, u32[]{:S(2)}, u32[]{:S(2)}) collective-permute-start(bf16[8,6144]{1,0:T(8,128)(2,1)S(1)} %shard_map.85), channel_id=1, source_target_pairs={{0,8},{1,9},{2,10},{3,11},{4,12},{5,13},{6,14},{7,15},{8,0},{9,1},... | collective-permute-start | bytes 294920 | tf_op jit(solution)/shard_map/ppermute | solution.py:16
  59.9 2.4 %collective-permute-start.15 = (bf16[8,6144]{1,0:T(8,128)(2,1)S(1)}, bf16[8,6144]{1,0:T(8,128)(2,1)S(1)}, u32[]{:S(2)}, u32[]{:S(2)}) collective-permute-start(bf16[8,6144]{1,0:T(8,128)(2,1)S(1)} %shard_map.85), channel_id=1, source_target_pairs={{0,4},{1,5},{2,6},{3,7},{4,0},{5,1},{6,2},{7,3},{8,12},{9,13},{10,... | collective-permute-start | bytes 294920 | tf_op jit(solution)/shard_map/ppermute | solution.py:16
  62.9 2.6 %collective-permute-done.17 = bf16[8,6144]{1,0:T(8,128)(2,1)S(1)} collective-permute-done((bf16[8,6144]{1,0:T(8,128)(2,1)S(1)}, bf16[8,6144]{1,0:T(8,128)(2,1)S(1)}, u32[]{:S(2)}, u32[]{:S(2)}) %collective-permute-start.17) | collective-permute-done | bytes 98336 | tf_op jit(solution)/shard_map/ppermute | solution.py:16
  66.0 2.8 %collective-permute-done.16 = bf16[8,6144]{1,0:T(8,128)(2,1)S(1)} collective-permute-done((bf16[8,6144]{1,0:T(8,128)(2,1)S(1)}, bf16[8,6144]{1,0:T(8,128)(2,1)S(1)}, u32[]{:S(2)}, u32[]{:S(2)}) %collective-permute-start.16) | collective-permute-done | bytes 98336 | tf_op jit(solution)/shard_map/ppermute | solution.py:16
  69.5 1.4 %collective-permute-start.20 = (bf16[8,6144]{1,0:T(8,128)(2,1)S(1)}, bf16[8,6144]{1,0:T(8,128)(2,1)S(1)}, u32[]{:S(2)}, u32[]{:S(2)}) collective-permute-start(bf16[8,6144]{1,0:T(8,128)(2,1)S(1)} %collective-permute-done.15), channel_id=1, source_target_pairs={{0,2},{1,3},{2,0},{3,1},{4,6},{5,7},{6,4},{7,5},{8,10},{9,11},{10,... | collective-permute-start | bytes 294920 | tf_op jit(solution)/shard_map/ppermute | solution.py:16
  71.0 2.7 %collective-permute-done.21 = bf16[8,6144]{1,0:T(8,128)(2,1)S(1)} collective-permute-done((bf16[8,6144]{1,0:T(8,128)(2,1)S(1)}, bf16[8,6144]{1,0:T(8,128)(2,1)S(1)}, u32[]{:S(2)}, u32[]{:S(2)}) %collective-permute-start.21) | collective-permute-done | bytes 98336 | tf_op jit(solution)/shard_map/ppermute | solution.py:16
  74.9 1.1 %shard_map.84 = (f32[8,6144]{1,0:T(8,128)}, f32[8,6144]{1,0:T(8,128)}, f32[8,6144]{1,0:T(8,128)}, f32[8,6144]{1,0:T(8,128)}) custom-call(f32[32,1,128]{2,1,0:T(1,128)S(1)} %all_to_all.5.squares, f32[8,6144]{1,0:T(8,128)S(1)} %get-tuple-element.44.summed, f32[8,6144]{1,0:T(8,128)S(1)} %bitcast.50, f32[8,6144]{1,0:T(8,128)S(1)} %bitcast.52, f32[8,6144]{1,0:T(8,128)S(1)} %bitcast.54), custom_call_target="tpu_custom_call" | custom-call | flops 1000000 | bytes 1000000 | tf_op jit(solution)/shard_map/pallas_call | solution.py:24
  76.6 1.3 %shard_map.86 = bf16[16,8,6144]{2,1,0:T(8,128)(2,1)} custom-call(bf16[4,8,6144]{2,1,0:T(8,128)(2,1)S(1)} %pad_maximum_fusion.refs_0_, bf16[4,8,6144]{2,1,0:T(8,128)(2,1)S(1)} %collective-permute-done.18.refs_1_, bf16[4,8,6144]{2,1,0:T(8,128)(2,1)S(1)} %pad_maximum_fusion.1.refs_2_, bf16[4,8,6144]{2,1,0:T(8,128)(2,1)S(1)} %collective-permute-done.23.refs_3_), custom_call_target="tpu_custom_call" | custom-call | tf_op jit(solution)/shard_map/pallas_call | solution.py:135
  (42 shorter events, 6.4 us)
Async XLA Ops:
  2.3 6.2 %collective-permute-start.7 = (bf16[8,6144]{1,0:T(8,128)(2,1)S(1)}, bf16[8,6144]{1,0:T(8,128)(2,1)S(1)}, u32[]{:S(2)}, u32[]{:S(2)}) collective-permute-start(bf16[8,6144]{1,0:T(8,128)(2,1)S(1)} %get-tuple-element.36), channel_id=1, source_target_pairs={{0,2},{1,3},{2,0},{3,1},{4,6},{5,7},{6,4},{7,5},{8,10},{9,11},{10,... | collective-permute-start | bytes 294920 | tf_op jit(solution)/shard_map/ppermute | solution.py:16
  5.4 5.7 %collective-permute-start.8 = (bf16[8,6144]{1,0:T(8,128)(2,1)S(1)}, bf16[8,6144]{1,0:T(8,128)(2,1)S(1)}, u32[]{:S(2)}, u32[]{:S(2)}) collective-permute-start(bf16[8,6144]{1,0:T(8,128)(2,1)S(1)} %get-tuple-element.37), channel_id=1, source_target_pairs={{0,3},{1,2},{2,1},{3,0},{4,7},{5,6},{6,5},{7,4},{8,11},{9,10},{10,... | collective-permute-start | bytes 294920 | tf_op jit(solution)/shard_map/ppermute | solution.py:16
  5.4 7.5 %collective-permute-start.9 = (bf16[8,6144]{1,0:T(8,128)(2,1)S(1)}, bf16[8,6144]{1,0:T(8,128)(2,1)S(1)}, u32[]{:S(2)}, u32[]{:S(2)}) collective-permute-start(bf16[8,6144]{1,0:T(8,128)(2,1)S(1)} %get-tuple-element.38), channel_id=1, source_target_pairs={{0,1},{1,0},{2,3},{3,2},{4,5},{5,4},{6,7},{7,6},{8,9},{9,8},{10,11... | collective-permute-start | bytes 294920 | tf_op jit(solution)/shard_map/ppermute | solution.py:16
  5.6 22.8 %collective-permute-start = (bf16[8,6144]{1,0:T(8,128)(2,1)S(1)}, bf16[8,6144]{1,0:T(8,128)(2,1)S(1)}, u32[]{:S(2)}, u32[]{:S(2)}) collective-permute-start(bf16[8,6144]{1,0:T(8,128)(2,1)S(1)} %get-tuple-element.28), channel_id=1, source_target_pairs={{0,2},{1,3},{2,0},{3,1},{4,6},{5,7},{6,4},{7,5},{8,10},{9,11},{10,... | collective-permute-start | bytes 294920 | tf_op jit(solution)/shard_map/ppermute | solution.py:16
  7.6 21.1 %collective-permute-start.1 = (bf16[8,6144]{1,0:T(8,128)(2,1)S(1)}, bf16[8,6144]{1,0:T(8,128)(2,1)S(1)}, u32[]{:S(2)}, u32[]{:S(2)}) collective-permute-start(bf16[8,6144]{1,0:T(8,128)(2,1)S(1)} %get-tuple-element.29), channel_id=1, source_target_pairs={{0,3},{1,2},{2,1},{3,0},{4,7},{5,6},{6,5},{7,4},{8,11},{9,10},{10,... | collective-permute-start | bytes 294920 | tf_op jit(solution)/shard_map/ppermute | solution.py:16
  8.6 8.3 %collective-permute-start.11 = (bf16[8,6144]{1,0:T(8,128)(2,1)S(1)}, bf16[8,6144]{1,0:T(8,128)(2,1)S(1)}, u32[]{:S(2)}, u32[]{:S(2)}) collective-permute-start(bf16[8,6144]{1,0:T(8,128)(2,1)S(1)} %get-tuple-element.40), channel_id=1, source_target_pairs={{0,2},{1,3},{2,0},{3,1},{4,6},{5,7},{6,4},{7,5},{8,10},{9,11},{10,... | collective-permute-start | bytes 294920 | tf_op jit(solution)/shard_map/ppermute | solution.py:16
  11.1 8.3 %collective-permute-start.12 = (bf16[8,6144]{1,0:T(8,128)(2,1)S(1)}, bf16[8,6144]{1,0:T(8,128)(2,1)S(1)}, u32[]{:S(2)}, u32[]{:S(2)}) collective-permute-start(bf16[8,6144]{1,0:T(8,128)(2,1)S(1)} %get-tuple-element.41), channel_id=1, source_target_pairs={{0,3},{1,2},{2,1},{3,0},{4,7},{5,6},{6,5},{7,4},{8,11},{9,10},{10,... | collective-permute-start | bytes 294920 | tf_op jit(solution)/shard_map/ppermute | solution.py:16
  12.9 7.8 %collective-permute-start.13 = (bf16[8,6144]{1,0:T(8,128)(2,1)S(1)}, bf16[8,6144]{1,0:T(8,128)(2,1)S(1)}, u32[]{:S(2)}, u32[]{:S(2)}) collective-permute-start(bf16[8,6144]{1,0:T(8,128)(2,1)S(1)} %get-tuple-element.42), channel_id=1, source_target_pairs={{0,1},{1,0},{2,3},{3,2},{4,5},{5,4},{6,7},{7,6},{8,9},{9,8},{10,11... | collective-permute-start | bytes 294920 | tf_op jit(solution)/shard_map/ppermute | solution.py:16
  16.9 5.1 %collective-permute-start.3 = (bf16[8,6144]{1,0:T(8,128)(2,1)S(1)}, bf16[8,6144]{1,0:T(8,128)(2,1)S(1)}, u32[]{:S(2)}, u32[]{:S(2)}) collective-permute-start(bf16[8,6144]{1,0:T(8,128)(2,1)S(1)} %get-tuple-element.32), channel_id=1, source_target_pairs={{0,2},{1,3},{2,0},{3,1},{4,6},{5,7},{6,4},{7,5},{8,10},{9,11},{10,... | collective-permute-start | bytes 294920 | tf_op jit(solution)/shard_map/ppermute | solution.py:16
  19.4 4.7 %collective-permute-start.4 = (bf16[8,6144]{1,0:T(8,128)(2,1)S(1)}, bf16[8,6144]{1,0:T(8,128)(2,1)S(1)}, u32[]{:S(2)}, u32[]{:S(2)}) collective-permute-start(bf16[8,6144]{1,0:T(8,128)(2,1)S(1)} %get-tuple-element.33), channel_id=1, source_target_pairs={{0,3},{1,2},{2,1},{3,0},{4,7},{5,6},{6,5},{7,4},{8,11},{9,10},{10,... | collective-permute-start | bytes 294920 | tf_op jit(solution)/shard_map/ppermute | solution.py:16
  20.7 5.2 %collective-permute-start.5 = (bf16[8,6144]{1,0:T(8,128)(2,1)S(1)}, bf16[8,6144]{1,0:T(8,128)(2,1)S(1)}, u32[]{:S(2)}, u32[]{:S(2)}) collective-permute-start(bf16[8,6144]{1,0:T(8,128)(2,1)S(1)} %get-tuple-element.34), channel_id=1, source_target_pairs={{0,1},{1,0},{2,3},{3,2},{4,5},{5,4},{6,7},{7,6},{8,9},{9,8},{10,11... | collective-permute-start | bytes 294920 | tf_op jit(solution)/shard_map/ppermute | solution.py:16
  22.0 6.6 %collective-permute-start.2 = (bf16[8,6144]{1,0:T(8,128)(2,1)S(1)}, bf16[8,6144]{1,0:T(8,128)(2,1)S(1)}, u32[]{:S(2)}, u32[]{:S(2)}) collective-permute-start(bf16[8,6144]{1,0:T(8,128)(2,1)S(1)} %get-tuple-element.30), channel_id=1, source_target_pairs={{0,1},{1,0},{2,3},{3,2},{4,5},{5,4},{6,7},{7,6},{8,9},{9,8},{10,11... | collective-permute-start | bytes 294920 | tf_op jit(solution)/shard_map/ppermute | solution.py:16
  24.1 7.1 %collective-permute-start.14 = (f32[8,6144]{1,0:T(8,128)S(1)}, f32[8,6144]{1,0:T(8,128)S(1)}, u32[]{:S(2)}, u32[]{:S(2)}) collective-permute-start(f32[8,6144]{1,0:T(8,128)S(1)} %convert_add_fusion), channel_id=1, source_target_pairs={{0,4},{1,5},{2,6},{3,7},{4,0},{5,1},{6,2},{7,3},{8,12},{9,13},{10,... | collective-permute-start | bytes 589832 | tf_op jit(solution)/shard_map/ppermute | solution.py:16
  25.9 12.5 %collective-permute-start.10 = (f32[8,6144]{1,0:T(8,128)S(1)}, f32[8,6144]{1,0:T(8,128)S(1)}, u32[]{:S(2)}, u32[]{:S(2)}) collective-permute-start(f32[8,6144]{1,0:T(8,128)S(1)} %convert_add_fusion.1), channel_id=1, source_target_pairs={{0,12},{1,13},{2,14},{3,15},{4,8},{5,9},{6,10},{7,11},{8,4},{9,5},... | collective-permute-start | bytes 589832 | tf_op jit(solution)/shard_map/ppermute | solution.py:16
  28.4 17.4 %collective-permute-start.6 = (f32[8,6144]{1,0:T(8,128)S(1)}, f32[8,6144]{1,0:T(8,128)S(1)}, u32[]{:S(2)}, u32[]{:S(2)}) collective-permute-start(f32[8,6144]{1,0:T(8,128)S(1)} %convert_add_fusion.2), channel_id=1, source_target_pairs={{0,8},{1,9},{2,10},{3,11},{4,12},{5,13},{6,14},{7,15},{8,0},{9,1},... | collective-permute-start | bytes 589832 | tf_op jit(solution)/shard_map/ppermute | solution.py:16
  57.9 7.6 %collective-permute-start.17 = (bf16[8,6144]{1,0:T(8,128)(2,1)S(1)}, bf16[8,6144]{1,0:T(8,128)(2,1)S(1)}, u32[]{:S(2)}, u32[]{:S(2)}) collective-permute-start(bf16[8,6144]{1,0:T(8,128)(2,1)S(1)} %shard_map.85), channel_id=1, source_target_pairs={{0,12},{1,13},{2,14},{3,15},{4,8},{5,9},{6,10},{7,11},{8,4},{9,5},... | collective-permute-start | bytes 294920 | tf_op jit(solution)/shard_map/ppermute | solution.py:16
  58.5 10.4 %collective-permute-start.16 = (bf16[8,6144]{1,0:T(8,128)(2,1)S(1)}, bf16[8,6144]{1,0:T(8,128)(2,1)S(1)}, u32[]{:S(2)}, u32[]{:S(2)}) collective-permute-start(bf16[8,6144]{1,0:T(8,128)(2,1)S(1)} %shard_map.85), channel_id=1, source_target_pairs={{0,8},{1,9},{2,10},{3,11},{4,12},{5,13},{6,14},{7,15},{8,0},{9,1},... | collective-permute-start | bytes 294920 | tf_op jit(solution)/shard_map/ppermute | solution.py:16
  59.9 9.5 %collective-permute-start.15 = (bf16[8,6144]{1,0:T(8,128)(2,1)S(1)}, bf16[8,6144]{1,0:T(8,128)(2,1)S(1)}, u32[]{:S(2)}, u32[]{:S(2)}) collective-permute-start(bf16[8,6144]{1,0:T(8,128)(2,1)S(1)} %shard_map.85), channel_id=1, source_target_pairs={{0,4},{1,5},{2,6},{3,7},{4,0},{5,1},{6,2},{7,3},{8,12},{9,13},{10,... | collective-permute-start | bytes 294920 | tf_op jit(solution)/shard_map/ppermute | solution.py:16
  62.3 8.7 %collective-permute-start.19 = (bf16[8,6144]{1,0:T(8,128)(2,1)S(1)}, bf16[8,6144]{1,0:T(8,128)(2,1)S(1)}, u32[]{:S(2)}, u32[]{:S(2)}) collective-permute-start(bf16[8,6144]{1,0:T(8,128)(2,1)S(1)} %shard_map.85), channel_id=1, source_target_pairs={{0,2},{1,3},{2,0},{3,1},{4,6},{5,7},{6,4},{7,5},{8,10},{9,11},{10,... | collective-permute-start | bytes 294920 | tf_op jit(solution)/shard_map/ppermute | solution.py:16
  65.5 5.5 %collective-permute-start.22 = (bf16[8,6144]{1,0:T(8,128)(2,1)S(1)}, bf16[8,6144]{1,0:T(8,128)(2,1)S(1)}, u32[]{:S(2)}, u32[]{:S(2)}) collective-permute-start(bf16[8,6144]{1,0:T(8,128)(2,1)S(1)} %collective-permute-done.17), channel_id=1, source_target_pairs={{0,2},{1,3},{2,0},{3,1},{4,6},{5,7},{6,4},{7,5},{8,10},{9,11},{10,... | collective-permute-start | bytes 294920 | tf_op jit(solution)/shard_map/ppermute | solution.py:16
  68.8 4.9 %collective-permute-start.21 = (bf16[8,6144]{1,0:T(8,128)(2,1)S(1)}, bf16[8,6144]{1,0:T(8,128)(2,1)S(1)}, u32[]{:S(2)}, u32[]{:S(2)}) collective-permute-start(bf16[8,6144]{1,0:T(8,128)(2,1)S(1)} %collective-permute-done.16), channel_id=1, source_target_pairs={{0,2},{1,3},{2,0},{3,1},{4,6},{5,7},{6,4},{7,5},{8,10},{9,11},{10,... | collective-permute-start | bytes 294920 | tf_op jit(solution)/shard_map/ppermute | solution.py:16
  69.5 5.3 %collective-permute-start.20 = (bf16[8,6144]{1,0:T(8,128)(2,1)S(1)}, bf16[8,6144]{1,0:T(8,128)(2,1)S(1)}, u32[]{:S(2)}, u32[]{:S(2)}) collective-permute-start(bf16[8,6144]{1,0:T(8,128)(2,1)S(1)} %collective-permute-done.15), channel_id=1, source_target_pairs={{0,2},{1,3},{2,0},{3,1},{4,6},{5,7},{6,4},{7,5},{8,10},{9,11},{10,... | collective-permute-start | bytes 294920 | tf_op jit(solution)/shard_map/ppermute | solution.py:16
  70.9 5.0 %collective-permute-start.18 = (bf16[4,8,6144]{2,1,0:T(8,128)(2,1)S(1)}, bf16[4,8,6144]{2,1,0:T(8,128)(2,1)S(1)}, u32[]{:S(2)}, u32[]{:S(2)}) collective-permute-start(bf16[4,8,6144]{2,1,0:T(8,128)(2,1)S(1)} %pad_maximum_fusion.refs_0_), channel_id=1, source_target_pairs={{0,1},{1,0},{2,3},{3,2},{4,5},{5,4},{6,7},{7,6},{8,9},{9,8},{10,11... | collective-permute-start | bytes 1179656 | tf_op jit(solution)/shard_map/ppermute | solution.py:16
  74.8 1.8 %collective-permute-start.23 = (bf16[4,8,6144]{2,1,0:T(8,128)(2,1)S(1)}, bf16[4,8,6144]{2,1,0:T(8,128)(2,1)S(1)}, u32[]{:S(2)}, u32[]{:S(2)}) collective-permute-start(bf16[4,8,6144]{2,1,0:T(8,128)(2,1)S(1)} %pad_maximum_fusion.1.refs_2_), channel_id=1, source_target_pairs={{0,1},{1,0},{2,3},{3,2},{4,5},{5,4},{6,7},{7,6},{8,9},{9,8},{10,11... | collective-permute-start | bytes 1179656 | tf_op jit(solution)/shard_map/ppermute | solution.py:16
  (3 other events, 165.7 us)

commit v2 on v1

--- a/solution.py
+++ b/solution.py
@@ -30,32 +30,53 @@
     )(*(pltpu.with_memory_space_constraint(arg, pltpu.VMEM) for arg in args))
 
 
+def _groups(size):
+    far = size // NEAR
+    return [[far - 2], list(reversed(range(1, far - 2))), [far - 1], [0]]
+
+
 def _far_order(size):
+    return [k for group in _groups(size) for k in group]
+
+
+def _outward(size):
     far = size // NEAR
-    return [far - 2, far - 1, *reversed(range(far - 2))]
+    return [far // 2, *(k for k in range(1, far) if k != far // 2)]
 
 
 def _near_sums(grads, rows, width, size):
     far = size // NEAR
     me = lax.axis_index("dp")
     far_at, near_at = me // NEAR, me % NEAR
-    blocks = grads.reshape(far, NEAR, rows, width)
+
+    def piece(grads, offsets, j):
+        blocks = grads.reshape(far, NEAR, rows, width)
+        return jnp.stack([_pick(_pick(blocks, far_at ^ k), near_at ^ j) for k in offsets])
+
+    groups = _groups(size)
     order = _far_order(size)
-    pieces = []
-    for k in order:
-        group = _pick(blocks, far_at ^ k)
-        pieces.append([_pick(group, near_at ^ j) for j in range(NEAR)])
-    pieces = lax.optimization_barrier(pieces)
+    first = lax.optimization_barrier([piece(grads, groups[0], j) for j in (2, 3)])
+    grads, _ = lax.optimization_barrier((grads, first))
+    own, pair = piece(grads, order, 0), piece(grads, order, 1)
+    rest = [[piece(grads, group, j) for j in (2, 3)] for group in groups[1:]]
+    own, pair, rest = lax.optimization_barrier((own, pair, rest))
     moved = []
-    for k, piece in zip(order, pieces):
-        moved.append([_swap(piece[j], size, j) for j in (2, 3, 1)])
+    for pieces in [first, *rest]:
+        moved.append([_swap(pieces[0], size, 2), _swap(pieces[1], size, 3)])
+    pair = _swap(pair, size, 1)
     sums = {}
-    for k, piece, others in zip(order, pieces, moved):
-        total = piece[0].astype(jnp.float32)
-        for other in others:
-            total = total + other.astype(jnp.float32)
-        sums[k] = total
+    block = pltpu.VMEM((rows, width), jnp.float32)
+    for g, group in enumerate(groups):
+        at = [order.index(k) for k in group]
+        totals = _call(functools.partial(_add_near, at), (block,) * len(at), own, pair, *moved[g])
+        sums.update(zip(group, totals))
     return sums
+
+
+def _add_near(at, own, pair, left, right, *totals):
+    for i, (k, total) in enumerate(zip(at, totals)):
+        here = own[k].astype(jnp.float32) + pair[k].astype(jnp.float32)
+        total[...] = here + left[i].astype(jnp.float32) + right[i].astype(jnp.float32)
 
 
 def _finish_sum(*refs):
@@ -90,19 +111,35 @@
         out[...] = value
 
 
-def _place(size, *refs):
-    *groups, out, done = refs
+def _place(offsets, blocks, *refs):
+    *_, out, done = refs
     me = lax.axis_index("dp")
-    far = size // NEAR
-    copies = []
-    for g, group in enumerate(groups):
-        for k in range(far):
-            offset = k * NEAR + g
-            copies.append(pltpu.make_async_copy(group.at[k], out.at[me ^ offset], done.at[offset]))
+    copies = [
+        pltpu.make_async_copy(block, out.at[me ^ offset], done.at[i])
+        for i, (offset, block) in enumerate(zip(offsets, blocks))
+    ]
     for copy in copies:
         copy.start()
     for copy in copies:
         copy.wait()
+
+
+def _placed(size, blocks, *rows):
+    offsets = list(blocks)
+    height, width = blocks[offsets[0]].shape
+
+    def body(*refs):
+        _place(offsets, refs[: len(offsets)], *refs[len(offsets) :])
+
+    return pl.pallas_call(
+        body,
+        out_shape=jax.ShapeDtypeStruct((size, height, width), jnp.bfloat16),
+        in_specs=[VMEM] * len(offsets) + [pl.BlockSpec(memory_space=pl.ANY)] * len(rows),
+        out_specs=pl.BlockSpec(memory_space=pl.ANY),
+        scratch_shapes=[pltpu.SemaphoreType.DMA((len(offsets),))],
+        input_output_aliases={len(offsets): 0} if rows else {},
+        cost_estimate=pl.CostEstimate(flops=1000000, bytes_accessed=1000000, transcendentals=0),
+    )(*(pltpu.with_memory_space_constraint(block, pltpu.VMEM) for block in blocks.values()), *rows)
 
 
 def _step(size, grads, master, first, second):
@@ -123,22 +160,19 @@
     (own,) = _call(_weights, (pltpu.VMEM((rows, width), jnp.bfloat16),), *state)
     results = _call(_states, (f32,) * 4, *state)
 
-    here, there = {0: own}, {}
-    for k in order[:-1]:
-        here[k] = _swap(own, size, k * NEAR)
-    for k in (0, *order[:-1]):
-        there[k] = _swap(here[k], size, 2)
-    here = jnp.stack([here[k] for k in range(size // NEAR)])
-    there = jnp.stack([there[k] for k in range(size // NEAR)])
-    here_pair = _swap(here, size, 1)
-    there_pair = _swap(there, size, 1)
-    new_weights = pl.pallas_call(
-        functools.partial(_place, size),
-        out_shape=jax.ShapeDtypeStruct((size, rows, width), jnp.bfloat16),
-        in_specs=[VMEM] * 4,
-        out_specs=pl.BlockSpec(memory_space=pl.ANY),
-        scratch_shapes=[pltpu.SemaphoreType.DMA((size,))],
-    )(*(pltpu.with_memory_space_constraint(x, pltpu.VMEM) for x in (here, here_pair, there, there_pair)))
+    blocks = {0: own}
+    for k in _outward(size):
+        blocks[k * NEAR] = _swap(own, size, k * NEAR)
+    for k in (0, *_outward(size)):
+        blocks[k * NEAR + 2] = _swap(blocks[k * NEAR], size, 2)
+    for offset in list(blocks):
+        blocks[offset + 1] = _swap(blocks[offset], size, 1)
+    last = size - 1
+    early = {k: block for k, block in blocks.items() if not k & 2}
+    late = {k: block for k, block in blocks.items() if k & 2 and k != last}
+    placed = _placed(size, early)
+    placed = _placed(size, late, placed)
+    new_weights = _placed(size, {last: blocks[last]}, placed)
     return results, new_weights
 
 

time: 78.1 us -> 69.4 us (0.89)
  waiting for transfers between devices: 35.3 us -> 25.1 us
  Pallas kernels: 2.84 us -> 4.27 us
  starting transfers between devices: 25.4 us -> 24.3 us
  local copies, waits for them, and re-layouts: 1.62 us -> 2.49 us
    ppermute x24 -> x27, waiting for transfers between devices: 35.3 us -> 25.1 us  [_swap(): return lax.ppermute(array, 'dp', [(i, i ^ offset) for i in range(size)])]
    dynamic_slice x0 -> x2, local copies, waits for them, and re-layouts: none -> 2.47 us  [_pick(): return lax.dynamic_index_in_dim(array, index, 0, keepdims=False)]
    squeeze x1 -> x0, local copies, waits for them, and re-layouts: 1.6 us -> none  [_pick(): return lax.dynamic_index_in_dim(array, index, 0, keepdims=False)]
    pallas_call x1 -> x3, Pallas kernels: 1.26 us -> 2.51 us  [_placed(): pl.pallas_call(body, out_shape=jax.ShapeDtypeStruct((size, height, width)...]
    ppermute x24 -> x27, starting transfers between devices: 25.4 us -> 24.3 us  [_swap(): return lax.ppermute(array, 'dp', [(i, i ^ offset) for i in range(size)])]
    pallas_call x3 -> x7, Pallas kernels: 1.58 us -> 1.77 us  [_call(): pl.pallas_call(body, out_shape=outs, in_specs=[VMEM] * len(args), out_spe...]
  transfers between devices with their start and end apart: 24 -> 27, of which waited for: 12 -> 11; matrix products, arithmetic and copies ran while one was open for 0% -> 0% of each run, Pallas kernels for 1% -> 4%
where the time goes in v2:
time: 69.4 us; the launch traced here: 69.1 us
  waiting for transfers between devices  25.1 us (36%)
  starting transfers between devices  24.3 us (35%)
  blocking collectives  12 us (17%)
  Pallas kernels  4.27 us (6%)
  local copies, waits for them, and re-layouts  2.49 us (4%)
  between operations  0.89 us (1%)
    ppermute x27, waiting for transfers between devices, _swap(): return lax.ppermute(array, 'dp', [(i, i ^ offset) for i in range(size)])  25.1 us
    ppermute x27, starting transfers between devices, _swap(): return lax.ppermute(array, 'dp', [(i, i ^ offset) for i in range(size)])  24.3 us
    all_to_all x1, blocking collectives, _step(): squares = lax.all_to_all(square, ('expert', 'dp'), 0, 0)  12 us
    pallas_call x3, Pallas kernels, _placed(): pl.pallas_call(body, out_shape=jax.ShapeDtypeStruct((size, height, width)...  2.51 us
    dynamic_slice x2, local copies, waits for them, and re-layouts, _pick(): return lax.dynamic_index_in_dim(array, index, 0, keepdims=False)  2.47 us
    pallas_call x7, Pallas kernels, _call(): pl.pallas_call(body, out_shape=outs, in_specs=[VMEM] * len(args), out_spe...  1.77 us
  transfers between devices with their start and end apart: 27, of which 11 were waited for; matrix products, arithmetic and copies ran while one was open for 0% of the time, Pallas kernels for 4%

profile of v2, /device:TPU:0, one launch (start us, length us, event | category | flops | bytes accessed | tf_op | source)
XLA Modules:
  0.0 69.1 jit_solution(2930226668773737337)
XLA Ops:
  0.7 1.0 %dynamic-slice_bitcast_fusion.14 = (bf16[1,8,6144]{2,1,0:T(8,128)(2,1)S(1)}, bf16[1,8,6144]{2,1,0:T(8,128)(2,1)S(1)}) fusion(bf16[4,4,8,6144]{3,2,1,0:T(8,128)(2,1)} %bitcast.50, s32[]{:T(128)S(6)} %select_n.79, s32[]{:T(128)S(6)} %select_n.84, s32[]{:T(128)S(6)} %select_n.82), kind=kLoop, calls=%fused_computation.16 | loop fusion | bytes 393228 | tf_op jit(solution)/shard_map/jit(dynamic_index_in_dim)/dynamic_slice | solution.py:20
  1.7 1.5 %dynamic-slice_bitcast_fusion = (bf16[1,8,6144]{2,1,0:T(8,128)(2,1)S(1)}, bf16[1,8,6144]{2,1,0:T(8,128)(2,1)S(1)}, bf16[1,8,6144]{2,1,0:T(8,128)(2,1)S(1)}, bf16...) fusion(bf16[4,4,8,6144]{3,2,1,0:T(8,128)(2,1)} %bitcast.51, ...), kind=kLoop, calls=%fused_computation.2 | loop fusion | bytes 2752544 | tf_op jit(solution)/shard_map/jit(dynamic_index_in_dim)/dynamic_slice | solution.py:20
  3.9 2.6 %collective-permute-start.10 = (bf16[1,8,6144]{2,1,0:T(8,128)(2,1)S(1)}, bf16[1,8,6144]{2,1,0:T(8,128)(2,1)S(1)}, u32[]{:S(2)}, u32[]{:S(2)}) collective-permute-start(bf16[1,8,6144]{2,1,0:T(8,128)(2,1)S(1)} %get-tuple-element.32), channel_id=1, source_target_pairs={{0,3},{1,2},{2,1},{3,0},{4,7},{5,6},{6,5},{7,4},{8,11},{9,10},{10,... | collective-permute-start | bytes 294920 | tf_op jit(solution)/shard_map/ppermute | solution.py:16
  6.5 2.0 %collective-permute-start.6 = (bf16[1,8,6144]{2,1,0:T(8,128)(2,1)S(1)}, bf16[1,8,6144]{2,1,0:T(8,128)(2,1)S(1)}, u32[]{:S(2)}, u32[]{:S(2)}) collective-permute-start(bf16[1,8,6144]{2,1,0:T(8,128)(2,1)S(1)} %get-tuple-element.29), channel_id=1, source_target_pairs={{0,2},{1,3},{2,0},{3,1},{4,6},{5,7},{6,4},{7,5},{8,10},{9,11},{10,... | collective-permute-start | bytes 294920 | tf_op jit(solution)/shard_map/ppermute | solution.py:16
  8.5 1.2 %collective-permute-done.10.right = bf16[1,8,6144]{2,1,0:T(8,128)(2,1)S(1)} collective-permute-done((bf16[1,8,6144]{2,1,0:T(8,128)(2,1)S(1)}, bf16[1,8,6144]{2,1,0:T(8,128)(2,1)S(1)}, u32[]{:S(2)}, u32[]{:S(2)}) %collective-permute-start.10) | collective-permute-done | bytes 98336 | tf_op jit(solution)/shard_map/ppermute | solution.py:16
  9.7 1.3 %collective-permute-start.3 = (bf16[1,8,6144]{2,1,0:T(8,128)(2,1)S(1)}, bf16[1,8,6144]{2,1,0:T(8,128)(2,1)S(1)}, u32[]{:S(2)}, u32[]{:S(2)}) collective-permute-start(bf16[1,8,6144]{2,1,0:T(8,128)(2,1)S(1)} %get-tuple-element.22), channel_id=1, source_target_pairs={{0,2},{1,3},{2,0},{3,1},{4,6},{5,7},{6,4},{7,5},{8,10},{9,11},{10,... | collective-permute-start | bytes 294920 | tf_op jit(solution)/shard_map/ppermute | solution.py:16
  10.9 1.3 %collective-permute-done.9.left = bf16[1,8,6144]{2,1,0:T(8,128)(2,1)S(1)} collective-permute-done((bf16[1,8,6144]{2,1,0:T(8,128)(2,1)S(1)}, bf16[1,8,6144]{2,1,0:T(8,128)(2,1)S(1)}, u32[]{:S(2)}, u32[]{:S(2)}) %collective-permute-start.9) | collective-permute-done | bytes 98336 | tf_op jit(solution)/shard_map/ppermute | solution.py:16
  12.8 3.7 %collective-permute-start.11 = (f32[8,6144]{1,0:T(8,128)S(1)}, f32[8,6144]{1,0:T(8,128)S(1)}, u32[]{:S(2)}, u32[]{:S(2)}) collective-permute-start(f32[8,6144]{1,0:T(8,128)S(1)} %shard_map.86), channel_id=1, source_target_pairs={{0,12},{1,13},{2,14},{3,15},{4,8},{5,9},{6,10},{7,11},{8,4},{9,5},... | collective-permute-start | bytes 589832 | tf_op jit(solution)/shard_map/ppermute | solution.py:16
  16.6 1.1 %collective-permute-start.8 = (f32[8,6144]{1,0:T(8,128)S(1)}, f32[8,6144]{1,0:T(8,128)S(1)}, u32[]{:S(2)}, u32[]{:S(2)}) collective-permute-start(f32[8,6144]{1,0:T(8,128)S(1)} %shard_map.85), channel_id=1, source_target_pairs={{0,4},{1,5},{2,6},{3,7},{4,0},{5,1},{6,2},{7,3},{8,12},{9,13},{10,... | collective-permute-start | bytes 589832 | tf_op jit(solution)/shard_map/ppermute | solution.py:16
  18.5 1.6 %collective-permute-done.4.right = bf16[1,8,6144]{2,1,0:T(8,128)(2,1)S(1)} collective-permute-done((bf16[1,8,6144]{2,1,0:T(8,128)(2,1)S(1)}, bf16[1,8,6144]{2,1,0:T(8,128)(2,1)S(1)}, u32[]{:S(2)}, u32[]{:S(2)}) %collective-permute-start.4) | collective-permute-done | bytes 98336 | tf_op jit(solution)/shard_map/ppermute | solution.py:16
  20.2 2.5 %collective-permute-start.5 = (f32[8,6144]{1,0:T(8,128)S(1)}, f32[8,6144]{1,0:T(8,128)S(1)}, u32[]{:S(2)}, u32[]{:S(2)}) collective-permute-start(f32[8,6144]{1,0:T(8,128)S(1)} %shard_map.84), channel_id=1, source_target_pairs={{0,8},{1,9},{2,10},{3,11},{4,12},{5,13},{6,14},{7,15},{8,0},{9,1},... | collective-permute-start | bytes 589832 | tf_op jit(solution)/shard_map/ppermute | solution.py:16
  22.7 1.5 %collective-permute-start.1 = (bf16[1,8,6144]{2,1,0:T(8,128)(2,1)S(1)}, bf16[1,8,6144]{2,1,0:T(8,128)(2,1)S(1)}, u32[]{:S(2)}, u32[]{:S(2)}) collective-permute-start(bf16[1,8,6144]{2,1,0:T(8,128)(2,1)S(1)} %get-tuple-element.27), channel_id=1, source_target_pairs={{0,2},{1,3},{2,0},{3,1},{4,6},{5,7},{6,4},{7,5},{8,10},{9,11},{10,... | collective-permute-start | bytes 294920 | tf_op jit(solution)/shard_map/ppermute | solution.py:16
  24.5 3.9 %collective-permute-done.1.left = bf16[1,8,6144]{2,1,0:T(8,128)(2,1)S(1)} collective-permute-done((bf16[1,8,6144]{2,1,0:T(8,128)(2,1)S(1)}, bf16[1,8,6144]{2,1,0:T(8,128)(2,1)S(1)}, u32[]{:S(2)}, u32[]{:S(2)}) %collective-permute-start.1) | collective-permute-done | bytes 98336 | tf_op jit(solution)/shard_map/ppermute | solution.py:16
  28.3 1.1 %collective-permute-done.2.right = bf16[1,8,6144]{2,1,0:T(8,128)(2,1)S(1)} collective-permute-done((bf16[1,8,6144]{2,1,0:T(8,128)(2,1)S(1)}, bf16[1,8,6144]{2,1,0:T(8,128)(2,1)S(1)}, u32[]{:S(2)}, u32[]{:S(2)}) %collective-permute-start.2) | collective-permute-done | bytes 98336 | tf_op jit(solution)/shard_map/ppermute | solution.py:16
  29.5 4.2 %collective-permute-done.5.refs_1_ = f32[8,6144]{1,0:T(8,128)S(1)} collective-permute-done((f32[8,6144]{1,0:T(8,128)S(1)}, f32[8,6144]{1,0:T(8,128)S(1)}, u32[]{:S(2)}, u32[]{:S(2)}) %collective-permute-start.5) | collective-permute-done | bytes 196640 | tf_op jit(solution)/shard_map/ppermute | solution.py:16
  33.8 12.0 %all_to_all.5.squares = f32[32,1,128]{2,1,0:T(1,128)S(1)} all-to-all(f32[32,1,128]{2,1,0:T(1,128)S(1)} %get-tuple-element.33), channel_id=1, replica_groups=mesh['expert'=2,'dp'=16] {'expert','dp'}, dimensions={0} | all-to-all | bytes 32768 | tf_op jit(solution)/shard_map/all_to_all | solution.py:158
  47.4 3.3 %collective-permute-start.12 = (bf16[8,6144]{1,0:T(8,128)(2,1)S(1)}, bf16[8,6144]{1,0:T(8,128)(2,1)S(1)}, u32[]{:S(2)}, u32[]{:S(2)}) collective-permute-start(bf16[8,6144]{1,0:T(8,128)(2,1)S(1)} %shard_map.89.refs_0_), channel_id=1, source_target_pairs={{0,12},{1,13},{2,14},{3,15},{4,8},{5,9},{6,10},{7,11},{8,4},{9,5},... | collective-permute-start | bytes 294920 | tf_op jit(solution)/shard_map/ppermute | solution.py:16
  51.2 4.8 %collective-permute-done.16.refs_1_ = bf16[8,6144]{1,0:T(8,128)(2,1)S(1)} collective-permute-done((bf16[8,6144]{1,0:T(8,128)(2,1)S(1)}, bf16[8,6144]{1,0:T(8,128)(2,1)S(1)}, u32[]{:S(2)}, u32[]{:S(2)}) %collective-permute-start.16) | collective-permute-done | bytes 98336 | tf_op jit(solution)/shard_map/ppermute | solution.py:16
  56.6 1.9 %collective-permute-start.19 = (bf16[8,6144]{1,0:T(8,128)(2,1)S(1)}, bf16[8,6144]{1,0:T(8,128)(2,1)S(1)}, u32[]{:S(2)}, u32[]{:S(2)}) collective-permute-start(bf16[8,6144]{1,0:T(8,128)(2,1)S(1)} %collective-permute-done.18.refs_2_), channel_id=1, source_target_pairs={{0,2},{1,3},{2,0},{3,1},{4,6},{5,7},{6,4},{7,5},{8,10},{9,11},{10,... | collective-permute-start | bytes 294920 | tf_op jit(solution)/shard_map/ppermute | solution.py:16
  59.2 3.0 %collective-permute-done.17.refs_1_ = bf16[8,6144]{1,0:T(8,128)(2,1)S(1)} collective-permute-done((bf16[8,6144]{1,0:T(8,128)(2,1)S(1)}, bf16[8,6144]{1,0:T(8,128)(2,1)S(1)}, u32[]{:S(2)}, u32[]{:S(2)}) %collective-permute-start.17) | collective-permute-done | bytes 98336 | tf_op jit(solution)/shard_map/ppermute | solution.py:16
  62.2 2.1 %collective-permute-done.19.refs_2_ = bf16[8,6144]{1,0:T(8,128)(2,1)S(1)} collective-permute-done((bf16[8,6144]{1,0:T(8,128)(2,1)S(1)}, bf16[8,6144]{1,0:T(8,128)(2,1)S(1)}, u32[]{:S(2)}, u32[]{:S(2)}) %collective-permute-start.19) | collective-permute-done | bytes 98336 | tf_op jit(solution)/shard_map/ppermute | solution.py:16
  64.3 1.2 %collective-permute-done.13.refs_3_ = bf16[8,6144]{1,0:T(8,128)(2,1)S(1)} collective-permute-done((bf16[8,6144]{1,0:T(8,128)(2,1)S(1)}, bf16[8,6144]{1,0:T(8,128)(2,1)S(1)}, u32[]{:S(2)}, u32[]{:S(2)}) %collective-permute-start.13) | collective-permute-done | bytes 98336 | tf_op jit(solution)/shard_map/ppermute | solution.py:16
  65.5 1.1 %shard_map.88 = (f32[8,6144]{1,0:T(8,128)}, f32[8,6144]{1,0:T(8,128)}, f32[8,6144]{1,0:T(8,128)}, f32[8,6144]{1,0:T(8,128)}) custom-call(f32[32,1,128]{2,1,0:T(1,128)S(1)} %all_to_all.5.squares, f32[8,6144]{1,0:T(8,128)S(1)} %get-tuple-element.34.summed, f32[8,6144]{1,0:T(8,128)S(1)} %bitcast.44, f32[8,6144]{1,0:T(8,128)S(1)} %bitcast.46, f32[8,6144]{1,0:T(8,128)S(1)} %bitcast.48), custom_call_target="tpu_custom_call" | custom-call | flops 1000000 | bytes 1000000 | tf_op jit(solution)/shard_map/pallas_call | solution.py:24
  66.6 0.9 %shard_map.90.refs_7_ = bf16[16,8,6144]{2,1,0:T(8,128)(2,1)} custom-call(bf16[8,6144]{1,0:T(8,128)(2,1)S(1)} %shard_map.89.refs_0_, bf16[8,6144]{1,0:T(8,128)(2,1)S(1)} %collective-permute-done.16.refs_1_, bf16[8,6144]{1,0:T(8,128)(2,1)S(1)} %collective-permute-done.18.refs_2_, bf16[8,6144]{1,0:T(8,128)(2,1)S(1)} %collective-permute-done.12.refs_3_, ...), custom_call_target="tpu_custom_call" | custom-call | flops 1000000 | bytes 1000000 | tf_op jit(solution)/shard_map/pallas_call | solution.py:134
  (50 shorter events, 7.6 us)
Async XLA Ops:
  3.3 9.5 %collective-permute-start = (bf16[4,8,6144]{2,1,0:T(8,128)(2,1)S(1)}, bf16[4,8,6144]{2,1,0:T(8,128)(2,1)S(1)}, u32[]{:S(2)}, u32[]{:S(2)}) collective-permute-start(bf16[4,8,6144]{2,1,0:T(8,128)(2,1)S(1)} %get-tuple-element.26), channel_id=1, source_target_pairs={{0,1},{1,0},{2,3},{3,2},{4,5},{5,4},{6,7},{7,6},{8,9},{9,8},{10,11... | collective-permute-start | bytes 1179656 | tf_op jit(solution)/shard_map/ppermute | solution.py:16
  3.9 5.8 %collective-permute-start.10 = (bf16[1,8,6144]{2,1,0:T(8,128)(2,1)S(1)}, bf16[1,8,6144]{2,1,0:T(8,128)(2,1)S(1)}, u32[]{:S(2)}, u32[]{:S(2)}) collective-permute-start(bf16[1,8,6144]{2,1,0:T(8,128)(2,1)S(1)} %get-tuple-element.32), channel_id=1, source_target_pairs={{0,3},{1,2},{2,1},{3,0},{4,7},{5,6},{6,5},{7,4},{8,11},{9,10},{10,... | collective-permute-start | bytes 294920 | tf_op jit(solution)/shard_map/ppermute | solution.py:16
  6.5 5.7 %collective-permute-start.9 = (bf16[1,8,6144]{2,1,0:T(8,128)(2,1)S(1)}, bf16[1,8,6144]{2,1,0:T(8,128)(2,1)S(1)}, u32[]{:S(2)}, u32[]{:S(2)}) collective-permute-start(bf16[1,8,6144]{2,1,0:T(8,128)(2,1)S(1)} %get-tuple-element.31), channel_id=1, source_target_pairs={{0,2},{1,3},{2,0},{3,1},{4,6},{5,7},{6,4},{7,5},{8,10},{9,11},{10,... | collective-permute-start | bytes 294920 | tf_op jit(solution)/shard_map/ppermute | solution.py:16
  6.5 10.0 %collective-permute-start.6 = (bf16[1,8,6144]{2,1,0:T(8,128)(2,1)S(1)}, bf16[1,8,6144]{2,1,0:T(8,128)(2,1)S(1)}, u32[]{:S(2)}, u32[]{:S(2)}) collective-permute-start(bf16[1,8,6144]{2,1,0:T(8,128)(2,1)S(1)} %get-tuple-element.29), channel_id=1, source_target_pairs={{0,2},{1,3},{2,0},{3,1},{4,6},{5,7},{6,4},{7,5},{8,10},{9,11},{10,... | collective-permute-start | bytes 294920 | tf_op jit(solution)/shard_map/ppermute | solution.py:16
  8.5 8.0 %collective-permute-start.7 = (bf16[1,8,6144]{2,1,0:T(8,128)(2,1)S(1)}, bf16[1,8,6144]{2,1,0:T(8,128)(2,1)S(1)}, u32[]{:S(2)}, u32[]{:S(2)}) collective-permute-start(bf16[1,8,6144]{2,1,0:T(8,128)(2,1)S(1)} %get-tuple-element.30), channel_id=1, source_target_pairs={{0,3},{1,2},{2,1},{3,0},{4,7},{5,6},{6,5},{7,4},{8,11},{9,10},{10,... | collective-permute-start | bytes 294920 | tf_op jit(solution)/shard_map/ppermute | solution.py:16
  9.7 8.8 %collective-permute-start.3 = (bf16[1,8,6144]{2,1,0:T(8,128)(2,1)S(1)}, bf16[1,8,6144]{2,1,0:T(8,128)(2,1)S(1)}, u32[]{:S(2)}, u32[]{:S(2)}) collective-permute-start(bf16[1,8,6144]{2,1,0:T(8,128)(2,1)S(1)} %get-tuple-element.22), channel_id=1, source_target_pairs={{0,2},{1,3},{2,0},{3,1},{4,6},{5,7},{6,4},{7,5},{8,10},{9,11},{10,... | collective-permute-start | bytes 294920 | tf_op jit(solution)/shard_map/ppermute | solution.py:16
  12.2 7.9 %collective-permute-start.4 = (bf16[1,8,6144]{2,1,0:T(8,128)(2,1)S(1)}, bf16[1,8,6144]{2,1,0:T(8,128)(2,1)S(1)}, u32[]{:S(2)}, u32[]{:S(2)}) collective-permute-start(bf16[1,8,6144]{2,1,0:T(8,128)(2,1)S(1)} %get-tuple-element.23), channel_id=1, source_target_pairs={{0,3},{1,2},{2,1},{3,0},{4,7},{5,6},{6,5},{7,4},{8,11},{9,10},{10,... | collective-permute-start | bytes 294920 | tf_op jit(solution)/shard_map/ppermute | solution.py:16
  12.8 16.6 %collective-permute-start.11 = (f32[8,6144]{1,0:T(8,128)S(1)}, f32[8,6144]{1,0:T(8,128)S(1)}, u32[]{:S(2)}, u32[]{:S(2)}) collective-permute-start(f32[8,6144]{1,0:T(8,128)S(1)} %shard_map.86), channel_id=1, source_target_pairs={{0,12},{1,13},{2,14},{3,15},{4,8},{5,9},{6,10},{7,11},{8,4},{9,5},... | collective-permute-start | bytes 589832 | tf_op jit(solution)/shard_map/ppermute | solution.py:16
  16.6 12.9 %collective-permute-start.8 = (f32[8,6144]{1,0:T(8,128)S(1)}, f32[8,6144]{1,0:T(8,128)S(1)}, u32[]{:S(2)}, u32[]{:S(2)}) collective-permute-start(f32[8,6144]{1,0:T(8,128)S(1)} %shard_map.85), channel_id=1, source_target_pairs={{0,4},{1,5},{2,6},{3,7},{4,0},{5,1},{6,2},{7,3},{8,12},{9,13},{10,... | collective-permute-start | bytes 589832 | tf_op jit(solution)/shard_map/ppermute | solution.py:16
  20.2 13.5 %collective-permute-start.5 = (f32[8,6144]{1,0:T(8,128)S(1)}, f32[8,6144]{1,0:T(8,128)S(1)}, u32[]{:S(2)}, u32[]{:S(2)}) collective-permute-start(f32[8,6144]{1,0:T(8,128)S(1)} %shard_map.84), channel_id=1, source_target_pairs={{0,8},{1,9},{2,10},{3,11},{4,12},{5,13},{6,14},{7,15},{8,0},{9,1},... | collective-permute-start | bytes 589832 | tf_op jit(solution)/shard_map/ppermute | solution.py:16
  22.7 5.7 %collective-permute-start.1 = (bf16[1,8,6144]{2,1,0:T(8,128)(2,1)S(1)}, bf16[1,8,6144]{2,1,0:T(8,128)(2,1)S(1)}, u32[]{:S(2)}, u32[]{:S(2)}) collective-permute-start(bf16[1,8,6144]{2,1,0:T(8,128)(2,1)S(1)} %get-tuple-element.27), channel_id=1, source_target_pairs={{0,2},{1,3},{2,0},{3,1},{4,6},{5,7},{6,4},{7,5},{8,10},{9,11},{10,... | collective-permute-start | bytes 294920 | tf_op jit(solution)/shard_map/ppermute | solution.py:16
  24.2 5.2 %collective-permute-start.2 = (bf16[1,8,6144]{2,1,0:T(8,128)(2,1)S(1)}, bf16[1,8,6144]{2,1,0:T(8,128)(2,1)S(1)}, u32[]{:S(2)}, u32[]{:S(2)}) collective-permute-start(bf16[1,8,6144]{2,1,0:T(8,128)(2,1)S(1)} %get-tuple-element.28), channel_id=1, source_target_pairs={{0,3},{1,2},{2,1},{3,0},{4,7},{5,6},{6,5},{7,4},{8,11},{9,10},{10,... | collective-permute-start | bytes 294920 | tf_op jit(solution)/shard_map/ppermute | solution.py:16
  46.2 9.8 %collective-permute-start.16 = (bf16[8,6144]{1,0:T(8,128)(2,1)S(1)}, bf16[8,6144]{1,0:T(8,128)(2,1)S(1)}, u32[]{:S(2)}, u32[]{:S(2)}) collective-permute-start(bf16[8,6144]{1,0:T(8,128)(2,1)S(1)} %shard_map.89.refs_0_), channel_id=1, source_target_pairs={{0,8},{1,9},{2,10},{3,11},{4,12},{5,13},{6,14},{7,15},{8,0},{9,1},... | collective-permute-start | bytes 294920 | tf_op jit(solution)/shard_map/ppermute | solution.py:16
  46.9 9.1 %collective-permute-start.18 = (bf16[8,6144]{1,0:T(8,128)(2,1)S(1)}, bf16[8,6144]{1,0:T(8,128)(2,1)S(1)}, u32[]{:S(2)}, u32[]{:S(2)}) collective-permute-start(bf16[8,6144]{1,0:T(8,128)(2,1)S(1)} %shard_map.89.refs_0_), channel_id=1, source_target_pairs={{0,4},{1,5},{2,6},{3,7},{4,0},{5,1},{6,2},{7,3},{8,12},{9,13},{10,... | collective-permute-start | bytes 294920 | tf_op jit(solution)/shard_map/ppermute | solution.py:16
  47.4 9.2 %collective-permute-start.12 = (bf16[8,6144]{1,0:T(8,128)(2,1)S(1)}, bf16[8,6144]{1,0:T(8,128)(2,1)S(1)}, u32[]{:S(2)}, u32[]{:S(2)}) collective-permute-start(bf16[8,6144]{1,0:T(8,128)(2,1)S(1)} %shard_map.89.refs_0_), channel_id=1, source_target_pairs={{0,12},{1,13},{2,14},{3,15},{4,8},{5,9},{6,10},{7,11},{8,4},{9,5},... | collective-permute-start | bytes 294920 | tf_op jit(solution)/shard_map/ppermute | solution.py:16
  50.7 6.0 %collective-permute-start.23 = (bf16[8,6144]{1,0:T(8,128)(2,1)S(1)}, bf16[8,6144]{1,0:T(8,128)(2,1)S(1)}, u32[]{:S(2)}, u32[]{:S(2)}) collective-permute-start(bf16[8,6144]{1,0:T(8,128)(2,1)S(1)} %shard_map.89.refs_0_), channel_id=1, source_target_pairs={{0,1},{1,0},{2,3},{3,2},{4,5},{5,4},{6,7},{7,6},{8,9},{9,8},{10,11... | collective-permute-start | bytes 294920 | tf_op jit(solution)/shard_map/ppermute | solution.py:16
  50.7 7.9 %collective-permute-start.15 = (bf16[8,6144]{1,0:T(8,128)(2,1)S(1)}, bf16[8,6144]{1,0:T(8,128)(2,1)S(1)}, u32[]{:S(2)}, u32[]{:S(2)}) collective-permute-start(bf16[8,6144]{1,0:T(8,128)(2,1)S(1)} %shard_map.89.refs_0_), channel_id=1, source_target_pairs={{0,2},{1,3},{2,0},{3,1},{4,6},{5,7},{6,4},{7,5},{8,10},{9,11},{10,... | collective-permute-start | bytes 294920 | tf_op jit(solution)/shard_map/ppermute | solution.py:16
  56.5 5.7 %collective-permute-start.17 = (bf16[8,6144]{1,0:T(8,128)(2,1)S(1)}, bf16[8,6144]{1,0:T(8,128)(2,1)S(1)}, u32[]{:S(2)}, u32[]{:S(2)}) collective-permute-start(bf16[8,6144]{1,0:T(8,128)(2,1)S(1)} %collective-permute-done.16.refs_1_), channel_id=1, source_target_pairs={{0,2},{1,3},{2,0},{3,1},{4,6},{5,7},{6,4},{7,5},{8,10},{9,11},{10,... | collective-permute-start | bytes 294920 | tf_op jit(solution)/shard_map/ppermute | solution.py:16
  56.6 7.7 %collective-permute-start.19 = (bf16[8,6144]{1,0:T(8,128)(2,1)S(1)}, bf16[8,6144]{1,0:T(8,128)(2,1)S(1)}, u32[]{:S(2)}, u32[]{:S(2)}) collective-permute-start(bf16[8,6144]{1,0:T(8,128)(2,1)S(1)} %collective-permute-done.18.refs_2_), channel_id=1, source_target_pairs={{0,2},{1,3},{2,0},{3,1},{4,6},{5,7},{6,4},{7,5},{8,10},{9,11},{10,... | collective-permute-start | bytes 294920 | tf_op jit(solution)/shard_map/ppermute | solution.py:16
  58.6 6.9 %collective-permute-start.13 = (bf16[8,6144]{1,0:T(8,128)(2,1)S(1)}, bf16[8,6144]{1,0:T(8,128)(2,1)S(1)}, u32[]{:S(2)}, u32[]{:S(2)}) collective-permute-start(bf16[8,6144]{1,0:T(8,128)(2,1)S(1)} %collective-permute-done.12.refs_3_), channel_id=1, source_target_pairs={{0,2},{1,3},{2,0},{3,1},{4,6},{5,7},{6,4},{7,5},{8,10},{9,11},{10,... | collective-permute-start | bytes 294920 | tf_op jit(solution)/shard_map/ppermute | solution.py:16
  58.7 7.9 %collective-permute-start.26 = (bf16[8,6144]{1,0:T(8,128)(2,1)S(1)}, bf16[8,6144]{1,0:T(8,128)(2,1)S(1)}, u32[]{:S(2)}, u32[]{:S(2)}) collective-permute-start(bf16[8,6144]{1,0:T(8,128)(2,1)S(1)} %collective-permute-done.12.refs_3_), channel_id=1, source_target_pairs={{0,1},{1,0},{2,3},{3,2},{4,5},{5,4},{6,7},{7,6},{8,9},{9,8},{10,11... | collective-permute-start | bytes 294920 | tf_op jit(solution)/shard_map/ppermute | solution.py:16
  58.7 8.9 %collective-permute-start.20 = (bf16[8,6144]{1,0:T(8,128)(2,1)S(1)}, bf16[8,6144]{1,0:T(8,128)(2,1)S(1)}, u32[]{:S(2)}, u32[]{:S(2)}) collective-permute-start(bf16[8,6144]{1,0:T(8,128)(2,1)S(1)} %collective-permute-done.15.refs_0_), channel_id=1, source_target_pairs={{0,1},{1,0},{2,3},{3,2},{4,5},{5,4},{6,7},{7,6},{8,9},{9,8},{10,11... | collective-permute-start | bytes 294920 | tf_op jit(solution)/shard_map/ppermute | solution.py:16
  62.2 5.3 %collective-permute-start.21 = (bf16[8,6144]{1,0:T(8,128)(2,1)S(1)}, bf16[8,6144]{1,0:T(8,128)(2,1)S(1)}, u32[]{:S(2)}, u32[]{:S(2)}) collective-permute-start(bf16[8,6144]{1,0:T(8,128)(2,1)S(1)} %collective-permute-done.17.refs_1_), channel_id=1, source_target_pairs={{0,1},{1,0},{2,3},{3,2},{4,5},{5,4},{6,7},{7,6},{8,9},{9,8},{10,11... | collective-permute-start | bytes 294920 | tf_op jit(solution)/shard_map/ppermute | solution.py:16
  64.3 3.2 %collective-permute-start.22 = (bf16[8,6144]{1,0:T(8,128)(2,1)S(1)}, bf16[8,6144]{1,0:T(8,128)(2,1)S(1)}, u32[]{:S(2)}, u32[]{:S(2)}) collective-permute-start(bf16[8,6144]{1,0:T(8,128)(2,1)S(1)} %collective-permute-done.19.refs_2_), channel_id=1, source_target_pairs={{0,1},{1,0},{2,3},{3,2},{4,5},{5,4},{6,7},{7,6},{8,9},{9,8},{10,11... | collective-permute-start | bytes 294920 | tf_op jit(solution)/shard_map/ppermute | solution.py:16
  (6 other events, 96.3 us)

commit v3 on v2

--- a/solution.py
+++ b/solution.py
@@ -14,6 +14,11 @@
 
 def _swap(array, size, offset):
     return lax.ppermute(array, "dp", [(i, i ^ offset) for i in range(size)])
+
+
+def _hop(array, moves):
+    near = range(NEAR)
+    return lax.ppermute(array, "dp", [(a * NEAR + j, b * NEAR + j) for a, b in moves.items() for j in near])
 
 
 def _pick(array, index):
@@ -32,7 +37,7 @@
 
 def _groups(size):
     far = size // NEAR
-    return [[far - 2], list(reversed(range(1, far - 2))), [far - 1], [0]]
+    return [[far - 1], [far - 2], list(reversed(range(1, far - 2))), [0]]
 
 
 def _far_order(size):
@@ -41,7 +46,7 @@
 
 def _outward(size):
     far = size // NEAR
-    return [far // 2, *(k for k in range(1, far) if k != far // 2)]
+    return [3, 1, 2] if far == 4 else list(range(1, far))
 
 
 def _near_sums(grads, rows, width, size):
@@ -79,6 +84,25 @@
         total[...] = here + left[i].astype(jnp.float32) + right[i].astype(jnp.float32)
 
 
+def _far_sums(sums, size):
+    far = size // NEAR
+    parts = []
+    order = _far_order(size)[:-1]
+    if far == 4:
+        relayed = _hop(sums[3], {3: 2, 0: 1})
+        parts.append(_hop(sums[3], {2: 1, 1: 2}))
+        (joined,) = _call(_add, (pltpu.VMEM(sums[2].shape, jnp.float32),), sums[2], relayed)
+        sums = {**sums, 2: joined}
+        order = order[1:]
+    for k in order:
+        parts.append(_swap(sums[k], size, k * NEAR))
+    return parts
+
+
+def _add(left, right, total):
+    total[...] = left[...] + right[...]
+
+
 def _finish_sum(*refs):
     *parts, summed, square = refs
     total = parts[0][...]
@@ -145,11 +169,8 @@
 def _step(size, grads, master, first, second):
     rows, width = master.shape
     f32 = jax.ShapeDtypeStruct((rows, width), jnp.float32)
-    order = _far_order(size)
     sums = _near_sums(grads, rows, width, size)
-    parts = [sums[0]]
-    for k in order[:-1]:
-        parts.append(_swap(sums[k], size, k * NEAR))
+    parts = [sums[0], *_far_sums(sums, size)]
 
     devices = size * lax.axis_size("expert")
     kept = pltpu.VMEM((rows, width), jnp.float32)
@@ -167,12 +188,9 @@
         blocks[k * NEAR + 2] = _swap(blocks[k * NEAR], size, 2)
     for offset in list(blocks):
         blocks[offset + 1] = _swap(blocks[offset], size, 1)
-    last = size - 1
-    early = {k: block for k, block in blocks.items() if not k & 2}
-    late = {k: block for k, block in blocks.items() if k & 2 and k != last}
-    placed = _placed(size, early)
-    placed = _placed(size, late, placed)
-    new_weights = _placed(size, {last: blocks[last]}, placed)
+    placed = _placed(size, {k: block for k, block in blocks.items() if not k & 2})
+    placed = _placed(size, {k: block for k, block in blocks.items() if k & 3 == 2}, placed)
+    new_weights = _placed(size, {k: block for k, block in blocks.items() if k & 3 == 3}, placed)
     return results, new_weights
 
 

time: 69.4 us -> 73.7 us (1.062)
  waiting for transfers between devices: 25.1 us -> 31.6 us
  starting transfers between devices: 24.3 us -> 23 us
  blocking collectives: 12 us -> 11.1 us
    ppermute x27 -> x26, waiting for transfers between devices: 25.1 us -> 31.6 us  [_swap(): return lax.ppermute(array, 'dp', [(i, i ^ offset) for i in range(size)])]
    ppermute x27 -> x26, starting transfers between devices: 24.3 us -> 18.9 us  [_swap(): return lax.ppermute(array, 'dp', [(i, i ^ offset) for i in range(size)])]
    ppermute x0 -> x2, starting transfers between devices: none -> 4.1 us  [_hop(): lax.ppermute(array, 'dp', [(a * NEAR + j, b * NEAR + j) for a, b in moves...]
    all_to_all x1, blocking collectives: 12 us -> 11.1 us  [_step(): squares = lax.all_to_all(square, ('expert', 'dp'), 0, 0)]
    pallas_call x7 -> x8, Pallas kernels: 1.77 us -> 1.79 us  [_call(): pl.pallas_call(body, out_shape=outs, in_specs=[VMEM] * len(args), out_spe...]
  transfers between devices with their start and end apart: 27 -> 28, of which waited for: 11 -> 15; matrix products, arithmetic and copies ran while one was open for 0% -> 0% of each run, Pallas kernels for 4% -> 4%
where the time goes in v3:
time: 73.7 us; the launch traced here: 73.5 us
  waiting for transfers between devices  31.6 us (43%)
  starting transfers between devices  23 us (31%)
  blocking collectives  11.1 us (15%)
  Pallas kernels  4.3 us (6%)
  local copies, waits for them, and re-layouts  2.49 us (3%)
  between operations  0.91 us (1%)
    ppermute x26, waiting for transfers between devices, _swap(): return lax.ppermute(array, 'dp', [(i, i ^ offset) for i in range(size)])  31.6 us
    ppermute x26, starting transfers between devices, _swap(): return lax.ppermute(array, 'dp', [(i, i ^ offset) for i in range(size)])  18.9 us
    all_to_all x1, blocking collectives, _step(): squares = lax.all_to_all(square, ('expert', 'dp'), 0, 0)  11.1 us
    ppermute x2, starting transfers between devices, _hop(): lax.ppermute(array, 'dp', [(a * NEAR + j, b * NEAR + j) for a, b in moves...  4.1 us
    pallas_call x3, Pallas kernels, _placed(): pl.pallas_call(body, out_shape=jax.ShapeDtypeStruct((size, height, width)...  2.51 us
    dynamic_slice x2, local copies, waits for them, and re-layouts, _pick(): return lax.dynamic_index_in_dim(array, index, 0, keepdims=False)  2.47 us
    pallas_call x8, Pallas kernels, _call(): pl.pallas_call(body, out_shape=outs, in_specs=[VMEM] * len(args), out_spe...  1.79 us
  transfers between devices with their start and end apart: 28, of which 15 were waited for; matrix products, arithmetic and copies ran while one was open for 0% of the time, Pallas kernels for 4%

profile of v3, /device:TPU:0, one launch (start us, length us, event | category | flops | bytes accessed | tf_op | source)
XLA Modules:
  0.0 73.5 jit_solution(7315446851555638712)
XLA Ops:
  1.7 1.5 %dynamic-slice_bitcast_fusion = (bf16[1,8,6144]{2,1,0:T(8,128)(2,1)S(1)}, bf16[1,8,6144]{2,1,0:T(8,128)(2,1)S(1)}, bf16[1,8,6144]{2,1,0:T(8,128)(2,1)S(1)}, bf16...) fusion(bf16[4,4,8,6144]{3,2,1,0:T(8,128)(2,1)} %bitcast.51, ...), kind=kLoop, calls=%fused_computation.2 | loop fusion | bytes 2752544 | tf_op jit(solution)/shard_map/jit(dynamic_index_in_dim)/dynamic_slice | solution.py:25
  3.9 2.6 %collective-permute-start.3 = (bf16[1,8,6144]{2,1,0:T(8,128)(2,1)S(1)}, bf16[1,8,6144]{2,1,0:T(8,128)(2,1)S(1)}, u32[]{:S(2)}, u32[]{:S(2)}) collective-permute-start(bf16[1,8,6144]{2,1,0:T(8,128)(2,1)S(1)} %get-tuple-element.22), channel_id=1, source_target_pairs={{0,2},{1,3},{2,0},{3,1},{4,6},{5,7},{6,4},{7,5},{8,10},{9,11},{10,... | collective-permute-start | bytes 294920 | tf_op jit(solution)/shard_map/ppermute | solution.py:16
  6.5 3.6 %collective-permute-done.3.left = bf16[1,8,6144]{2,1,0:T(8,128)(2,1)S(1)} collective-permute-done((bf16[1,8,6144]{2,1,0:T(8,128)(2,1)S(1)}, bf16[1,8,6144]{2,1,0:T(8,128)(2,1)S(1)}, u32[]{:S(2)}, u32[]{:S(2)}) %collective-permute-start.3) | collective-permute-done | bytes 98336 | tf_op jit(solution)/shard_map/ppermute | solution.py:16
  10.1 1.6 %collective-permute-done.4.right = bf16[1,8,6144]{2,1,0:T(8,128)(2,1)S(1)} collective-permute-done((bf16[1,8,6144]{2,1,0:T(8,128)(2,1)S(1)}, bf16[1,8,6144]{2,1,0:T(8,128)(2,1)S(1)}, u32[]{:S(2)}, u32[]{:S(2)}) %collective-permute-start.4) | collective-permute-done | bytes 98336 | tf_op jit(solution)/shard_map/ppermute | solution.py:16
  11.7 3.4 %collective-permute-start.8 = (f32[8,6144]{1,0:T(8,128)S(1)}, f32[8,6144]{1,0:T(8,128)S(1)}, u32[]{:S(2)}, u32[]{:S(2)}) collective-permute-start(f32[8,6144]{1,0:T(8,128)S(1)} %shard_map.84), channel_id=1, source_target_pairs={{12,8},{13,9},{14,10},{15,11},{0,4},{1,5},{2,6},{3,7},{28,24},{29,... | collective-permute-start | bytes 589832 | tf_op jit(solution)/shard_map/ppermute | solution.py:21
  15.2 1.6 %collective-permute-start.10 = (bf16[1,8,6144]{2,1,0:T(8,128)(2,1)S(1)}, bf16[1,8,6144]{2,1,0:T(8,128)(2,1)S(1)}, u32[]{:S(2)}, u32[]{:S(2)}) collective-permute-start(bf16[1,8,6144]{2,1,0:T(8,128)(2,1)S(1)} %get-tuple-element.31), channel_id=1, source_target_pairs={{0,2},{1,3},{2,0},{3,1},{4,6},{5,7},{6,4},{7,5},{8,10},{9,11},{10,... | collective-permute-start | bytes 294920 | tf_op jit(solution)/shard_map/ppermute | solution.py:16
  16.8 1.4 %collective-permute-start.6 = (bf16[1,8,6144]{2,1,0:T(8,128)(2,1)S(1)}, bf16[1,8,6144]{2,1,0:T(8,128)(2,1)S(1)}, u32[]{:S(2)}, u32[]{:S(2)}) collective-permute-start(bf16[1,8,6144]{2,1,0:T(8,128)(2,1)S(1)} %get-tuple-element.29), channel_id=1, source_target_pairs={{0,2},{1,3},{2,0},{3,1},{4,6},{5,7},{6,4},{7,5},{8,10},{9,11},{10,... | collective-permute-start | bytes 294920 | tf_op jit(solution)/shard_map/ppermute | solution.py:16
  18.7 1.6 %collective-permute-done.10.left = bf16[1,8,6144]{2,1,0:T(8,128)(2,1)S(1)} collective-permute-done((bf16[1,8,6144]{2,1,0:T(8,128)(2,1)S(1)}, bf16[1,8,6144]{2,1,0:T(8,128)(2,1)S(1)}, u32[]{:S(2)}, u32[]{:S(2)}) %collective-permute-start.10) | collective-permute-done | bytes 98336 | tf_op jit(solution)/shard_map/ppermute | solution.py:16
  21.0 1.1 %collective-permute-done.11.right = bf16[1,8,6144]{2,1,0:T(8,128)(2,1)S(1)} collective-permute-done((bf16[1,8,6144]{2,1,0:T(8,128)(2,1)S(1)}, bf16[1,8,6144]{2,1,0:T(8,128)(2,1)S(1)}, u32[]{:S(2)}, u32[]{:S(2)}) %collective-permute-start.11) | collective-permute-done | bytes 98336 | tf_op jit(solution)/shard_map/ppermute | solution.py:16
  22.1 1.7 %collective-permute-start.12 = (f32[8,6144]{1,0:T(8,128)S(1)}, f32[8,6144]{1,0:T(8,128)S(1)}, u32[]{:S(2)}, u32[]{:S(2)}) collective-permute-start(f32[8,6144]{1,0:T(8,128)S(1)} %shard_map.87), channel_id=1, source_target_pairs={{0,4},{1,5},{2,6},{3,7},{4,0},{5,1},{6,2},{7,3},{8,12},{9,13},{10,... | collective-permute-start | bytes 589832 | tf_op jit(solution)/shard_map/ppermute | solution.py:16
  24.5 1.6 %collective-permute-done.7.right = bf16[1,8,6144]{2,1,0:T(8,128)(2,1)S(1)} collective-permute-done((bf16[1,8,6144]{2,1,0:T(8,128)(2,1)S(1)}, bf16[1,8,6144]{2,1,0:T(8,128)(2,1)S(1)}, u32[]{:S(2)}, u32[]{:S(2)}) %collective-permute-start.7) | collective-permute-done | bytes 98336 | tf_op jit(solution)/shard_map/ppermute | solution.py:16
  26.7 1.5 %collective-permute-start.1 = (bf16[1,8,6144]{2,1,0:T(8,128)(2,1)S(1)}, bf16[1,8,6144]{2,1,0:T(8,128)(2,1)S(1)}, u32[]{:S(2)}, u32[]{:S(2)}) collective-permute-start(bf16[1,8,6144]{2,1,0:T(8,128)(2,1)S(1)} %get-tuple-element.27), channel_id=1, source_target_pairs={{0,2},{1,3},{2,0},{3,1},{4,6},{5,7},{6,4},{7,5},{8,10},{9,11},{10,... | collective-permute-start | bytes 294920 | tf_op jit(solution)/shard_map/ppermute | solution.py:16
  28.4 3.9 %collective-permute-done.1.left = bf16[1,8,6144]{2,1,0:T(8,128)(2,1)S(1)} collective-permute-done((bf16[1,8,6144]{2,1,0:T(8,128)(2,1)S(1)}, bf16[1,8,6144]{2,1,0:T(8,128)(2,1)S(1)}, u32[]{:S(2)}, u32[]{:S(2)}) %collective-permute-start.1) | collective-permute-done | bytes 98336 | tf_op jit(solution)/shard_map/ppermute | solution.py:16
  33.4 5.1 %collective-permute-done.9.refs_2_ = f32[8,6144]{1,0:T(8,128)S(1)} collective-permute-done((f32[8,6144]{1,0:T(8,128)S(1)}, f32[8,6144]{1,0:T(8,128)S(1)}, u32[]{:S(2)}, u32[]{:S(2)}) %collective-permute-start.9) | collective-permute-done | bytes 196640 | tf_op jit(solution)/shard_map/ppermute | solution.py:16
  38.6 11.1 %all_to_all.5.squares = f32[32,1,128]{2,1,0:T(1,128)S(1)} all-to-all(f32[32,1,128]{2,1,0:T(1,128)S(1)} %get-tuple-element.33), channel_id=1, replica_groups=mesh['expert'=2,'dp'=16] {'expert','dp'}, dimensions={0} | all-to-all | bytes 32768 | tf_op jit(solution)/shard_map/all_to_all | solution.py:179
  51.2 3.2 %collective-permute-start.21 = (bf16[8,6144]{1,0:T(8,128)(2,1)S(1)}, bf16[8,6144]{1,0:T(8,128)(2,1)S(1)}, u32[]{:S(2)}, u32[]{:S(2)}) collective-permute-start(bf16[8,6144]{1,0:T(8,128)(2,1)S(1)} %shard_map.90.refs_0_), channel_id=1, source_target_pairs={{0,8},{1,9},{2,10},{3,11},{4,12},{5,13},{6,14},{7,15},{8,0},{9,1},... | collective-permute-start | bytes 294920 | tf_op jit(solution)/shard_map/ppermute | solution.py:16
  55.0 2.5 %collective-permute-done.15.refs_1_ = bf16[8,6144]{1,0:T(8,128)(2,1)S(1)} collective-permute-done((bf16[8,6144]{1,0:T(8,128)(2,1)S(1)}, bf16[8,6144]{1,0:T(8,128)(2,1)S(1)}, u32[]{:S(2)}, u32[]{:S(2)}) %collective-permute-start.15) | collective-permute-done | bytes 98336 | tf_op jit(solution)/shard_map/ppermute | solution.py:16
  57.6 1.1 %collective-permute-done.18.refs_2_ = bf16[8,6144]{1,0:T(8,128)(2,1)S(1)} collective-permute-done((bf16[8,6144]{1,0:T(8,128)(2,1)S(1)}, bf16[8,6144]{1,0:T(8,128)(2,1)S(1)}, u32[]{:S(2)}, u32[]{:S(2)}) %collective-permute-start.18) | collective-permute-done | bytes 98336 | tf_op jit(solution)/shard_map/ppermute | solution.py:16
  58.7 2.3 %collective-permute-done.21.refs_3_ = bf16[8,6144]{1,0:T(8,128)(2,1)S(1)} collective-permute-done((bf16[8,6144]{1,0:T(8,128)(2,1)S(1)}, bf16[8,6144]{1,0:T(8,128)(2,1)S(1)}, u32[]{:S(2)}, u32[]{:S(2)}) %collective-permute-start.21) | collective-permute-done | bytes 98336 | tf_op jit(solution)/shard_map/ppermute | solution.py:16
  61.7 1.4 %collective-permute-start.19 = (bf16[8,6144]{1,0:T(8,128)(2,1)S(1)}, bf16[8,6144]{1,0:T(8,128)(2,1)S(1)}, u32[]{:S(2)}, u32[]{:S(2)}) collective-permute-start(bf16[8,6144]{1,0:T(8,128)(2,1)S(1)} %collective-permute-done.18.refs_2_), channel_id=1, source_target_pairs={{0,2},{1,3},{2,0},{3,1},{4,6},{5,7},{6,4},{7,5},{8,10},{9,11},{10,... | collective-permute-start | bytes 294920 | tf_op jit(solution)/shard_map/ppermute | solution.py:16
  64.2 2.4 %collective-permute-done.16.refs_1_ = bf16[8,6144]{1,0:T(8,128)(2,1)S(1)} collective-permute-done((bf16[8,6144]{1,0:T(8,128)(2,1)S(1)}, bf16[8,6144]{1,0:T(8,128)(2,1)S(1)}, u32[]{:S(2)}, u32[]{:S(2)}) %collective-permute-start.16) | collective-permute-done | bytes 98336 | tf_op jit(solution)/shard_map/ppermute | solution.py:16
  66.7 2.1 %collective-permute-done.19.refs_2_ = bf16[8,6144]{1,0:T(8,128)(2,1)S(1)} collective-permute-done((bf16[8,6144]{1,0:T(8,128)(2,1)S(1)}, bf16[8,6144]{1,0:T(8,128)(2,1)S(1)}, u32[]{:S(2)}, u32[]{:S(2)}) %collective-permute-start.19) | collective-permute-done | bytes 98336 | tf_op jit(solution)/shard_map/ppermute | solution.py:16
  68.8 1.1 %collective-permute-done.22.refs_3_ = bf16[8,6144]{1,0:T(8,128)(2,1)S(1)} collective-permute-done((bf16[8,6144]{1,0:T(8,128)(2,1)S(1)}, bf16[8,6144]{1,0:T(8,128)(2,1)S(1)}, u32[]{:S(2)}, u32[]{:S(2)}) %collective-permute-start.22) | collective-permute-done | bytes 98336 | tf_op jit(solution)/shard_map/ppermute | solution.py:16
  69.8 1.1 %shard_map.89 = (f32[8,6144]{1,0:T(8,128)}, f32[8,6144]{1,0:T(8,128)}, f32[8,6144]{1,0:T(8,128)}, f32[8,6144]{1,0:T(8,128)}) custom-call(f32[32,1,128]{2,1,0:T(1,128)S(1)} %all_to_all.5.squares, f32[8,6144]{1,0:T(8,128)S(1)} %get-tuple-element.34.summed, f32[8,6144]{1,0:T(8,128)S(1)} %bitcast.44, f32[8,6144]{1,0:T(8,128)S(1)} %bitcast.46, f32[8,6144]{1,0:T(8,128)S(1)} %bitcast.48), custom_call_target="tpu_custom_call" | custom-call | flops 1000000 | bytes 1000000 | tf_op jit(solution)/shard_map/pallas_call | solution.py:29
  (53 shorter events, 12.1 us)
Async XLA Ops:
  3.3 8.4 %collective-permute-start = (bf16[4,8,6144]{2,1,0:T(8,128)(2,1)S(1)}, bf16[4,8,6144]{2,1,0:T(8,128)(2,1)S(1)}, u32[]{:S(2)}, u32[]{:S(2)}) collective-permute-start(bf16[4,8,6144]{2,1,0:T(8,128)(2,1)S(1)} %get-tuple-element.26), channel_id=1, source_target_pairs={{0,1},{1,0},{2,3},{3,2},{4,5},{5,4},{6,7},{7,6},{8,9},{9,8},{10,11... | collective-permute-start | bytes 1179656 | tf_op jit(solution)/shard_map/ppermute | solution.py:16
  3.9 6.2 %collective-permute-start.3 = (bf16[1,8,6144]{2,1,0:T(8,128)(2,1)S(1)}, bf16[1,8,6144]{2,1,0:T(8,128)(2,1)S(1)}, u32[]{:S(2)}, u32[]{:S(2)}) collective-permute-start(bf16[1,8,6144]{2,1,0:T(8,128)(2,1)S(1)} %get-tuple-element.22), channel_id=1, source_target_pairs={{0,2},{1,3},{2,0},{3,1},{4,6},{5,7},{6,4},{7,5},{8,10},{9,11},{10,... | collective-permute-start | bytes 294920 | tf_op jit(solution)/shard_map/ppermute | solution.py:16
  6.5 5.2 %collective-permute-start.4 = (bf16[1,8,6144]{2,1,0:T(8,128)(2,1)S(1)}, bf16[1,8,6144]{2,1,0:T(8,128)(2,1)S(1)}, u32[]{:S(2)}, u32[]{:S(2)}) collective-permute-start(bf16[1,8,6144]{2,1,0:T(8,128)(2,1)S(1)} %get-tuple-element.23), channel_id=1, source_target_pairs={{0,3},{1,2},{2,1},{3,0},{4,7},{5,6},{6,5},{7,4},{8,11},{9,10},{10,... | collective-permute-start | bytes 294920 | tf_op jit(solution)/shard_map/ppermute | solution.py:16
  11.7 14.4 %collective-permute-start.8 = (f32[8,6144]{1,0:T(8,128)S(1)}, f32[8,6144]{1,0:T(8,128)S(1)}, u32[]{:S(2)}, u32[]{:S(2)}) collective-permute-start(f32[8,6144]{1,0:T(8,128)S(1)} %shard_map.84), channel_id=1, source_target_pairs={{12,8},{13,9},{14,10},{15,11},{0,4},{1,5},{2,6},{3,7},{28,24},{29,... | collective-permute-start | bytes 589832 | tf_op jit(solution)/shard_map/ppermute | solution.py:21
  16.8 5.3 %collective-permute-start.11 = (bf16[1,8,6144]{2,1,0:T(8,128)(2,1)S(1)}, bf16[1,8,6144]{2,1,0:T(8,128)(2,1)S(1)}, u32[]{:S(2)}, u32[]{:S(2)}) collective-permute-start(bf16[1,8,6144]{2,1,0:T(8,128)(2,1)S(1)} %get-tuple-element.32), channel_id=1, source_target_pairs={{0,3},{1,2},{2,1},{3,0},{4,7},{5,6},{6,5},{7,4},{8,11},{9,10},{10,... | collective-permute-start | bytes 294920 | tf_op jit(solution)/shard_map/ppermute | solution.py:16
  16.8 7.7 %collective-permute-start.6 = (bf16[1,8,6144]{2,1,0:T(8,128)(2,1)S(1)}, bf16[1,8,6144]{2,1,0:T(8,128)(2,1)S(1)}, u32[]{:S(2)}, u32[]{:S(2)}) collective-permute-start(bf16[1,8,6144]{2,1,0:T(8,128)(2,1)S(1)} %get-tuple-element.29), channel_id=1, source_target_pairs={{0,2},{1,3},{2,0},{3,1},{4,6},{5,7},{6,4},{7,5},{8,10},{9,11},{10,... | collective-permute-start | bytes 294920 | tf_op jit(solution)/shard_map/ppermute | solution.py:16
  18.2 7.9 %collective-permute-start.7 = (bf16[1,8,6144]{2,1,0:T(8,128)(2,1)S(1)}, bf16[1,8,6144]{2,1,0:T(8,128)(2,1)S(1)}, u32[]{:S(2)}, u32[]{:S(2)}) collective-permute-start(bf16[1,8,6144]{2,1,0:T(8,128)(2,1)S(1)} %get-tuple-element.30), channel_id=1, source_target_pairs={{0,3},{1,2},{2,1},{3,0},{4,7},{5,6},{6,5},{7,4},{8,11},{9,10},{10,... | collective-permute-start | bytes 294920 | tf_op jit(solution)/shard_map/ppermute | solution.py:16
  20.3 13.0 %collective-permute-start.5 = (f32[8,6144]{1,0:T(8,128)S(1)}, f32[8,6144]{1,0:T(8,128)S(1)}, u32[]{:S(2)}, u32[]{:S(2)}) collective-permute-start(f32[8,6144]{1,0:T(8,128)S(1)} %shard_map.84), channel_id=1, source_target_pairs={{8,4},{9,5},{10,6},{11,7},{4,8},{5,9},{6,10},{7,11},{24,20},{25,21... | collective-permute-start | bytes 589832 | tf_op jit(solution)/shard_map/ppermute | solution.py:21
  22.1 11.2 %collective-permute-start.12 = (f32[8,6144]{1,0:T(8,128)S(1)}, f32[8,6144]{1,0:T(8,128)S(1)}, u32[]{:S(2)}, u32[]{:S(2)}) collective-permute-start(f32[8,6144]{1,0:T(8,128)S(1)} %shard_map.87), channel_id=1, source_target_pairs={{0,4},{1,5},{2,6},{3,7},{4,0},{5,1},{6,2},{7,3},{8,12},{9,13},{10,... | collective-permute-start | bytes 589832 | tf_op jit(solution)/shard_map/ppermute | solution.py:16
  26.2 12.2 %collective-permute-start.9 = (f32[8,6144]{1,0:T(8,128)S(1)}, f32[8,6144]{1,0:T(8,128)S(1)}, u32[]{:S(2)}, u32[]{:S(2)}) collective-permute-start(f32[8,6144]{1,0:T(8,128)S(1)} %shard_map.86), channel_id=1, source_target_pairs={{0,8},{1,9},{2,10},{3,11},{4,12},{5,13},{6,14},{7,15},{8,0},{9,1},... | collective-permute-start | bytes 589832 | tf_op jit(solution)/shard_map/ppermute | solution.py:16
  26.7 5.7 %collective-permute-start.1 = (bf16[1,8,6144]{2,1,0:T(8,128)(2,1)S(1)}, bf16[1,8,6144]{2,1,0:T(8,128)(2,1)S(1)}, u32[]{:S(2)}, u32[]{:S(2)}) collective-permute-start(bf16[1,8,6144]{2,1,0:T(8,128)(2,1)S(1)} %get-tuple-element.27), channel_id=1, source_target_pairs={{0,2},{1,3},{2,0},{3,1},{4,6},{5,7},{6,4},{7,5},{8,10},{9,11},{10,... | collective-permute-start | bytes 294920 | tf_op jit(solution)/shard_map/ppermute | solution.py:16
  28.1 5.2 %collective-permute-start.2 = (bf16[1,8,6144]{2,1,0:T(8,128)(2,1)S(1)}, bf16[1,8,6144]{2,1,0:T(8,128)(2,1)S(1)}, u32[]{:S(2)}, u32[]{:S(2)}) collective-permute-start(bf16[1,8,6144]{2,1,0:T(8,128)(2,1)S(1)} %get-tuple-element.28), channel_id=1, source_target_pairs={{0,3},{1,2},{2,1},{3,0},{4,7},{5,6},{6,5},{7,4},{8,11},{9,10},{10,... | collective-permute-start | bytes 294920 | tf_op jit(solution)/shard_map/ppermute | solution.py:16
  50.0 7.5 %collective-permute-start.15 = (bf16[8,6144]{1,0:T(8,128)(2,1)S(1)}, bf16[8,6144]{1,0:T(8,128)(2,1)S(1)}, u32[]{:S(2)}, u32[]{:S(2)}) collective-permute-start(bf16[8,6144]{1,0:T(8,128)(2,1)S(1)} %shard_map.90.refs_0_), channel_id=1, source_target_pairs={{0,12},{1,13},{2,14},{3,15},{4,8},{5,9},{6,10},{7,11},{8,4},{9,5},... | collective-permute-start | bytes 294920 | tf_op jit(solution)/shard_map/ppermute | solution.py:16
  50.6 8.1 %collective-permute-start.18 = (bf16[8,6144]{1,0:T(8,128)(2,1)S(1)}, bf16[8,6144]{1,0:T(8,128)(2,1)S(1)}, u32[]{:S(2)}, u32[]{:S(2)}) collective-permute-start(bf16[8,6144]{1,0:T(8,128)(2,1)S(1)} %shard_map.90.refs_0_), channel_id=1, source_target_pairs={{0,4},{1,5},{2,6},{3,7},{4,0},{5,1},{6,2},{7,3},{8,12},{9,13},{10,... | collective-permute-start | bytes 294920 | tf_op jit(solution)/shard_map/ppermute | solution.py:16
  51.2 9.7 %collective-permute-start.21 = (bf16[8,6144]{1,0:T(8,128)(2,1)S(1)}, bf16[8,6144]{1,0:T(8,128)(2,1)S(1)}, u32[]{:S(2)}, u32[]{:S(2)}) collective-permute-start(bf16[8,6144]{1,0:T(8,128)(2,1)S(1)} %shard_map.90.refs_0_), channel_id=1, source_target_pairs={{0,8},{1,9},{2,10},{3,11},{4,12},{5,13},{6,14},{7,15},{8,0},{9,1},... | collective-permute-start | bytes 294920 | tf_op jit(solution)/shard_map/ppermute | solution.py:16
  54.5 7.2 %collective-permute-start.24 = (bf16[8,6144]{1,0:T(8,128)(2,1)S(1)}, bf16[8,6144]{1,0:T(8,128)(2,1)S(1)}, u32[]{:S(2)}, u32[]{:S(2)}) collective-permute-start(bf16[8,6144]{1,0:T(8,128)(2,1)S(1)} %shard_map.90.refs_0_), channel_id=1, source_target_pairs={{0,1},{1,0},{2,3},{3,2},{4,5},{5,4},{6,7},{7,6},{8,9},{9,8},{10,11... | collective-permute-start | bytes 294920 | tf_op jit(solution)/shard_map/ppermute | solution.py:16
  54.5 8.5 %collective-permute-start.13 = (bf16[8,6144]{1,0:T(8,128)(2,1)S(1)}, bf16[8,6144]{1,0:T(8,128)(2,1)S(1)}, u32[]{:S(2)}, u32[]{:S(2)}) collective-permute-start(bf16[8,6144]{1,0:T(8,128)(2,1)S(1)} %shard_map.90.refs_0_), channel_id=1, source_target_pairs={{0,2},{1,3},{2,0},{3,1},{4,6},{5,7},{6,4},{7,5},{8,10},{9,11},{10,... | collective-permute-start | bytes 294920 | tf_op jit(solution)/shard_map/ppermute | solution.py:16
  57.6 6.1 %collective-permute-start.25 = (bf16[8,6144]{1,0:T(8,128)(2,1)S(1)}, bf16[8,6144]{1,0:T(8,128)(2,1)S(1)}, u32[]{:S(2)}, u32[]{:S(2)}) collective-permute-start(bf16[8,6144]{1,0:T(8,128)(2,1)S(1)} %collective-permute-done.15.refs_1_), channel_id=1, source_target_pairs={{0,1},{1,0},{2,3},{3,2},{4,5},{5,4},{6,7},{7,6},{8,9},{9,8},{10,11... | collective-permute-start | bytes 294920 | tf_op jit(solution)/shard_map/ppermute | solution.py:16
  61.0 5.7 %collective-permute-start.16 = (bf16[8,6144]{1,0:T(8,128)(2,1)S(1)}, bf16[8,6144]{1,0:T(8,128)(2,1)S(1)}, u32[]{:S(2)}, u32[]{:S(2)}) collective-permute-start(bf16[8,6144]{1,0:T(8,128)(2,1)S(1)} %collective-permute-done.15.refs_1_), channel_id=1, source_target_pairs={{0,2},{1,3},{2,0},{3,1},{4,6},{5,7},{6,4},{7,5},{8,10},{9,11},{10,... | collective-permute-start | bytes 294920 | tf_op jit(solution)/shard_map/ppermute | solution.py:16
  61.7 7.1 %collective-permute-start.19 = (bf16[8,6144]{1,0:T(8,128)(2,1)S(1)}, bf16[8,6144]{1,0:T(8,128)(2,1)S(1)}, u32[]{:S(2)}, u32[]{:S(2)}) collective-permute-start(bf16[8,6144]{1,0:T(8,128)(2,1)S(1)} %collective-permute-done.18.refs_2_), channel_id=1, source_target_pairs={{0,2},{1,3},{2,0},{3,1},{4,6},{5,7},{6,4},{7,5},{8,10},{9,11},{10,... | collective-permute-start | bytes 294920 | tf_op jit(solution)/shard_map/ppermute | solution.py:16
  63.0 6.8 %collective-permute-start.22 = (bf16[8,6144]{1,0:T(8,128)(2,1)S(1)}, bf16[8,6144]{1,0:T(8,128)(2,1)S(1)}, u32[]{:S(2)}, u32[]{:S(2)}) collective-permute-start(bf16[8,6144]{1,0:T(8,128)(2,1)S(1)} %collective-permute-done.21.refs_3_), channel_id=1, source_target_pairs={{0,2},{1,3},{2,0},{3,1},{4,6},{5,7},{6,4},{7,5},{8,10},{9,11},{10,... | collective-permute-start | bytes 294920 | tf_op jit(solution)/shard_map/ppermute | solution.py:16
  63.7 7.2 %collective-permute-start.27 = (bf16[8,6144]{1,0:T(8,128)(2,1)S(1)}, bf16[8,6144]{1,0:T(8,128)(2,1)S(1)}, u32[]{:S(2)}, u32[]{:S(2)}) collective-permute-start(bf16[8,6144]{1,0:T(8,128)(2,1)S(1)} %collective-permute-done.21.refs_3_), channel_id=1, source_target_pairs={{0,1},{1,0},{2,3},{3,2},{4,5},{5,4},{6,7},{7,6},{8,9},{9,8},{10,11... | collective-permute-start | bytes 294920 | tf_op jit(solution)/shard_map/ppermute | solution.py:16
  63.7 8.9 %collective-permute-start.14 = (bf16[8,6144]{1,0:T(8,128)(2,1)S(1)}, bf16[8,6144]{1,0:T(8,128)(2,1)S(1)}, u32[]{:S(2)}, u32[]{:S(2)}) collective-permute-start(bf16[8,6144]{1,0:T(8,128)(2,1)S(1)} %collective-permute-done.13.refs_0_), channel_id=1, source_target_pairs={{0,1},{1,0},{2,3},{3,2},{4,5},{5,4},{6,7},{7,6},{8,9},{9,8},{10,11... | collective-permute-start | bytes 294920 | tf_op jit(solution)/shard_map/ppermute | solution.py:16
  66.7 6.0 %collective-permute-start.17 = (bf16[8,6144]{1,0:T(8,128)(2,1)S(1)}, bf16[8,6144]{1,0:T(8,128)(2,1)S(1)}, u32[]{:S(2)}, u32[]{:S(2)}) collective-permute-start(bf16[8,6144]{1,0:T(8,128)(2,1)S(1)} %collective-permute-done.16.refs_1_), channel_id=1, source_target_pairs={{0,1},{1,0},{2,3},{3,2},{4,5},{5,4},{6,7},{7,6},{8,9},{9,8},{10,11... | collective-permute-start | bytes 294920 | tf_op jit(solution)/shard_map/ppermute | solution.py:16
  (7 other events, 87.5 us)

commit v4 on v3

--- a/solution.py
+++ b/solution.py
@@ -19,10 +19,6 @@
 def _hop(array, moves):
     near = range(NEAR)
     return lax.ppermute(array, "dp", [(a * NEAR + j, b * NEAR + j) for a, b in moves.items() for j in near])
-
-
-def _pick(array, index):
-    return lax.dynamic_index_in_dim(array, index, 0, keepdims=False)
 
 
 def _call(body, outs, *args):
@@ -49,22 +45,40 @@
     return [3, 1, 2] if far == 4 else list(range(1, far))
 
 
+def _copy_rows(wanted, blocks, *refs):
+    *outs, done = refs
+    me = lax.axis_index("dp")
+    copies = []
+    for offsets, out in zip(wanted, outs):
+        for i, offset in enumerate(offsets):
+            copies.append(pltpu.make_async_copy(blocks.at[me ^ offset], out.at[i], done.at[len(copies)]))
+    for copy in copies:
+        copy.start()
+    for copy in copies:
+        copy.wait()
+
+
+def _cut(blocks, wanted):
+    _, rows, width = blocks.shape
+    return pl.pallas_call(
+        functools.partial(_copy_rows, wanted),
+        out_shape=[pltpu.VMEM((len(offsets), rows, width), blocks.dtype) for offsets in wanted],
+        in_specs=[pl.BlockSpec(memory_space=pl.ANY)],
+        out_specs=[VMEM] * len(wanted),
+        scratch_shapes=[pltpu.SemaphoreType.DMA((sum(map(len, wanted)),))],
+        cost_estimate=pl.CostEstimate(flops=1000000, bytes_accessed=1000000, transcendentals=0),
+    )(pltpu.with_memory_space_constraint(blocks, pltpu.HBM))
+
+
 def _near_sums(grads, rows, width, size):
-    far = size // NEAR
-    me = lax.axis_index("dp")
-    far_at, near_at = me // NEAR, me % NEAR
-
-    def piece(grads, offsets, j):
-        blocks = grads.reshape(far, NEAR, rows, width)
-        return jnp.stack([_pick(_pick(blocks, far_at ^ k), near_at ^ j) for k in offsets])
-
+    blocks = grads.reshape(size, rows, width)
     groups = _groups(size)
     order = _far_order(size)
-    first = lax.optimization_barrier([piece(grads, groups[0], j) for j in (2, 3)])
-    grads, _ = lax.optimization_barrier((grads, first))
-    own, pair = piece(grads, order, 0), piece(grads, order, 1)
-    rest = [[piece(grads, group, j) for j in (2, 3)] for group in groups[1:]]
-    own, pair, rest = lax.optimization_barrier((own, pair, rest))
+    first = _cut(blocks, [[k * NEAR + j for k in groups[0]] for j in (2, 3)])
+    wanted = [[k * NEAR + j for k in group] for group in groups[1:] for j in (2, 3)]
+    rest = _cut(blocks, [[k * NEAR + j for k in order] for j in (0, 1)] + wanted)
+    own, pair, *rest = rest
+    rest = list(zip(rest[::2], rest[1::2]))
     moved = []
     for pieces in [first, *rest]:
         moved.append([_swap(pieces[0], size, 2), _swap(pieces[1], size, 3)])

time: 73.7 us -> 73.6 us (level)
  Pallas kernels: 4.3 us -> 6.78 us
  local copies, waits for them, and re-layouts: 2.49 us -> 0.02 us
    pallas_call x0 -> x2, Pallas kernels: none -> 2.48 us  [_cut(): pl.pallas_call(functools.partial(_copy_rows, wanted), out_shape=[pltpu.VM...]
    dynamic_slice x2 -> x0, local copies, waits for them, and re-layouts: 2.47 us -> none  [_pick(): return lax.dynamic_index_in_dim(array, index, 0, keepdims=False)]
  transfers between devices with their start and end apart: 28 -> 28, of which waited for: 15 -> 15; matrix products, arithmetic and copies ran while one was open for 0% -> 0% of each run, Pallas kernels for 4% -> 5%
where the time goes in v4:
time: 73.6 us; the launch traced here: 73.4 us
  waiting for transfers between devices  31.7 us (43%)
  starting transfers between devices  23 us (31%)
  blocking collectives  11.1 us (15%)
  Pallas kernels  6.78 us (9%)
  between operations  0.81 us (1%)
    ppermute x26, waiting for transfers between devices, _swap(): return lax.ppermute(array, 'dp', [(i, i ^ offset) for i in range(size)])  31.7 us
    ppermute x26, starting transfers between devices, _swap(): return lax.ppermute(array, 'dp', [(i, i ^ offset) for i in range(size)])  18.9 us
    all_to_all x1, blocking collectives, _step(): squares = lax.all_to_all(square, ('expert', 'dp'), 0, 0)  11.1 us
    ppermute x2, starting transfers between devices, _hop(): lax.ppermute(array, 'dp', [(a * NEAR + j, b * NEAR + j) for a, b in moves...  4.09 us
    pallas_call x3, Pallas kernels, _placed(): pl.pallas_call(body, out_shape=jax.ShapeDtypeStruct((size, height, width)...  2.51 us
    pallas_call x2, Pallas kernels, _cut(): pl.pallas_call(functools.partial(_copy_rows, wanted), out_shape=[pltpu.VM...  2.48 us
    pallas_call x8, Pallas kernels, _call(): pl.pallas_call(body, out_shape=outs, in_specs=[VMEM] * len(args), out_spe...  1.79 us
  transfers between devices with their start and end apart: 28, of which 15 were waited for; matrix products, arithmetic and copies ran while one was open for 0% of the time, Pallas kernels for 5%

profile of v4, /device:TPU:0, one launch (start us, length us, event | category | flops | bytes accessed | tf_op | source)
XLA Modules:
  0.0 73.4 jit_solution(14141754008320551167)
XLA Ops:
  0.6 1.5 %shard_map.83 = (bf16[4,8,6144]{2,1,0:T(8,128)(2,1)S(1)}, bf16[4,8,6144]{2,1,0:T(8,128)(2,1)S(1)}, bf16[1,8,6144]{2,1,0:T(8,128)(2,1)S(1)}, bf16[1,8,6144]{2,1,0...) custom-call(bf16[16,8,6144]{2,1,0:T(8,128)(2,1)} %bitcast.16), custom_call_target="tpu_custom_call" | custom-call | flops 1000000 | bytes 1000000 | tf_op jit(solution)/shard_map/pallas_call | solution.py:63
  3.7 2.6 %collective-permute-start.3 = (bf16[1,8,6144]{2,1,0:T(8,128)(2,1)S(1)}, bf16[1,8,6144]{2,1,0:T(8,128)(2,1)S(1)}, u32[]{:S(2)}, u32[]{:S(2)}) collective-permute-start(bf16[1,8,6144]{2,1,0:T(8,128)(2,1)S(1)} %get-tuple-element.25), channel_id=1, source_target_pairs={{0,2},{1,3},{2,0},{3,1},{4,6},{5,7},{6,4},{7,5},{8,10},{9,11},{10,... | collective-permute-start | bytes 294920 | tf_op jit(solution)/shard_map/ppermute | solution.py:16
  6.4 3.5 %collective-permute-done.3.left = bf16[1,8,6144]{2,1,0:T(8,128)(2,1)S(1)} collective-permute-done((bf16[1,8,6144]{2,1,0:T(8,128)(2,1)S(1)}, bf16[1,8,6144]{2,1,0:T(8,128)(2,1)S(1)}, u32[]{:S(2)}, u32[]{:S(2)}) %collective-permute-start.3) | collective-permute-done | bytes 98336 | tf_op jit(solution)/shard_map/ppermute | solution.py:16
  9.9 1.7 %collective-permute-done.4.right = bf16[1,8,6144]{2,1,0:T(8,128)(2,1)S(1)} collective-permute-done((bf16[1,8,6144]{2,1,0:T(8,128)(2,1)S(1)}, bf16[1,8,6144]{2,1,0:T(8,128)(2,1)S(1)}, u32[]{:S(2)}, u32[]{:S(2)}) %collective-permute-start.4) | collective-permute-done | bytes 98336 | tf_op jit(solution)/shard_map/ppermute | solution.py:16
  11.7 3.4 %collective-permute-start.8 = (f32[8,6144]{1,0:T(8,128)S(1)}, f32[8,6144]{1,0:T(8,128)S(1)}, u32[]{:S(2)}, u32[]{:S(2)}) collective-permute-start(f32[8,6144]{1,0:T(8,128)S(1)} %shard_map.86), channel_id=1, source_target_pairs={{12,8},{13,9},{14,10},{15,11},{0,4},{1,5},{2,6},{3,7},{28,24},{29,... | collective-permute-start | bytes 589832 | tf_op jit(solution)/shard_map/ppermute | solution.py:21
  15.1 1.6 %collective-permute-start.10 = (bf16[1,8,6144]{2,1,0:T(8,128)(2,1)S(1)}, bf16[1,8,6144]{2,1,0:T(8,128)(2,1)S(1)}, u32[]{:S(2)}, u32[]{:S(2)}) collective-permute-start(bf16[1,8,6144]{2,1,0:T(8,128)(2,1)S(1)} %get-tuple-element.29), channel_id=1, source_target_pairs={{0,2},{1,3},{2,0},{3,1},{4,6},{5,7},{6,4},{7,5},{8,10},{9,11},{10,... | collective-permute-start | bytes 294920 | tf_op jit(solution)/shard_map/ppermute | solution.py:16
  16.7 1.4 %collective-permute-start.6 = (bf16[1,8,6144]{2,1,0:T(8,128)(2,1)S(1)}, bf16[1,8,6144]{2,1,0:T(8,128)(2,1)S(1)}, u32[]{:S(2)}, u32[]{:S(2)}) collective-permute-start(bf16[1,8,6144]{2,1,0:T(8,128)(2,1)S(1)} %get-tuple-element.27), channel_id=1, source_target_pairs={{0,2},{1,3},{2,0},{3,1},{4,6},{5,7},{6,4},{7,5},{8,10},{9,11},{10,... | collective-permute-start | bytes 294920 | tf_op jit(solution)/shard_map/ppermute | solution.py:16
  18.7 1.5 %collective-permute-done.10.left = bf16[1,8,6144]{2,1,0:T(8,128)(2,1)S(1)} collective-permute-done((bf16[1,8,6144]{2,1,0:T(8,128)(2,1)S(1)}, bf16[1,8,6144]{2,1,0:T(8,128)(2,1)S(1)}, u32[]{:S(2)}, u32[]{:S(2)}) %collective-permute-start.10) | collective-permute-done | bytes 98336 | tf_op jit(solution)/shard_map/ppermute | solution.py:16
  20.8 1.2 %collective-permute-done.11.right = bf16[1,8,6144]{2,1,0:T(8,128)(2,1)S(1)} collective-permute-done((bf16[1,8,6144]{2,1,0:T(8,128)(2,1)S(1)}, bf16[1,8,6144]{2,1,0:T(8,128)(2,1)S(1)}, u32[]{:S(2)}, u32[]{:S(2)}) %collective-permute-start.11) | collective-permute-done | bytes 98336 | tf_op jit(solution)/shard_map/ppermute | solution.py:16
  22.0 1.6 %collective-permute-start.12 = (f32[8,6144]{1,0:T(8,128)S(1)}, f32[8,6144]{1,0:T(8,128)S(1)}, u32[]{:S(2)}, u32[]{:S(2)}) collective-permute-start(f32[8,6144]{1,0:T(8,128)S(1)} %shard_map.89), channel_id=1, source_target_pairs={{0,4},{1,5},{2,6},{3,7},{4,0},{5,1},{6,2},{7,3},{8,12},{9,13},{10,... | collective-permute-start | bytes 589832 | tf_op jit(solution)/shard_map/ppermute | solution.py:16
  24.3 1.7 %collective-permute-done.7.right = bf16[1,8,6144]{2,1,0:T(8,128)(2,1)S(1)} collective-permute-done((bf16[1,8,6144]{2,1,0:T(8,128)(2,1)S(1)}, bf16[1,8,6144]{2,1,0:T(8,128)(2,1)S(1)}, u32[]{:S(2)}, u32[]{:S(2)}) %collective-permute-start.7) | collective-permute-done | bytes 98336 | tf_op jit(solution)/shard_map/ppermute | solution.py:16
  26.6 1.4 %collective-permute-start.1 = (bf16[1,8,6144]{2,1,0:T(8,128)(2,1)S(1)}, bf16[1,8,6144]{2,1,0:T(8,128)(2,1)S(1)}, u32[]{:S(2)}, u32[]{:S(2)}) collective-permute-start(bf16[1,8,6144]{2,1,0:T(8,128)(2,1)S(1)} %get-tuple-element.23), channel_id=1, source_target_pairs={{0,2},{1,3},{2,0},{3,1},{4,6},{5,7},{6,4},{7,5},{8,10},{9,11},{10,... | collective-permute-start | bytes 294920 | tf_op jit(solution)/shard_map/ppermute | solution.py:16
  28.3 4.0 %collective-permute-done.1.left = bf16[1,8,6144]{2,1,0:T(8,128)(2,1)S(1)} collective-permute-done((bf16[1,8,6144]{2,1,0:T(8,128)(2,1)S(1)}, bf16[1,8,6144]{2,1,0:T(8,128)(2,1)S(1)}, u32[]{:S(2)}, u32[]{:S(2)}) %collective-permute-start.1) | collective-permute-done | bytes 98336 | tf_op jit(solution)/shard_map/ppermute | solution.py:16
  33.2 5.1 %collective-permute-done.9.refs_2_ = f32[8,6144]{1,0:T(8,128)S(1)} collective-permute-done((f32[8,6144]{1,0:T(8,128)S(1)}, f32[8,6144]{1,0:T(8,128)S(1)}, u32[]{:S(2)}, u32[]{:S(2)}) %collective-permute-start.9) | collective-permute-done | bytes 196640 | tf_op jit(solution)/shard_map/ppermute | solution.py:16
  38.5 11.1 %all_to_all.5.squares = f32[32,1,128]{2,1,0:T(1,128)S(1)} all-to-all(f32[32,1,128]{2,1,0:T(1,128)S(1)} %get-tuple-element.31), channel_id=1, replica_groups=mesh['expert'=2,'dp'=16] {'expert','dp'}, dimensions={0} | all-to-all | bytes 32768 | tf_op jit(solution)/shard_map/all_to_all | solution.py:193
  51.2 3.2 %collective-permute-start.21 = (bf16[8,6144]{1,0:T(8,128)(2,1)S(1)}, bf16[8,6144]{1,0:T(8,128)(2,1)S(1)}, u32[]{:S(2)}, u32[]{:S(2)}) collective-permute-start(bf16[8,6144]{1,0:T(8,128)(2,1)S(1)} %shard_map.92.refs_0_), channel_id=1, source_target_pairs={{0,8},{1,9},{2,10},{3,11},{4,12},{5,13},{6,14},{7,15},{8,0},{9,1},... | collective-permute-start | bytes 294920 | tf_op jit(solution)/shard_map/ppermute | solution.py:16
  55.0 2.5 %collective-permute-done.15.refs_1_ = bf16[8,6144]{1,0:T(8,128)(2,1)S(1)} collective-permute-done((bf16[8,6144]{1,0:T(8,128)(2,1)S(1)}, bf16[8,6144]{1,0:T(8,128)(2,1)S(1)}, u32[]{:S(2)}, u32[]{:S(2)}) %collective-permute-start.15) | collective-permute-done | bytes 98336 | tf_op jit(solution)/shard_map/ppermute | solution.py:16
  57.5 1.1 %collective-permute-done.18.refs_2_ = bf16[8,6144]{1,0:T(8,128)(2,1)S(1)} collective-permute-done((bf16[8,6144]{1,0:T(8,128)(2,1)S(1)}, bf16[8,6144]{1,0:T(8,128)(2,1)S(1)}, u32[]{:S(2)}, u32[]{:S(2)}) %collective-permute-start.18) | collective-permute-done | bytes 98336 | tf_op jit(solution)/shard_map/ppermute | solution.py:16
  58.6 2.3 %collective-permute-done.21.refs_3_ = bf16[8,6144]{1,0:T(8,128)(2,1)S(1)} collective-permute-done((bf16[8,6144]{1,0:T(8,128)(2,1)S(1)}, bf16[8,6144]{1,0:T(8,128)(2,1)S(1)}, u32[]{:S(2)}, u32[]{:S(2)}) %collective-permute-start.21) | collective-permute-done | bytes 98336 | tf_op jit(solution)/shard_map/ppermute | solution.py:16
  61.6 1.4 %collective-permute-start.19 = (bf16[8,6144]{1,0:T(8,128)(2,1)S(1)}, bf16[8,6144]{1,0:T(8,128)(2,1)S(1)}, u32[]{:S(2)}, u32[]{:S(2)}) collective-permute-start(bf16[8,6144]{1,0:T(8,128)(2,1)S(1)} %collective-permute-done.18.refs_2_), channel_id=1, source_target_pairs={{0,2},{1,3},{2,0},{3,1},{4,6},{5,7},{6,4},{7,5},{8,10},{9,11},{10,... | collective-permute-start | bytes 294920 | tf_op jit(solution)/shard_map/ppermute | solution.py:16
  64.1 2.4 %collective-permute-done.16.refs_1_ = bf16[8,6144]{1,0:T(8,128)(2,1)S(1)} collective-permute-done((bf16[8,6144]{1,0:T(8,128)(2,1)S(1)}, bf16[8,6144]{1,0:T(8,128)(2,1)S(1)}, u32[]{:S(2)}, u32[]{:S(2)}) %collective-permute-start.16) | collective-permute-done | bytes 98336 | tf_op jit(solution)/shard_map/ppermute | solution.py:16
  66.6 2.1 %collective-permute-done.19.refs_2_ = bf16[8,6144]{1,0:T(8,128)(2,1)S(1)} collective-permute-done((bf16[8,6144]{1,0:T(8,128)(2,1)S(1)}, bf16[8,6144]{1,0:T(8,128)(2,1)S(1)}, u32[]{:S(2)}, u32[]{:S(2)}) %collective-permute-start.19) | collective-permute-done | bytes 98336 | tf_op jit(solution)/shard_map/ppermute | solution.py:16
  68.7 1.1 %collective-permute-done.22.refs_3_ = bf16[8,6144]{1,0:T(8,128)(2,1)S(1)} collective-permute-done((bf16[8,6144]{1,0:T(8,128)(2,1)S(1)}, bf16[8,6144]{1,0:T(8,128)(2,1)S(1)}, u32[]{:S(2)}, u32[]{:S(2)}) %collective-permute-start.22) | collective-permute-done | bytes 98336 | tf_op jit(solution)/shard_map/ppermute | solution.py:16
  69.8 1.1 %shard_map.91 = (f32[8,6144]{1,0:T(8,128)}, f32[8,6144]{1,0:T(8,128)}, f32[8,6144]{1,0:T(8,128)}, f32[8,6144]{1,0:T(8,128)}) custom-call(f32[32,1,128]{2,1,0:T(1,128)S(1)} %all_to_all.5.squares, f32[8,6144]{1,0:T(8,128)S(1)} %get-tuple-element.32.summed, f32[8,6144]{1,0:T(8,128)S(1)} %bitcast.10, f32[8,6144]{1,0:T(8,128)S(1)} %bitcast.12, f32[8,6144]{1,0:T(8,128)S(1)} %bitcast.14), custom_call_target="tpu_custom_call" | custom-call | flops 1000000 | bytes 1000000 | tf_op jit(solution)/shard_map/pallas_call | solution.py:25
  (52 shorter events, 12.1 us)
Async XLA Ops:
  2.2 9.5 %collective-permute-start = (bf16[4,8,6144]{2,1,0:T(8,128)(2,1)S(1)}, bf16[4,8,6144]{2,1,0:T(8,128)(2,1)S(1)}, u32[]{:S(2)}, u32[]{:S(2)}) collective-permute-start(bf16[4,8,6144]{2,1,0:T(8,128)(2,1)S(1)} %get-tuple-element.22), channel_id=1, source_target_pairs={{0,1},{1,0},{2,3},{3,2},{4,5},{5,4},{6,7},{7,6},{8,9},{9,8},{10,11... | collective-permute-start | bytes 1179656 | tf_op jit(solution)/shard_map/ppermute | solution.py:16
  3.7 6.2 %collective-permute-start.3 = (bf16[1,8,6144]{2,1,0:T(8,128)(2,1)S(1)}, bf16[1,8,6144]{2,1,0:T(8,128)(2,1)S(1)}, u32[]{:S(2)}, u32[]{:S(2)}) collective-permute-start(bf16[1,8,6144]{2,1,0:T(8,128)(2,1)S(1)} %get-tuple-element.25), channel_id=1, source_target_pairs={{0,2},{1,3},{2,0},{3,1},{4,6},{5,7},{6,4},{7,5},{8,10},{9,11},{10,... | collective-permute-start | bytes 294920 | tf_op jit(solution)/shard_map/ppermute | solution.py:16
  6.3 5.3 %collective-permute-start.4 = (bf16[1,8,6144]{2,1,0:T(8,128)(2,1)S(1)}, bf16[1,8,6144]{2,1,0:T(8,128)(2,1)S(1)}, u32[]{:S(2)}, u32[]{:S(2)}) collective-permute-start(bf16[1,8,6144]{2,1,0:T(8,128)(2,1)S(1)} %get-tuple-element.26), channel_id=1, source_target_pairs={{0,3},{1,2},{2,1},{3,0},{4,7},{5,6},{6,5},{7,4},{8,11},{9,10},{10,... | collective-permute-start | bytes 294920 | tf_op jit(solution)/shard_map/ppermute | solution.py:16
  11.7 14.4 %collective-permute-start.8 = (f32[8,6144]{1,0:T(8,128)S(1)}, f32[8,6144]{1,0:T(8,128)S(1)}, u32[]{:S(2)}, u32[]{:S(2)}) collective-permute-start(f32[8,6144]{1,0:T(8,128)S(1)} %shard_map.86), channel_id=1, source_target_pairs={{12,8},{13,9},{14,10},{15,11},{0,4},{1,5},{2,6},{3,7},{28,24},{29,... | collective-permute-start | bytes 589832 | tf_op jit(solution)/shard_map/ppermute | solution.py:21
  16.7 5.3 %collective-permute-start.11 = (bf16[1,8,6144]{2,1,0:T(8,128)(2,1)S(1)}, bf16[1,8,6144]{2,1,0:T(8,128)(2,1)S(1)}, u32[]{:S(2)}, u32[]{:S(2)}) collective-permute-start(bf16[1,8,6144]{2,1,0:T(8,128)(2,1)S(1)} %get-tuple-element.30), channel_id=1, source_target_pairs={{0,3},{1,2},{2,1},{3,0},{4,7},{5,6},{6,5},{7,4},{8,11},{9,10},{10,... | collective-permute-start | bytes 294920 | tf_op jit(solution)/shard_map/ppermute | solution.py:16
  16.7 7.6 %collective-permute-start.6 = (bf16[1,8,6144]{2,1,0:T(8,128)(2,1)S(1)}, bf16[1,8,6144]{2,1,0:T(8,128)(2,1)S(1)}, u32[]{:S(2)}, u32[]{:S(2)}) collective-permute-start(bf16[1,8,6144]{2,1,0:T(8,128)(2,1)S(1)} %get-tuple-element.27), channel_id=1, source_target_pairs={{0,2},{1,3},{2,0},{3,1},{4,6},{5,7},{6,4},{7,5},{8,10},{9,11},{10,... | collective-permute-start | bytes 294920 | tf_op jit(solution)/shard_map/ppermute | solution.py:16
  18.1 7.9 %collective-permute-start.7 = (bf16[1,8,6144]{2,1,0:T(8,128)(2,1)S(1)}, bf16[1,8,6144]{2,1,0:T(8,128)(2,1)S(1)}, u32[]{:S(2)}, u32[]{:S(2)}) collective-permute-start(bf16[1,8,6144]{2,1,0:T(8,128)(2,1)S(1)} %get-tuple-element.28), channel_id=1, source_target_pairs={{0,3},{1,2},{2,1},{3,0},{4,7},{5,6},{6,5},{7,4},{8,11},{9,10},{10,... | collective-permute-start | bytes 294920 | tf_op jit(solution)/shard_map/ppermute | solution.py:16
  20.1 13.0 %collective-permute-start.5 = (f32[8,6144]{1,0:T(8,128)S(1)}, f32[8,6144]{1,0:T(8,128)S(1)}, u32[]{:S(2)}, u32[]{:S(2)}) collective-permute-start(f32[8,6144]{1,0:T(8,128)S(1)} %shard_map.86), channel_id=1, source_target_pairs={{8,4},{9,5},{10,6},{11,7},{4,8},{5,9},{6,10},{7,11},{24,20},{25,21... | collective-permute-start | bytes 589832 | tf_op jit(solution)/shard_map/ppermute | solution.py:21
  22.0 11.1 %collective-permute-start.12 = (f32[8,6144]{1,0:T(8,128)S(1)}, f32[8,6144]{1,0:T(8,128)S(1)}, u32[]{:S(2)}, u32[]{:S(2)}) collective-permute-start(f32[8,6144]{1,0:T(8,128)S(1)} %shard_map.89), channel_id=1, source_target_pairs={{0,4},{1,5},{2,6},{3,7},{4,0},{5,1},{6,2},{7,3},{8,12},{9,13},{10,... | collective-permute-start | bytes 589832 | tf_op jit(solution)/shard_map/ppermute | solution.py:16
  26.1 12.2 %collective-permute-start.9 = (f32[8,6144]{1,0:T(8,128)S(1)}, f32[8,6144]{1,0:T(8,128)S(1)}, u32[]{:S(2)}, u32[]{:S(2)}) collective-permute-start(f32[8,6144]{1,0:T(8,128)S(1)} %shard_map.88), channel_id=1, source_target_pairs={{0,8},{1,9},{2,10},{3,11},{4,12},{5,13},{6,14},{7,15},{8,0},{9,1},... | collective-permute-start | bytes 589832 | tf_op jit(solution)/shard_map/ppermute | solution.py:16
  26.6 5.7 %collective-permute-start.1 = (bf16[1,8,6144]{2,1,0:T(8,128)(2,1)S(1)}, bf16[1,8,6144]{2,1,0:T(8,128)(2,1)S(1)}, u32[]{:S(2)}, u32[]{:S(2)}) collective-permute-start(bf16[1,8,6144]{2,1,0:T(8,128)(2,1)S(1)} %get-tuple-element.23), channel_id=1, source_target_pairs={{0,2},{1,3},{2,0},{3,1},{4,6},{5,7},{6,4},{7,5},{8,10},{9,11},{10,... | collective-permute-start | bytes 294920 | tf_op jit(solution)/shard_map/ppermute | solution.py:16
  28.0 5.2 %collective-permute-start.2 = (bf16[1,8,6144]{2,1,0:T(8,128)(2,1)S(1)}, bf16[1,8,6144]{2,1,0:T(8,128)(2,1)S(1)}, u32[]{:S(2)}, u32[]{:S(2)}) collective-permute-start(bf16[1,8,6144]{2,1,0:T(8,128)(2,1)S(1)} %get-tuple-element.24), channel_id=1, source_target_pairs={{0,3},{1,2},{2,1},{3,0},{4,7},{5,6},{6,5},{7,4},{8,11},{9,10},{10,... | collective-permute-start | bytes 294920 | tf_op jit(solution)/shard_map/ppermute | solution.py:16
  50.0 7.5 %collective-permute-start.15 = (bf16[8,6144]{1,0:T(8,128)(2,1)S(1)}, bf16[8,6144]{1,0:T(8,128)(2,1)S(1)}, u32[]{:S(2)}, u32[]{:S(2)}) collective-permute-start(bf16[8,6144]{1,0:T(8,128)(2,1)S(1)} %shard_map.92.refs_0_), channel_id=1, source_target_pairs={{0,12},{1,13},{2,14},{3,15},{4,8},{5,9},{6,10},{7,11},{8,4},{9,5},... | collective-permute-start | bytes 294920 | tf_op jit(solution)/shard_map/ppermute | solution.py:16
  50.5 8.1 %collective-permute-start.18 = (bf16[8,6144]{1,0:T(8,128)(2,1)S(1)}, bf16[8,6144]{1,0:T(8,128)(2,1)S(1)}, u32[]{:S(2)}, u32[]{:S(2)}) collective-permute-start(bf16[8,6144]{1,0:T(8,128)(2,1)S(1)} %shard_map.92.refs_0_), channel_id=1, source_target_pairs={{0,4},{1,5},{2,6},{3,7},{4,0},{5,1},{6,2},{7,3},{8,12},{9,13},{10,... | collective-permute-start | bytes 294920 | tf_op jit(solution)/shard_map/ppermute | solution.py:16
  51.2 9.7 %collective-permute-start.21 = (bf16[8,6144]{1,0:T(8,128)(2,1)S(1)}, bf16[8,6144]{1,0:T(8,128)(2,1)S(1)}, u32[]{:S(2)}, u32[]{:S(2)}) collective-permute-start(bf16[8,6144]{1,0:T(8,128)(2,1)S(1)} %shard_map.92.refs_0_), channel_id=1, source_target_pairs={{0,8},{1,9},{2,10},{3,11},{4,12},{5,13},{6,14},{7,15},{8,0},{9,1},... | collective-permute-start | bytes 294920 | tf_op jit(solution)/shard_map/ppermute | solution.py:16
  54.4 7.2 %collective-permute-start.24 = (bf16[8,6144]{1,0:T(8,128)(2,1)S(1)}, bf16[8,6144]{1,0:T(8,128)(2,1)S(1)}, u32[]{:S(2)}, u32[]{:S(2)}) collective-permute-start(bf16[8,6144]{1,0:T(8,128)(2,1)S(1)} %shard_map.92.refs_0_), channel_id=1, source_target_pairs={{0,1},{1,0},{2,3},{3,2},{4,5},{5,4},{6,7},{7,6},{8,9},{9,8},{10,11... | collective-permute-start | bytes 294920 | tf_op jit(solution)/shard_map/ppermute | solution.py:16
  54.4 8.5 %collective-permute-start.13 = (bf16[8,6144]{1,0:T(8,128)(2,1)S(1)}, bf16[8,6144]{1,0:T(8,128)(2,1)S(1)}, u32[]{:S(2)}, u32[]{:S(2)}) collective-permute-start(bf16[8,6144]{1,0:T(8,128)(2,1)S(1)} %shard_map.92.refs_0_), channel_id=1, source_target_pairs={{0,2},{1,3},{2,0},{3,1},{4,6},{5,7},{6,4},{7,5},{8,10},{9,11},{10,... | collective-permute-start | bytes 294920 | tf_op jit(solution)/shard_map/ppermute | solution.py:16
  57.5 6.1 %collective-permute-start.25 = (bf16[8,6144]{1,0:T(8,128)(2,1)S(1)}, bf16[8,6144]{1,0:T(8,128)(2,1)S(1)}, u32[]{:S(2)}, u32[]{:S(2)}) collective-permute-start(bf16[8,6144]{1,0:T(8,128)(2,1)S(1)} %collective-permute-done.15.refs_1_), channel_id=1, source_target_pairs={{0,1},{1,0},{2,3},{3,2},{4,5},{5,4},{6,7},{7,6},{8,9},{9,8},{10,11... | collective-permute-start | bytes 294920 | tf_op jit(solution)/shard_map/ppermute | solution.py:16
  60.9 5.7 %collective-permute-start.16 = (bf16[8,6144]{1,0:T(8,128)(2,1)S(1)}, bf16[8,6144]{1,0:T(8,128)(2,1)S(1)}, u32[]{:S(2)}, u32[]{:S(2)}) collective-permute-start(bf16[8,6144]{1,0:T(8,128)(2,1)S(1)} %collective-permute-done.15.refs_1_), channel_id=1, source_target_pairs={{0,2},{1,3},{2,0},{3,1},{4,6},{5,7},{6,4},{7,5},{8,10},{9,11},{10,... | collective-permute-start | bytes 294920 | tf_op jit(solution)/shard_map/ppermute | solution.py:16
  61.6 7.1 %collective-permute-start.19 = (bf16[8,6144]{1,0:T(8,128)(2,1)S(1)}, bf16[8,6144]{1,0:T(8,128)(2,1)S(1)}, u32[]{:S(2)}, u32[]{:S(2)}) collective-permute-start(bf16[8,6144]{1,0:T(8,128)(2,1)S(1)} %collective-permute-done.18.refs_2_), channel_id=1, source_target_pairs={{0,2},{1,3},{2,0},{3,1},{4,6},{5,7},{6,4},{7,5},{8,10},{9,11},{10,... | collective-permute-start | bytes 294920 | tf_op jit(solution)/shard_map/ppermute | solution.py:16
  62.9 6.8 %collective-permute-start.22 = (bf16[8,6144]{1,0:T(8,128)(2,1)S(1)}, bf16[8,6144]{1,0:T(8,128)(2,1)S(1)}, u32[]{:S(2)}, u32[]{:S(2)}) collective-permute-start(bf16[8,6144]{1,0:T(8,128)(2,1)S(1)} %collective-permute-done.21.refs_3_), channel_id=1, source_target_pairs={{0,2},{1,3},{2,0},{3,1},{4,6},{5,7},{6,4},{7,5},{8,10},{9,11},{10,... | collective-permute-start | bytes 294920 | tf_op jit(solution)/shard_map/ppermute | solution.py:16
  63.6 7.2 %collective-permute-start.27 = (bf16[8,6144]{1,0:T(8,128)(2,1)S(1)}, bf16[8,6144]{1,0:T(8,128)(2,1)S(1)}, u32[]{:S(2)}, u32[]{:S(2)}) collective-permute-start(bf16[8,6144]{1,0:T(8,128)(2,1)S(1)} %collective-permute-done.21.refs_3_), channel_id=1, source_target_pairs={{0,1},{1,0},{2,3},{3,2},{4,5},{5,4},{6,7},{7,6},{8,9},{9,8},{10,11... | collective-permute-start | bytes 294920 | tf_op jit(solution)/shard_map/ppermute | solution.py:16
  63.6 8.9 %collective-permute-start.14 = (bf16[8,6144]{1,0:T(8,128)(2,1)S(1)}, bf16[8,6144]{1,0:T(8,128)(2,1)S(1)}, u32[]{:S(2)}, u32[]{:S(2)}) collective-permute-start(bf16[8,6144]{1,0:T(8,128)(2,1)S(1)} %collective-permute-done.13.refs_0_), channel_id=1, source_target_pairs={{0,1},{1,0},{2,3},{3,2},{4,5},{5,4},{6,7},{7,6},{8,9},{9,8},{10,11... | collective-permute-start | bytes 294920 | tf_op jit(solution)/shard_map/ppermute | solution.py:16
  66.6 6.0 %collective-permute-start.17 = (bf16[8,6144]{1,0:T(8,128)(2,1)S(1)}, bf16[8,6144]{1,0:T(8,128)(2,1)S(1)}, u32[]{:S(2)}, u32[]{:S(2)}) collective-permute-start(bf16[8,6144]{1,0:T(8,128)(2,1)S(1)} %collective-permute-done.16.refs_1_), channel_id=1, source_target_pairs={{0,1},{1,0},{2,3},{3,2},{4,5},{5,4},{6,7},{7,6},{8,9},{9,8},{10,11... | collective-permute-start | bytes 294920 | tf_op jit(solution)/shard_map/ppermute | solution.py:16
  (7 other events, 87.4 us)

commit v5 on v4

--- a/solution.py
+++ b/solution.py
@@ -14,11 +14,6 @@
 
 def _swap(array, size, offset):
     return lax.ppermute(array, "dp", [(i, i ^ offset) for i in range(size)])
-
-
-def _hop(array, moves):
-    near = range(NEAR)
-    return lax.ppermute(array, "dp", [(a * NEAR + j, b * NEAR + j) for a, b in moves.items() for j in near])
 
 
 def _call(body, outs, *args):
@@ -99,22 +94,11 @@
 
 
 def _far_sums(sums, size):
-    far = size // NEAR
     parts = []
     order = _far_order(size)[:-1]
-    if far == 4:
-        relayed = _hop(sums[3], {3: 2, 0: 1})
-        parts.append(_hop(sums[3], {2: 1, 1: 2}))
-        (joined,) = _call(_add, (pltpu.VMEM(sums[2].shape, jnp.float32),), sums[2], relayed)
-        sums = {**sums, 2: joined}
-        order = order[1:]
     for k in order:
         parts.append(_swap(sums[k], size, k * NEAR))
     return parts
-
-
-def _add(left, right, total):
-    total[...] = left[...] + right[...]
 
 
 def _finish_sum(*refs):

time: 73.6 us -> 72 us (0.978)
  waiting for transfers between devices: 31.7 us -> 23.8 us
  blocking collectives: 11.1 us -> 15.8 us
  starting transfers between devices: 23 us -> 24.6 us
    ppermute x26 -> x27, waiting for transfers between devices: 31.7 us -> 23.8 us  [_swap(): return lax.ppermute(array, 'dp', [(i, i ^ offset) for i in range(size)])]
    ppermute x26 -> x27, starting transfers between devices: 18.9 us -> 24.6 us  [_swap(): return lax.ppermute(array, 'dp', [(i, i ^ offset) for i in range(size)])]
    all_to_all x1, blocking collectives: 11.1 us -> 15.8 us  [_step(): squares = lax.all_to_all(square, ('expert', 'dp'), 0, 0)]
    ppermute x2 -> x0, starting transfers between devices: 4.09 us -> none  [_hop(): lax.ppermute(array, 'dp', [(a * NEAR + j, b * NEAR + j) for a, b in moves...]
    pallas_call x8 -> x7, Pallas kernels: 1.79 us -> 1.77 us  [_call(): pl.pallas_call(body, out_shape=outs, in_specs=[VMEM] * len(args), out_spe...]
  transfers between devices with their start and end apart: 28 -> 27, of which waited for: 15 -> 13; matrix products, arithmetic and copies ran while one was open for 0% -> 0% of each run, Pallas kernels for 5% -> 5%
where the time goes in v5:
time: 72 us; the launch traced here: 71.8 us
  starting transfers between devices  24.6 us (34%)
  waiting for transfers between devices  23.8 us (33%)
  blocking collectives  15.8 us (22%)
  Pallas kernels  6.76 us (9%)
  between operations  0.78 us (1%)
    ppermute x27, starting transfers between devices, _swap(): return lax.ppermute(array, 'dp', [(i, i ^ offset) for i in range(size)])  24.6 us
    ppermute x27, waiting for transfers between devices, _swap(): return lax.ppermute(array, 'dp', [(i, i ^ offset) for i in range(size)])  23.8 us
    all_to_all x1, blocking collectives, _step(): squares = lax.all_to_all(square, ('expert', 'dp'), 0, 0)  15.8 us
    pallas_call x3, Pallas kernels, _placed(): pl.pallas_call(body, out_shape=jax.ShapeDtypeStruct((size, height, width)...  2.51 us
    pallas_call x2, Pallas kernels, _cut(): pl.pallas_call(functools.partial(_copy_rows, wanted), out_shape=[pltpu.VM...  2.48 us
    pallas_call x7, Pallas kernels, _call(): pl.pallas_call(body, out_shape=outs, in_specs=[VMEM] * len(args), out_spe...  1.77 us
  transfers between devices with their start and end apart: 27, of which 13 were waited for; matrix products, arithmetic and copies ran while one was open for 0% of the time, Pallas kernels for 5%

profile of v5, /device:TPU:0, one launch (start us, length us, event | category | flops | bytes accessed | tf_op | source)
XLA Modules:
  0.0 71.8 jit_solution(15363258058492777146)
XLA Ops:
  0.6 1.5 %shard_map.83 = (bf16[4,8,6144]{2,1,0:T(8,128)(2,1)S(1)}, bf16[4,8,6144]{2,1,0:T(8,128)(2,1)S(1)}, bf16[1,8,6144]{2,1,0:T(8,128)(2,1)S(1)}, bf16[1,8,6144]{2,1,0...) custom-call(bf16[16,8,6144]{2,1,0:T(8,128)(2,1)} %bitcast.16), custom_call_target="tpu_custom_call" | custom-call | flops 1000000 | bytes 1000000 | tf_op jit(solution)/shard_map/pallas_call | solution.py:58
  2.7 2.6 %collective-permute-start.10 = (bf16[1,8,6144]{2,1,0:T(8,128)(2,1)S(1)}, bf16[1,8,6144]{2,1,0:T(8,128)(2,1)S(1)}, u32[]{:S(2)}, u32[]{:S(2)}) collective-permute-start(bf16[1,8,6144]{2,1,0:T(8,128)(2,1)S(1)} %get-tuple-element.30), channel_id=1, source_target_pairs={{0,3},{1,2},{2,1},{3,0},{4,7},{5,6},{6,5},{7,4},{8,11},{9,10},{10,... | collective-permute-start | bytes 294920 | tf_op jit(solution)/shard_map/ppermute | solution.py:16
  5.4 2.0 %collective-permute-start.6 = (bf16[1,8,6144]{2,1,0:T(8,128)(2,1)S(1)}, bf16[1,8,6144]{2,1,0:T(8,128)(2,1)S(1)}, u32[]{:S(2)}, u32[]{:S(2)}) collective-permute-start(bf16[1,8,6144]{2,1,0:T(8,128)(2,1)S(1)} %get-tuple-element.27), channel_id=1, source_target_pairs={{0,2},{1,3},{2,0},{3,1},{4,6},{5,7},{6,4},{7,5},{8,10},{9,11},{10,... | collective-permute-start | bytes 294920 | tf_op jit(solution)/shard_map/ppermute | solution.py:16
  8.5 1.3 %collective-permute-start.3 = (bf16[1,8,6144]{2,1,0:T(8,128)(2,1)S(1)}, bf16[1,8,6144]{2,1,0:T(8,128)(2,1)S(1)}, u32[]{:S(2)}, u32[]{:S(2)}) collective-permute-start(bf16[1,8,6144]{2,1,0:T(8,128)(2,1)S(1)} %get-tuple-element.25), channel_id=1, source_target_pairs={{0,2},{1,3},{2,0},{3,1},{4,6},{5,7},{6,4},{7,5},{8,10},{9,11},{10,... | collective-permute-start | bytes 294920 | tf_op jit(solution)/shard_map/ppermute | solution.py:16
  9.8 1.3 %collective-permute-done.9.left = bf16[1,8,6144]{2,1,0:T(8,128)(2,1)S(1)} collective-permute-done((bf16[1,8,6144]{2,1,0:T(8,128)(2,1)S(1)}, bf16[1,8,6144]{2,1,0:T(8,128)(2,1)S(1)}, u32[]{:S(2)}, u32[]{:S(2)}) %collective-permute-start.9) | collective-permute-done | bytes 98336 | tf_op jit(solution)/shard_map/ppermute | solution.py:16
  11.7 1.6 %collective-permute-start.11 = (f32[8,6144]{1,0:T(8,128)S(1)}, f32[8,6144]{1,0:T(8,128)S(1)}, u32[]{:S(2)}, u32[]{:S(2)}) collective-permute-start(f32[8,6144]{1,0:T(8,128)S(1)} %shard_map.88), channel_id=1, source_target_pairs={{0,4},{1,5},{2,6},{3,7},{4,0},{5,1},{6,2},{7,3},{8,12},{9,13},{10,... | collective-permute-start | bytes 589832 | tf_op jit(solution)/shard_map/ppermute | solution.py:16
  13.3 1.5 %collective-permute-done.7.right = bf16[1,8,6144]{2,1,0:T(8,128)(2,1)S(1)} collective-permute-done((bf16[1,8,6144]{2,1,0:T(8,128)(2,1)S(1)}, bf16[1,8,6144]{2,1,0:T(8,128)(2,1)S(1)}, u32[]{:S(2)}, u32[]{:S(2)}) %collective-permute-start.7) | collective-permute-done | bytes 98336 | tf_op jit(solution)/shard_map/ppermute | solution.py:16
  14.9 2.7 %collective-permute-start.8 = (f32[8,6144]{1,0:T(8,128)S(1)}, f32[8,6144]{1,0:T(8,128)S(1)}, u32[]{:S(2)}, u32[]{:S(2)}) collective-permute-start(f32[8,6144]{1,0:T(8,128)S(1)} %shard_map.87), channel_id=1, source_target_pairs={{0,8},{1,9},{2,10},{3,11},{4,12},{5,13},{6,14},{7,15},{8,0},{9,1},... | collective-permute-start | bytes 589832 | tf_op jit(solution)/shard_map/ppermute | solution.py:16
  17.6 1.4 %collective-permute-done.4.right = bf16[1,8,6144]{2,1,0:T(8,128)(2,1)S(1)} collective-permute-done((bf16[1,8,6144]{2,1,0:T(8,128)(2,1)S(1)}, bf16[1,8,6144]{2,1,0:T(8,128)(2,1)S(1)}, u32[]{:S(2)}, u32[]{:S(2)}) %collective-permute-start.4) | collective-permute-done | bytes 98336 | tf_op jit(solution)/shard_map/ppermute | solution.py:16
  19.0 3.5 %collective-permute-start.5 = (f32[8,6144]{1,0:T(8,128)S(1)}, f32[8,6144]{1,0:T(8,128)S(1)}, u32[]{:S(2)}, u32[]{:S(2)}) collective-permute-start(f32[8,6144]{1,0:T(8,128)S(1)} %shard_map.86), channel_id=1, source_target_pairs={{0,12},{1,13},{2,14},{3,15},{4,8},{5,9},{6,10},{7,11},{8,4},{9,5},... | collective-permute-start | bytes 589832 | tf_op jit(solution)/shard_map/ppermute | solution.py:16
  22.5 1.5 %collective-permute-start.1 = (bf16[1,8,6144]{2,1,0:T(8,128)(2,1)S(1)}, bf16[1,8,6144]{2,1,0:T(8,128)(2,1)S(1)}, u32[]{:S(2)}, u32[]{:S(2)}) collective-permute-start(bf16[1,8,6144]{2,1,0:T(8,128)(2,1)S(1)} %get-tuple-element.23), channel_id=1, source_target_pairs={{0,2},{1,3},{2,0},{3,1},{4,6},{5,7},{6,4},{7,5},{8,10},{9,11},{10,... | collective-permute-start | bytes 294920 | tf_op jit(solution)/shard_map/ppermute | solution.py:16
  24.1 3.8 %collective-permute-done.1.left = bf16[1,8,6144]{2,1,0:T(8,128)(2,1)S(1)} collective-permute-done((bf16[1,8,6144]{2,1,0:T(8,128)(2,1)S(1)}, bf16[1,8,6144]{2,1,0:T(8,128)(2,1)S(1)}, u32[]{:S(2)}, u32[]{:S(2)}) %collective-permute-start.1) | collective-permute-done | bytes 98336 | tf_op jit(solution)/shard_map/ppermute | solution.py:16
  27.9 1.3 %collective-permute-done.2.right = bf16[1,8,6144]{2,1,0:T(8,128)(2,1)S(1)} collective-permute-done((bf16[1,8,6144]{2,1,0:T(8,128)(2,1)S(1)}, bf16[1,8,6144]{2,1,0:T(8,128)(2,1)S(1)}, u32[]{:S(2)}, u32[]{:S(2)}) %collective-permute-start.2) | collective-permute-done | bytes 98336 | tf_op jit(solution)/shard_map/ppermute | solution.py:16
  29.2 2.9 %collective-permute-done.8.refs_2_ = f32[8,6144]{1,0:T(8,128)S(1)} collective-permute-done((f32[8,6144]{1,0:T(8,128)S(1)}, f32[8,6144]{1,0:T(8,128)S(1)}, u32[]{:S(2)}, u32[]{:S(2)}) %collective-permute-start.8) | collective-permute-done | bytes 196640 | tf_op jit(solution)/shard_map/ppermute | solution.py:16
  32.2 15.8 %all_to_all.5.squares = f32[32,1,128]{2,1,0:T(1,128)S(1)} all-to-all(f32[32,1,128]{2,1,0:T(1,128)S(1)} %get-tuple-element.31), channel_id=1, replica_groups=mesh['expert'=2,'dp'=16] {'expert','dp'}, dimensions={0} | all-to-all | bytes 32768 | tf_op jit(solution)/shard_map/all_to_all | solution.py:177
  49.6 3.2 %collective-permute-start.20 = (bf16[8,6144]{1,0:T(8,128)(2,1)S(1)}, bf16[8,6144]{1,0:T(8,128)(2,1)S(1)}, u32[]{:S(2)}, u32[]{:S(2)}) collective-permute-start(bf16[8,6144]{1,0:T(8,128)(2,1)S(1)} %shard_map.91.refs_0_), channel_id=1, source_target_pairs={{0,8},{1,9},{2,10},{3,11},{4,12},{5,13},{6,14},{7,15},{8,0},{9,1},... | collective-permute-start | bytes 294920 | tf_op jit(solution)/shard_map/ppermute | solution.py:16
  53.4 2.5 %collective-permute-done.14.refs_1_ = bf16[8,6144]{1,0:T(8,128)(2,1)S(1)} collective-permute-done((bf16[8,6144]{1,0:T(8,128)(2,1)S(1)}, bf16[8,6144]{1,0:T(8,128)(2,1)S(1)}, u32[]{:S(2)}, u32[]{:S(2)}) %collective-permute-start.14) | collective-permute-done | bytes 98336 | tf_op jit(solution)/shard_map/ppermute | solution.py:16
  55.9 1.1 %collective-permute-done.17.refs_2_ = bf16[8,6144]{1,0:T(8,128)(2,1)S(1)} collective-permute-done((bf16[8,6144]{1,0:T(8,128)(2,1)S(1)}, bf16[8,6144]{1,0:T(8,128)(2,1)S(1)}, u32[]{:S(2)}, u32[]{:S(2)}) %collective-permute-start.17) | collective-permute-done | bytes 98336 | tf_op jit(solution)/shard_map/ppermute | solution.py:16
  57.0 2.3 %collective-permute-done.20.refs_3_ = bf16[8,6144]{1,0:T(8,128)(2,1)S(1)} collective-permute-done((bf16[8,6144]{1,0:T(8,128)(2,1)S(1)}, bf16[8,6144]{1,0:T(8,128)(2,1)S(1)}, u32[]{:S(2)}, u32[]{:S(2)}) %collective-permute-start.20) | collective-permute-done | bytes 98336 | tf_op jit(solution)/shard_map/ppermute | solution.py:16
  60.0 1.4 %collective-permute-start.18 = (bf16[8,6144]{1,0:T(8,128)(2,1)S(1)}, bf16[8,6144]{1,0:T(8,128)(2,1)S(1)}, u32[]{:S(2)}, u32[]{:S(2)}) collective-permute-start(bf16[8,6144]{1,0:T(8,128)(2,1)S(1)} %collective-permute-done.17.refs_2_), channel_id=1, source_target_pairs={{0,2},{1,3},{2,0},{3,1},{4,6},{5,7},{6,4},{7,5},{8,10},{9,11},{10,... | collective-permute-start | bytes 294920 | tf_op jit(solution)/shard_map/ppermute | solution.py:16
  62.5 2.4 %collective-permute-done.15.refs_1_ = bf16[8,6144]{1,0:T(8,128)(2,1)S(1)} collective-permute-done((bf16[8,6144]{1,0:T(8,128)(2,1)S(1)}, bf16[8,6144]{1,0:T(8,128)(2,1)S(1)}, u32[]{:S(2)}, u32[]{:S(2)}) %collective-permute-start.15) | collective-permute-done | bytes 98336 | tf_op jit(solution)/shard_map/ppermute | solution.py:16
  65.0 2.1 %collective-permute-done.18.refs_2_ = bf16[8,6144]{1,0:T(8,128)(2,1)S(1)} collective-permute-done((bf16[8,6144]{1,0:T(8,128)(2,1)S(1)}, bf16[8,6144]{1,0:T(8,128)(2,1)S(1)}, u32[]{:S(2)}, u32[]{:S(2)}) %collective-permute-start.18) | collective-permute-done | bytes 98336 | tf_op jit(solution)/shard_map/ppermute | solution.py:16
  67.1 1.1 %collective-permute-done.21.refs_3_ = bf16[8,6144]{1,0:T(8,128)(2,1)S(1)} collective-permute-done((bf16[8,6144]{1,0:T(8,128)(2,1)S(1)}, bf16[8,6144]{1,0:T(8,128)(2,1)S(1)}, u32[]{:S(2)}, u32[]{:S(2)}) %collective-permute-start.21) | collective-permute-done | bytes 98336 | tf_op jit(solution)/shard_map/ppermute | solution.py:16
  68.2 1.1 %shard_map.90 = (f32[8,6144]{1,0:T(8,128)}, f32[8,6144]{1,0:T(8,128)}, f32[8,6144]{1,0:T(8,128)}, f32[8,6144]{1,0:T(8,128)}) custom-call(f32[32,1,128]{2,1,0:T(1,128)S(1)} %all_to_all.5.squares, f32[8,6144]{1,0:T(8,128)S(1)} %get-tuple-element.32.summed, f32[8,6144]{1,0:T(8,128)S(1)} %bitcast.10, f32[8,6144]{1,0:T(8,128)S(1)} %bitcast.12, f32[8,6144]{1,0:T(8,128)S(1)} %bitcast.14), custom_call_target="tpu_custom_call" | custom-call | flops 1000000 | bytes 1000000 | tf_op jit(solution)/shard_map/pallas_call | solution.py:20
  (49 shorter events, 9.2 us)
Async XLA Ops:
  2.2 9.5 %collective-permute-start = (bf16[4,8,6144]{2,1,0:T(8,128)(2,1)S(1)}, bf16[4,8,6144]{2,1,0:T(8,128)(2,1)S(1)}, u32[]{:S(2)}, u32[]{:S(2)}) collective-permute-start(bf16[4,8,6144]{2,1,0:T(8,128)(2,1)S(1)} %get-tuple-element.22), channel_id=1, source_target_pairs={{0,1},{1,0},{2,3},{3,2},{4,5},{5,4},{6,7},{7,6},{8,9},{9,8},{10,11... | collective-permute-start | bytes 1179656 | tf_op jit(solution)/shard_map/ppermute | solution.py:16
  2.7 5.8 %collective-permute-start.10 = (bf16[1,8,6144]{2,1,0:T(8,128)(2,1)S(1)}, bf16[1,8,6144]{2,1,0:T(8,128)(2,1)S(1)}, u32[]{:S(2)}, u32[]{:S(2)}) collective-permute-start(bf16[1,8,6144]{2,1,0:T(8,128)(2,1)S(1)} %get-tuple-element.30), channel_id=1, source_target_pairs={{0,3},{1,2},{2,1},{3,0},{4,7},{5,6},{6,5},{7,4},{8,11},{9,10},{10,... | collective-permute-start | bytes 294920 | tf_op jit(solution)/shard_map/ppermute | solution.py:16
  5.3 5.7 %collective-permute-start.9 = (bf16[1,8,6144]{2,1,0:T(8,128)(2,1)S(1)}, bf16[1,8,6144]{2,1,0:T(8,128)(2,1)S(1)}, u32[]{:S(2)}, u32[]{:S(2)}) collective-permute-start(bf16[1,8,6144]{2,1,0:T(8,128)(2,1)S(1)} %get-tuple-element.29), channel_id=1, source_target_pairs={{0,2},{1,3},{2,0},{3,1},{4,6},{5,7},{6,4},{7,5},{8,10},{9,11},{10,... | collective-permute-start | bytes 294920 | tf_op jit(solution)/shard_map/ppermute | solution.py:16
  5.4 7.9 %collective-permute-start.6 = (bf16[1,8,6144]{2,1,0:T(8,128)(2,1)S(1)}, bf16[1,8,6144]{2,1,0:T(8,128)(2,1)S(1)}, u32[]{:S(2)}, u32[]{:S(2)}) collective-permute-start(bf16[1,8,6144]{2,1,0:T(8,128)(2,1)S(1)} %get-tuple-element.27), channel_id=1, source_target_pairs={{0,2},{1,3},{2,0},{3,1},{4,6},{5,7},{6,4},{7,5},{8,10},{9,11},{10,... | collective-permute-start | bytes 294920 | tf_op jit(solution)/shard_map/ppermute | solution.py:16
  7.4 7.5 %collective-permute-start.7 = (bf16[1,8,6144]{2,1,0:T(8,128)(2,1)S(1)}, bf16[1,8,6144]{2,1,0:T(8,128)(2,1)S(1)}, u32[]{:S(2)}, u32[]{:S(2)}) collective-permute-start(bf16[1,8,6144]{2,1,0:T(8,128)(2,1)S(1)} %get-tuple-element.28), channel_id=1, source_target_pairs={{0,3},{1,2},{2,1},{3,0},{4,7},{5,6},{6,5},{7,4},{8,11},{9,10},{10,... | collective-permute-start | bytes 294920 | tf_op jit(solution)/shard_map/ppermute | solution.py:16
  8.5 9.1 %collective-permute-start.3 = (bf16[1,8,6144]{2,1,0:T(8,128)(2,1)S(1)}, bf16[1,8,6144]{2,1,0:T(8,128)(2,1)S(1)}, u32[]{:S(2)}, u32[]{:S(2)}) collective-permute-start(bf16[1,8,6144]{2,1,0:T(8,128)(2,1)S(1)} %get-tuple-element.25), channel_id=1, source_target_pairs={{0,2},{1,3},{2,0},{3,1},{4,6},{5,7},{6,4},{7,5},{8,10},{9,11},{10,... | collective-permute-start | bytes 294920 | tf_op jit(solution)/shard_map/ppermute | solution.py:16
  11.1 7.9 %collective-permute-start.4 = (bf16[1,8,6144]{2,1,0:T(8,128)(2,1)S(1)}, bf16[1,8,6144]{2,1,0:T(8,128)(2,1)S(1)}, u32[]{:S(2)}, u32[]{:S(2)}) collective-permute-start(bf16[1,8,6144]{2,1,0:T(8,128)(2,1)S(1)} %get-tuple-element.26), channel_id=1, source_target_pairs={{0,3},{1,2},{2,1},{3,0},{4,7},{5,6},{6,5},{7,4},{8,11},{9,10},{10,... | collective-permute-start | bytes 294920 | tf_op jit(solution)/shard_map/ppermute | solution.py:16
  11.7 17.5 %collective-permute-start.11 = (f32[8,6144]{1,0:T(8,128)S(1)}, f32[8,6144]{1,0:T(8,128)S(1)}, u32[]{:S(2)}, u32[]{:S(2)}) collective-permute-start(f32[8,6144]{1,0:T(8,128)S(1)} %shard_map.88), channel_id=1, source_target_pairs={{0,4},{1,5},{2,6},{3,7},{4,0},{5,1},{6,2},{7,3},{8,12},{9,13},{10,... | collective-permute-start | bytes 589832 | tf_op jit(solution)/shard_map/ppermute | solution.py:16
  14.9 17.1 %collective-permute-start.8 = (f32[8,6144]{1,0:T(8,128)S(1)}, f32[8,6144]{1,0:T(8,128)S(1)}, u32[]{:S(2)}, u32[]{:S(2)}) collective-permute-start(f32[8,6144]{1,0:T(8,128)S(1)} %shard_map.87), channel_id=1, source_target_pairs={{0,8},{1,9},{2,10},{3,11},{4,12},{5,13},{6,14},{7,15},{8,0},{9,1},... | collective-permute-start | bytes 589832 | tf_op jit(solution)/shard_map/ppermute | solution.py:16
  19.0 13.0 %collective-permute-start.5 = (f32[8,6144]{1,0:T(8,128)S(1)}, f32[8,6144]{1,0:T(8,128)S(1)}, u32[]{:S(2)}, u32[]{:S(2)}) collective-permute-start(f32[8,6144]{1,0:T(8,128)S(1)} %shard_map.86), channel_id=1, source_target_pairs={{0,12},{1,13},{2,14},{3,15},{4,8},{5,9},{6,10},{7,11},{8,4},{9,5},... | collective-permute-start | bytes 589832 | tf_op jit(solution)/shard_map/ppermute | solution.py:16
  22.5 5.3 %collective-permute-start.1 = (bf16[1,8,6144]{2,1,0:T(8,128)(2,1)S(1)}, bf16[1,8,6144]{2,1,0:T(8,128)(2,1)S(1)}, u32[]{:S(2)}, u32[]{:S(2)}) collective-permute-start(bf16[1,8,6144]{2,1,0:T(8,128)(2,1)S(1)} %get-tuple-element.23), channel_id=1, source_target_pairs={{0,2},{1,3},{2,0},{3,1},{4,6},{5,7},{6,4},{7,5},{8,10},{9,11},{10,... | collective-permute-start | bytes 294920 | tf_op jit(solution)/shard_map/ppermute | solution.py:16
  24.0 5.1 %collective-permute-start.2 = (bf16[1,8,6144]{2,1,0:T(8,128)(2,1)S(1)}, bf16[1,8,6144]{2,1,0:T(8,128)(2,1)S(1)}, u32[]{:S(2)}, u32[]{:S(2)}) collective-permute-start(bf16[1,8,6144]{2,1,0:T(8,128)(2,1)S(1)} %get-tuple-element.24), channel_id=1, source_target_pairs={{0,3},{1,2},{2,1},{3,0},{4,7},{5,6},{6,5},{7,4},{8,11},{9,10},{10,... | collective-permute-start | bytes 294920 | tf_op jit(solution)/shard_map/ppermute | solution.py:16
  48.4 7.5 %collective-permute-start.14 = (bf16[8,6144]{1,0:T(8,128)(2,1)S(1)}, bf16[8,6144]{1,0:T(8,128)(2,1)S(1)}, u32[]{:S(2)}, u32[]{:S(2)}) collective-permute-start(bf16[8,6144]{1,0:T(8,128)(2,1)S(1)} %shard_map.91.refs_0_), channel_id=1, source_target_pairs={{0,12},{1,13},{2,14},{3,15},{4,8},{5,9},{6,10},{7,11},{8,4},{9,5},... | collective-permute-start | bytes 294920 | tf_op jit(solution)/shard_map/ppermute | solution.py:16
  48.9 8.1 %collective-permute-start.17 = (bf16[8,6144]{1,0:T(8,128)(2,1)S(1)}, bf16[8,6144]{1,0:T(8,128)(2,1)S(1)}, u32[]{:S(2)}, u32[]{:S(2)}) collective-permute-start(bf16[8,6144]{1,0:T(8,128)(2,1)S(1)} %shard_map.91.refs_0_), channel_id=1, source_target_pairs={{0,4},{1,5},{2,6},{3,7},{4,0},{5,1},{6,2},{7,3},{8,12},{9,13},{10,... | collective-permute-start | bytes 294920 | tf_op jit(solution)/shard_map/ppermute | solution.py:16
  49.6 9.7 %collective-permute-start.20 = (bf16[8,6144]{1,0:T(8,128)(2,1)S(1)}, bf16[8,6144]{1,0:T(8,128)(2,1)S(1)}, u32[]{:S(2)}, u32[]{:S(2)}) collective-permute-start(bf16[8,6144]{1,0:T(8,128)(2,1)S(1)} %shard_map.91.refs_0_), channel_id=1, source_target_pairs={{0,8},{1,9},{2,10},{3,11},{4,12},{5,13},{6,14},{7,15},{8,0},{9,1},... | collective-permute-start | bytes 294920 | tf_op jit(solution)/shard_map/ppermute | solution.py:16
  52.8 7.2 %collective-permute-start.23 = (bf16[8,6144]{1,0:T(8,128)(2,1)S(1)}, bf16[8,6144]{1,0:T(8,128)(2,1)S(1)}, u32[]{:S(2)}, u32[]{:S(2)}) collective-permute-start(bf16[8,6144]{1,0:T(8,128)(2,1)S(1)} %shard_map.91.refs_0_), channel_id=1, source_target_pairs={{0,1},{1,0},{2,3},{3,2},{4,5},{5,4},{6,7},{7,6},{8,9},{9,8},{10,11... | collective-permute-start | bytes 294920 | tf_op jit(solution)/shard_map/ppermute | solution.py:16
  52.8 8.5 %collective-permute-start.12 = (bf16[8,6144]{1,0:T(8,128)(2,1)S(1)}, bf16[8,6144]{1,0:T(8,128)(2,1)S(1)}, u32[]{:S(2)}, u32[]{:S(2)}) collective-permute-start(bf16[8,6144]{1,0:T(8,128)(2,1)S(1)} %shard_map.91.refs_0_), channel_id=1, source_target_pairs={{0,2},{1,3},{2,0},{3,1},{4,6},{5,7},{6,4},{7,5},{8,10},{9,11},{10,... | collective-permute-start | bytes 294920 | tf_op jit(solution)/shard_map/ppermute | solution.py:16
  55.9 6.1 %collective-permute-start.24 = (bf16[8,6144]{1,0:T(8,128)(2,1)S(1)}, bf16[8,6144]{1,0:T(8,128)(2,1)S(1)}, u32[]{:S(2)}, u32[]{:S(2)}) collective-permute-start(bf16[8,6144]{1,0:T(8,128)(2,1)S(1)} %collective-permute-done.14.refs_1_), channel_id=1, source_target_pairs={{0,1},{1,0},{2,3},{3,2},{4,5},{5,4},{6,7},{7,6},{8,9},{9,8},{10,11... | collective-permute-start | bytes 294920 | tf_op jit(solution)/shard_map/ppermute | solution.py:16
  59.3 5.7 %collective-permute-start.15 = (bf16[8,6144]{1,0:T(8,128)(2,1)S(1)}, bf16[8,6144]{1,0:T(8,128)(2,1)S(1)}, u32[]{:S(2)}, u32[]{:S(2)}) collective-permute-start(bf16[8,6144]{1,0:T(8,128)(2,1)S(1)} %collective-permute-done.14.refs_1_), channel_id=1, source_target_pairs={{0,2},{1,3},{2,0},{3,1},{4,6},{5,7},{6,4},{7,5},{8,10},{9,11},{10,... | collective-permute-start | bytes 294920 | tf_op jit(solution)/shard_map/ppermute | solution.py:16
  60.0 7.1 %collective-permute-start.18 = (bf16[8,6144]{1,0:T(8,128)(2,1)S(1)}, bf16[8,6144]{1,0:T(8,128)(2,1)S(1)}, u32[]{:S(2)}, u32[]{:S(2)}) collective-permute-start(bf16[8,6144]{1,0:T(8,128)(2,1)S(1)} %collective-permute-done.17.refs_2_), channel_id=1, source_target_pairs={{0,2},{1,3},{2,0},{3,1},{4,6},{5,7},{6,4},{7,5},{8,10},{9,11},{10,... | collective-permute-start | bytes 294920 | tf_op jit(solution)/shard_map/ppermute | solution.py:16
  61.4 6.8 %collective-permute-start.21 = (bf16[8,6144]{1,0:T(8,128)(2,1)S(1)}, bf16[8,6144]{1,0:T(8,128)(2,1)S(1)}, u32[]{:S(2)}, u32[]{:S(2)}) collective-permute-start(bf16[8,6144]{1,0:T(8,128)(2,1)S(1)} %collective-permute-done.20.refs_3_), channel_id=1, source_target_pairs={{0,2},{1,3},{2,0},{3,1},{4,6},{5,7},{6,4},{7,5},{8,10},{9,11},{10,... | collective-permute-start | bytes 294920 | tf_op jit(solution)/shard_map/ppermute | solution.py:16
  62.0 7.2 %collective-permute-start.26 = (bf16[8,6144]{1,0:T(8,128)(2,1)S(1)}, bf16[8,6144]{1,0:T(8,128)(2,1)S(1)}, u32[]{:S(2)}, u32[]{:S(2)}) collective-permute-start(bf16[8,6144]{1,0:T(8,128)(2,1)S(1)} %collective-permute-done.20.refs_3_), channel_id=1, source_target_pairs={{0,1},{1,0},{2,3},{3,2},{4,5},{5,4},{6,7},{7,6},{8,9},{9,8},{10,11... | collective-permute-start | bytes 294920 | tf_op jit(solution)/shard_map/ppermute | solution.py:16
  62.0 8.9 %collective-permute-start.13 = (bf16[8,6144]{1,0:T(8,128)(2,1)S(1)}, bf16[8,6144]{1,0:T(8,128)(2,1)S(1)}, u32[]{:S(2)}, u32[]{:S(2)}) collective-permute-start(bf16[8,6144]{1,0:T(8,128)(2,1)S(1)} %collective-permute-done.12.refs_0_), channel_id=1, source_target_pairs={{0,1},{1,0},{2,3},{3,2},{4,5},{5,4},{6,7},{7,6},{8,9},{9,8},{10,11... | collective-permute-start | bytes 294920 | tf_op jit(solution)/shard_map/ppermute | solution.py:16
  65.0 6.0 %collective-permute-start.16 = (bf16[8,6144]{1,0:T(8,128)(2,1)S(1)}, bf16[8,6144]{1,0:T(8,128)(2,1)S(1)}, u32[]{:S(2)}, u32[]{:S(2)}) collective-permute-start(bf16[8,6144]{1,0:T(8,128)(2,1)S(1)} %collective-permute-done.15.refs_1_), channel_id=1, source_target_pairs={{0,1},{1,0},{2,3},{3,2},{4,5},{5,4},{6,7},{7,6},{8,9},{9,8},{10,11... | collective-permute-start | bytes 294920 | tf_op jit(solution)/shard_map/ppermute | solution.py:16
  (6 other events, 111.1 us)
